TPU v7x, 32 devices: a whole 2x2x4 slice. The times are simulated.
32 devices in a mesh: dp: 8 (over z, y), tensor: 4 (over x, core).
Axes of the slice: x: 2, y: 2, z: 4, core: 2. Of those that a mesh axis runs over, the one named last changes fastest.
Arguments:
- input_img: bfloat16 [24, 256, 1536], P('dp'), may hold values from -6 to 6
- input_txt: bfloat16 [24, 154, 1536], P('dp'), may hold values from -6 to 6
- conditioning: bfloat16 [24, 1536], replicated, may hold values from -6 to 6
- ada_weight: bfloat16 [2, 1536, 9216], P(None, None, ('dp', 'tensor')), may hold values from -0.15625 to 0.15625
- ada_bias: bfloat16 [2, 9216], P(None, ('dp', 'tensor')), may hold values from -3 to 3
- qkv_weight: bfloat16 [2, 1536, 3, 1536], P(None, None, None, 'tensor'), may hold values from -0.15625 to 0.15625
- qkv_bias: bfloat16 [2, 3, 1536], P(None, None, 'tensor'), may hold values from -3 to 3
- norm_gain: float32 [2, 2, 64], replicated, may hold values from 0.1 to 1.9
- proj_weight: bfloat16 [2, 1536, 1536], P(None, 'tensor'), may hold values from -0.4375 to 0.4375
- proj_bias: bfloat16 [2, 1536], replicated, may hold values from -3 to 3
- up_weight: bfloat16 [2, 1536, 6144], P(None, None, 'tensor'), may hold values from -0.15625 to 0.15625
- up_bias: bfloat16 [2, 6144], P(None, 'tensor'), may hold values from -3 to 3
- down_weight: bfloat16 [2, 6144, 1536], P(None, 'tensor'), may hold values from -0.078125 to 0.078125
- down_bias: bfloat16 [2, 1536], replicated, may hold values from -3 to 3
- cotangent_img: bfloat16 [24, 256, 1536], P('dp'), may hold values from -6 to 6
- cotangent_txt: bfloat16 [24, 154, 1536], P('dp'), may hold values from -6 to 6
Outputs:
- output_img: bfloat16 [24, 256, 1536], P('dp')
- output_txt: bfloat16 [24, 154, 1536], P('dp')
- grad_input_img: bfloat16 [24, 256, 1536], P('dp')
- grad_input_txt: bfloat16 [24, 154, 1536], P('dp')
- grad_conditioning: float32 [24, 1536], P('dp')
- grad_ada_weight: float32 [2, 1536, 9216], P(None, None, ('dp', 'tensor'))
- grad_ada_bias: float32 [2, 9216], P(None, ('dp', 'tensor'))
- grad_qkv_weight: float32 [2, 1536, 3, 1536], P(None, 'dp', None, 'tensor')
- grad_qkv_bias: float32 [2, 3, 1536], P(None, None, 'tensor')
- grad_norm_gain: float32 [2, 2, 64], replicated
- grad_proj_weight: float32 [2, 1536, 1536], P(None, 'tensor', 'dp')
- grad_proj_bias: float32 [2, 1536], replicated
- grad_up_weight: float32 [2, 1536, 6144], P(None, 'dp', 'tensor')
- grad_up_bias: float32 [2, 6144], P(None, 'tensor')
- grad_down_weight: float32 [2, 6144, 1536], P(None, 'tensor', 'dp')
- grad_down_bias: float32 [2, 1536], replicated
All inputs are finite; a program needn't handle non-finite values.
Results may differ from a plain program's by a relative error of at most 0.012.
Values sent between devices are 32-bit elements; how exact they have to be, the bound alone decides.
A program may use at most 384 MiB of HBM per device.

v0:
```python
import jax
import jax.numpy as jnp
from jax import lax
from jax.sharding import PartitionSpec as P

D = 1536
IMG = 256


epsilon = 1e-06
GELU_C = 0.7978845608028654
GELU_A = 0.044715


def mixed(pattern, first_op, second_op):
    return jnp.einsum(pattern, first_op, second_op, preferred_element_type=jnp.float32)


def dot_plain(first_op, second_op):
    return jnp.dot(first_op, second_op, preferred_element_type=jnp.float32)


def dot_right_t(first_op, second_op):
    return lax.dot_general(
        first_op, second_op, (((1,), (1,)), ((), ())), preferred_element_type=jnp.float32
    )


def dot_left_t(first_op, second_op):
    return lax.dot_general(
        first_op, second_op, (((0,), (0,)), ((), ())), preferred_element_type=jnp.float32
    )


def layer_norm(values):
    center = values - jnp.mean(values, axis=-1, keepdims=True)
    inverse = lax.rsqrt(jnp.mean(center * center, axis=-1, keepdims=True) + epsilon)
    return (center * inverse, inverse)


def norm_back(grad_normed, normed, inverse):
    return inverse * (
        grad_normed
        - jnp.mean(grad_normed, axis=-1, keepdims=True)
        - normed * jnp.mean(grad_normed * normed, axis=-1, keepdims=True)
    )


def gelu_tanh(values):
    return 0.5 * values * (1.0 + jnp.tanh(GELU_C * (values + GELU_A * values * values * values)))


def gelu_slope(values):
    inner = jnp.tanh(GELU_C * (values + GELU_A * values * values * values))
    return 0.5 * (1.0 + inner) + 0.5 * values * (1.0 - inner * inner) * GELU_C * (
        1.0 + 3.0 * GELU_A * values * values
    )


def piece_of(modulate, piece_index):
    feat_width = modulate.shape[1] // 6
    return modulate[:, None, piece_index * feat_width : (piece_index + 1) * feat_width]


def token_span(array_in, stream):
    if stream == 0:
        return array_in[:, :IMG]
    return array_in[:, IMG:]


def paired(records, field_name):
    return jnp.stack([records[0][field_name], records[1][field_name]])


def front_part(values, modulate, qkv_w, qkv_b, gain_pair):
    batch_size, length, feat_width = values.shape
    normed, inverse = layer_norm(values.astype(jnp.float32))
    hidden = (normed * (1.0 + piece_of(modulate, 1)) + piece_of(modulate, 0)).astype(jnp.bfloat16)
    packed = dot_plain(
        hidden.reshape(batch_size * length, feat_width), qkv_w.reshape(feat_width, -1)
    )
    head_dim = gain_pair.shape[1]
    packed = (packed.reshape(batch_size, length, 3, -1) + qkv_b).reshape(
        batch_size, length, 3, -1, head_dim
    )
    q_raw = packed[:, :, 0]
    k_raw = packed[:, :, 1]
    q_factor = lax.rsqrt(jnp.mean(q_raw * q_raw, axis=-1, keepdims=True) + epsilon)
    k_factor = lax.rsqrt(jnp.mean(k_raw * k_raw, axis=-1, keepdims=True) + epsilon)
    return {
        "normed": normed,
        "inverse": inverse,
        "hidden": hidden,
        "q_raw": q_raw,
        "k_raw": k_raw,
        "q_factor": q_factor,
        "k_factor": k_factor,
        "q_low": (q_raw * q_factor * gain_pair[0]).astype(jnp.bfloat16),
        "k_low": (k_raw * k_factor * gain_pair[1]).astype(jnp.bfloat16),
        "v_low": packed[:, :, 2].astype(jnp.bfloat16),
    }


def attn_scores(q_all, k_all):
    return mixed("bqhd,bkhd->bhqk", q_all, k_all) * q_all.shape[3] ** (-0.5)


def attn_forward(q_all, k_all, v_all):
    scores = attn_scores(q_all, k_all)
    row_top = jnp.max(scores, axis=-1, keepdims=True)
    log_total = row_top + jnp.log(jnp.sum(jnp.exp(scores - row_top), axis=-1, keepdims=True))
    prob_low = jnp.exp(scores - log_total).astype(jnp.bfloat16)
    attn_all = mixed("bhqk,bkhd->bqhd", prob_low, v_all).astype(jnp.bfloat16)
    return (attn_all, log_total)


def attn_backward(q_all, k_all, v_all, log_total, grad_attn):
    scores = attn_scores(q_all, k_all)
    prob_full = jnp.exp(scores - log_total)
    prob_low = prob_full.astype(jnp.bfloat16)
    grad_vals = mixed("bhqk,bqhd->bkhd", prob_low, grad_attn)
    grad_prob = mixed("bqhd,bkhd->bhqk", grad_attn, v_all)
    grad_scores = (
        prob_full * (grad_prob - jnp.sum(prob_full * grad_prob, axis=-1, keepdims=True))
    ).astype(jnp.bfloat16)
    score_scale = q_all.shape[3] ** (-0.5)
    grad_query = mixed("bhqk,bkhd->bqhd", grad_scores, k_all) * score_scale
    grad_keys = mixed("bhqk,bqhd->bkhd", grad_scores, q_all) * score_scale
    return (grad_query, grad_keys, grad_vals)


def middle_part(values, modulate, branch_sum, proj_b, up_w, up_b):
    batch_size, length, feat_width = values.shape
    branch = branch_sum.reshape(batch_size, length, feat_width) + proj_b
    residual = values.astype(jnp.float32) + piece_of(modulate, 2) * branch
    normed, inverse = layer_norm(residual)
    hidden = (normed * (1.0 + piece_of(modulate, 4)) + piece_of(modulate, 3)).astype(jnp.bfloat16)
    upward = dot_plain(hidden.reshape(-1, feat_width), up_w) + up_b
    return {
        "branch": branch,
        "residual": residual,
        "normed": normed,
        "inverse": inverse,
        "hidden": hidden,
        "upward": upward,
        "active": gelu_tanh(upward).astype(jnp.bfloat16),
    }


def finish_part(state, mlp_sum, modulate, down_b):
    mlp_out = mlp_sum.reshape(state["residual"].shape) + down_b
    state["mlp_out"] = mlp_out
    return (state["residual"] + piece_of(modulate, 5) * mlp_out).astype(jnp.bfloat16)


def mlp_back_part(state, cotangent, modulate, down_w):
    feat_width = cotangent.shape[2]
    grad_out = cotangent.astype(jnp.float32)
    grad_mlp = grad_out * piece_of(modulate, 5)
    grad_mlp_low = grad_mlp.astype(jnp.bfloat16).reshape(-1, feat_width)
    grad_upward = dot_right_t(grad_mlp_low, down_w) * gelu_slope(state["upward"])
    grad_up_low = grad_upward.astype(jnp.bfloat16)
    return {
        "grad_out": grad_out,
        "gate_two": jnp.sum(grad_out * state["mlp_out"], axis=1),
        "down_b": jnp.sum(grad_mlp, axis=(0, 1)),
        "down_w": dot_left_t(state["active"], grad_mlp_low),
        "up_b": jnp.sum(grad_upward, axis=0),
        "up_w": dot_left_t(state["hidden"].reshape(-1, feat_width), grad_up_low),
        "up_low": grad_up_low,
    }


def resid_back_part(state, mlp_back, hidden_sum, modulate, proj_w, attn_part):
    grad_hidden = hidden_sum.reshape(state["residual"].shape)
    grad_resid = mlp_back["grad_out"] + norm_back(
        grad_hidden * (1.0 + piece_of(modulate, 4)), state["normed"], state["inverse"]
    )
    grad_branch = grad_resid * piece_of(modulate, 2)
    local_width = attn_part.shape[2] * attn_part.shape[3]
    grad_branch_low = grad_branch.astype(jnp.bfloat16).reshape(-1, grad_branch.shape[2])
    return {
        "shift_two": jnp.sum(grad_hidden, axis=1),
        "scale_two": jnp.sum(grad_hidden * state["normed"], axis=1),
        "gate_one": jnp.sum(grad_resid * state["branch"], axis=1),
        "grad_resid": grad_resid,
        "proj_b": jnp.sum(grad_branch, axis=(0, 1)),
        "proj_w": dot_left_t(attn_part.reshape(-1, local_width), grad_branch_low),
        "grad_attn": dot_right_t(grad_branch_low, proj_w)
        .astype(jnp.bfloat16)
        .reshape(attn_part.shape),
    }


def qkv_back_part(front, grad_query, grad_keys, grad_vals, gain_pair, qkv_w):
    grad_q_gain = grad_query * gain_pair[0]
    grad_q_raw = front["q_factor"] * grad_q_gain - front["q_raw"] * front[
        "q_factor"
    ] ** 3 * jnp.mean(grad_q_gain * front["q_raw"], axis=-1, keepdims=True)
    grad_k_gain = grad_keys * gain_pair[1]
    grad_k_raw = front["k_factor"] * grad_k_gain - front["k_raw"] * front[
        "k_factor"
    ] ** 3 * jnp.mean(grad_k_gain * front["k_raw"], axis=-1, keepdims=True)
    gain_term = jnp.stack(
        [
            jnp.sum(grad_query * front["q_raw"] * front["q_factor"], axis=(0, 1, 2)),
            jnp.sum(grad_keys * front["k_raw"] * front["k_factor"], axis=(0, 1, 2)),
        ]
    )
    batch_size, length, feat_width = front["hidden"].shape
    grad_packed = jnp.stack([grad_q_raw, grad_k_raw, grad_vals], axis=2).reshape(
        batch_size * length, -1
    )
    grad_packed_low = grad_packed.astype(jnp.bfloat16)
    return {
        "gain": gain_term,
        "qkv_b": jnp.sum(grad_packed, axis=0).reshape(3, -1),
        "qkv_w": dot_left_t(
            front["hidden"].reshape(batch_size * length, feat_width), grad_packed_low
        ).reshape(feat_width, 3, -1),
        "grad_hidden": dot_right_t(grad_packed_low, qkv_w.reshape(feat_width, -1)),
    }


def input_back_part(front, grad_resid, hidden_sum, modulate):
    grad_hidden = hidden_sum.reshape(grad_resid.shape)
    grad_input = grad_resid + norm_back(
        grad_hidden * (1.0 + piece_of(modulate, 1)), front["normed"], front["inverse"]
    )
    return {
        "shift_one": jnp.sum(grad_hidden, axis=1),
        "scale_one": jnp.sum(grad_hidden * front["normed"], axis=1),
        "grad_input": grad_input.astype(jnp.bfloat16),
    }


def on_device(
    input_img,
    input_txt,
    conditioning,
    ada_weight,
    ada_bias,
    qkv_weight,
    qkv_bias,
    norm_gain,
    proj_weight,
    proj_bias,
    up_weight,
    up_bias,
    down_weight,
    down_bias,
    cotangent_img,
    cotangent_txt,
):
    data_size = lax.axis_size("dp")
    seq_here = input_img.shape[0]
    piece_cols = ada_weight.shape[2]
    cond_wide = conditioning.astype(jnp.float32)
    cond_sig = jax.nn.sigmoid(cond_wide)
    silu_cond = (cond_wide * cond_sig).astype(jnp.bfloat16)
    mod_cols = jnp.stack(
        [dot_plain(silu_cond, ada_weight[stream]) + ada_bias[stream] for stream in range(2)], axis=1
    )
    mod_rows = lax.all_to_all(mod_cols, "dp", split_axis=0, concat_axis=2, tiled=True).reshape(
        seq_here, 2, data_size, piece_cols
    )
    modulate = lax.all_gather(mod_rows, "tensor", axis=3, tiled=True).reshape(seq_here, 2, 6 * D)
    inputs = (input_img, input_txt)
    cotangents = (cotangent_img, cotangent_txt)
    fronts = [
        front_part(
            inputs[stream],
            modulate[:, stream],
            qkv_weight[stream],
            qkv_bias[stream],
            norm_gain[stream],
        )
        for stream in range(2)
    ]
    q_all = jnp.concatenate([fronts[0]["q_low"], fronts[1]["q_low"]], axis=1)
    k_all = jnp.concatenate([fronts[0]["k_low"], fronts[1]["k_low"]], axis=1)
    v_all = jnp.concatenate([fronts[0]["v_low"], fronts[1]["v_low"]], axis=1)
    attn_all, log_total = attn_forward(q_all, k_all, v_all)
    attn_parts = [token_span(attn_all, stream) for stream in range(2)]
    local_width = attn_all.shape[2] * attn_all.shape[3]
    branch_img, branch_txt = lax.psum(
        (
            dot_plain(attn_parts[0].reshape(-1, local_width), proj_weight[0]),
            dot_plain(attn_parts[1].reshape(-1, local_width), proj_weight[1]),
        ),
        "tensor",
    )
    branch_sums = (branch_img, branch_txt)
    states = [
        middle_part(
            inputs[stream],
            modulate[:, stream],
            branch_sums[stream],
            proj_bias[stream],
            up_weight[stream],
            up_bias[stream],
        )
        for stream in range(2)
    ]
    mlp_img, mlp_txt = lax.psum(
        (
            dot_plain(states[0]["active"], down_weight[0]),
            dot_plain(states[1]["active"], down_weight[1]),
        ),
        "tensor",
    )
    mlp_sums = (mlp_img, mlp_txt)
    outputs = [
        finish_part(states[stream], mlp_sums[stream], modulate[:, stream], down_bias[stream])
        for stream in range(2)
    ]
    mlp_backs = [
        mlp_back_part(states[stream], cotangents[stream], modulate[:, stream], down_weight[stream])
        for stream in range(2)
    ]
    grad_up_w = paired(mlp_backs, "up_w")
    grad_down_w = paired(mlp_backs, "down_w")
    hidden_img, hidden_txt = lax.psum(
        (
            dot_right_t(mlp_backs[0]["up_low"], up_weight[0]),
            dot_right_t(mlp_backs[1]["up_low"], up_weight[1]),
        ),
        "tensor",
    )
    hidden_sums = (hidden_img, hidden_txt)
    resid_backs = [
        resid_back_part(
            states[stream],
            mlp_backs[stream],
            hidden_sums[stream],
            modulate[:, stream],
            proj_weight[stream],
            attn_parts[stream],
        )
        for stream in range(2)
    ]
    grad_attn = jnp.concatenate([resid_backs[0]["grad_attn"], resid_backs[1]["grad_attn"]], axis=1)
    grad_query, grad_keys, grad_vals = attn_backward(q_all, k_all, v_all, log_total, grad_attn)
    qkv_backs = [
        qkv_back_part(
            fronts[stream],
            token_span(grad_query, stream),
            token_span(grad_keys, stream),
            token_span(grad_vals, stream),
            norm_gain[stream],
            qkv_weight[stream],
        )
        for stream in range(2)
    ]
    first_img, first_txt, gain_sum = lax.psum(
        (qkv_backs[0]["grad_hidden"], qkv_backs[1]["grad_hidden"], paired(qkv_backs, "gain")),
        "tensor",
    )
    first_sums = (first_img, first_txt)
    input_backs = [
        input_back_part(
            fronts[stream],
            resid_backs[stream]["grad_resid"],
            first_sums[stream],
            modulate[:, stream],
        )
        for stream in range(2)
    ]
    grad_modulate = jnp.stack(
        [
            jnp.concatenate(
                [
                    input_backs[stream]["shift_one"],
                    input_backs[stream]["scale_one"],
                    resid_backs[stream]["gate_one"],
                    resid_backs[stream]["shift_two"],
                    resid_backs[stream]["scale_two"],
                    mlp_backs[stream]["gate_two"],
                ],
                axis=-1,
            )
            for stream in range(2)
        ],
        axis=1,
    )
    tensor_size = lax.axis_size("tensor")
    own_cols = grad_modulate.reshape(seq_here, 2, data_size, tensor_size * piece_cols)
    own_cols = lax.dynamic_slice_in_dim(
        own_cols, lax.axis_index("tensor") * piece_cols, piece_cols, axis=3
    )
    grad_cols = lax.all_to_all(
        own_cols.reshape(seq_here, 2, data_size * piece_cols),
        "dp",
        split_axis=2,
        concat_axis=0,
        tiled=True,
    )
    grad_ada_bias = jnp.sum(grad_cols, axis=0)
    grad_cols_low = grad_cols.astype(jnp.bfloat16)
    grad_ada_weight = jnp.stack(
        [dot_left_t(silu_cond, grad_cols_low[:, stream]) for stream in range(2)]
    )
    grad_silu = dot_right_t(grad_cols_low[:, 0], ada_weight[0]) + dot_right_t(
        grad_cols_low[:, 1], ada_weight[1]
    )
    silu_rows = lax.psum_scatter(grad_silu, "dp", scatter_dimension=0, tiled=True)
    silu_rows = lax.psum(silu_rows, "tensor")
    start_row = lax.axis_index("dp") * seq_here
    own_cond = lax.dynamic_slice_in_dim(cond_wide, start_row, seq_here, axis=0)
    own_sig = lax.dynamic_slice_in_dim(cond_sig, start_row, seq_here, axis=0)
    grad_conditioning = silu_rows * own_sig * (1.0 + own_cond * (1.0 - own_sig))
    grad_qkv_w = paired(qkv_backs, "qkv_w")
    grad_proj_w = paired(resid_backs, "proj_w")
    grad_qkv_w, grad_proj_w, grad_up_w, grad_down_w = (
        lax.psum_scatter(grad_qkv_w, "dp", scatter_dimension=1, tiled=True),
        lax.psum_scatter(grad_proj_w, "dp", scatter_dimension=2, tiled=True),
        lax.psum_scatter(grad_up_w, "dp", scatter_dimension=1, tiled=True),
        lax.psum_scatter(grad_down_w, "dp", scatter_dimension=2, tiled=True),
    )
    grad_qkv_b, grad_gain, grad_proj_b, grad_up_b, grad_down_b = lax.psum(
        (
            paired(qkv_backs, "qkv_b"),
            gain_sum,
            paired(resid_backs, "proj_b"),
            paired(mlp_backs, "up_b"),
            paired(mlp_backs, "down_b"),
        ),
        "dp",
    )
    return (
        outputs[0],
        outputs[1],
        input_backs[0]["grad_input"],
        input_backs[1]["grad_input"],
        grad_conditioning,
        grad_ada_weight,
        grad_ada_bias,
        grad_qkv_w,
        grad_qkv_b,
        grad_gain,
        grad_proj_w,
        grad_proj_b,
        grad_up_w,
        grad_up_b,
        grad_down_w,
        grad_down_b,
    )


def solution(mesh):
    in_specs = (
        P("dp", None, None),
        P("dp", None, None),
        P(),
        P(None, None, ("dp", "tensor")),
        P(None, ("dp", "tensor")),
        P(None, None, None, "tensor"),
        P(None, None, "tensor"),
        P(),
        P(None, "tensor", None),
        P(),
        P(None, None, "tensor"),
        P(None, "tensor"),
        P(None, "tensor", None),
        P(),
        P("dp", None, None),
        P("dp", None, None),
    )
    out_specs = (
        P("dp", None, None),
        P("dp", None, None),
        P("dp", None, None),
        P("dp", None, None),
        P("dp", None),
        P(None, None, ("dp", "tensor")),
        P(None, ("dp", "tensor")),
        P(None, "dp", None, "tensor"),
        P(None, None, "tensor"),
        P(),
        P(None, "tensor", "dp"),
        P(),
        P(None, "dp", "tensor"),
        P(None, "tensor"),
        P(None, "tensor", "dp"),
        P(),
    )
    return jax.shard_map(
        on_device, mesh=mesh, in_specs=in_specs, out_specs=out_specs, check_vma=False
    )
```

profile of v0, /device:TPU:0, one launch (start us, length us, event | category | flops | bytes accessed | tf_op | source)
XLA Modules:
  0.0 2175.3 jit_solution(17408335903478610186)
XLA Ops:
  11.9 7.3 all-to-all-start
  42.2 24.5 %all_gather.3 = f32[3,2,8,1152]{2,1,0,3:T(2,128)} all-gather(f32[3,2,8,288]{2,1,0,3:T(2,128)S(1)} %copy.146), channel_id=1, replica_groups=mesh['dp'=8,'tensor'=4] {'tensor'}, dimensions={3}, use_global_device_ids=true | all-gather | bytes 276480 | tf_op jit(solution)/shard_map/all_gather | solution.py:267
  104.2 6.8 multiply_reduce_fusion.1
  111.0 8.2 exponential_reduce_fusion
  119.2 8.2 fusion.100
  148.0 134.2 %all-reduce.20.cloned.1.call-done = (f32[3,256,1536]{2,1,0:T(8,128)}, f32[3,154,1536]{2,1,0:T(8,128)}) async-done(((f32[3,256,1536]{2,1,0:T(8,128)}, f32[3,154,1536]{2,1,0:T(8,128)}), (f32[3,256,1536]{2,1,0:T(8,128)}, f32[3,154,1536]{2,1,0:T(8,128)})) %all-reduce.20.cloned.1.call-update) | async-done | bytes 7557136 | tf_op jit(solution)/shard_map/psum | solution.py:286
  315.5 8.5 fusion.157
  337.2 7.9 fusion.29
  349.0 10.4 fusion.37
  359.4 112.3 %all-reduce.18.cloned.1.call-done = (f32[768,1536]{1,0:T(8,128)}, f32[462,1536]{1,0:T(8,128)}) async-done(((f32[768,1536]{1,0:T(8,128)}, f32[462,1536]{1,0:T(8,128)}), (f32[768,1536]{1,0:T(8,128)}, f32[462,1536]{1,0:T(8,128)})) %all-reduce.18.cloned.1.call-update) | async-done | bytes 7557136 | tf_op jit(solution)/shard_map/psum | solution.py:323
  479.7 8.1 multiply_reduce_fusion.6
  522.4 13.9 multiply_reduce_fusion
  537.4 7.7 multiply_convert_fusion
  608.5 6.9 pad_maximum_fusion.1
  615.4 28.5 %copy.177 = f32[2,1536,1536]{1,0,2:T(2,128)} copy(f32[2,1536,1536]{2,1,0:T(8,128)} %pad_maximum_fusion.1) | data formatting | bytes 37748736 | tf_op jit(solution)/shard_map/stack | solution.py:72
  648.6 211.5 %all-reduce.16.cloned.1.call-done = (f32[3,256,1536]{2,1,0:T(8,128)}, f32[3,154,1536]{2,1,0:T(8,128)}, f32[768,1536]{1,0:T(8,128)}, f32[462,1536]{1,0:T(8,128)}) async-done(((f32[3,256,1536]{2,1,0:T(8,128)}, f32[3,154,1536]{2,1,0:T(8,128)}, f32[768,1536]{1,0:T(8,128)}, f32[462,1536]{1,0:T(8,128)}), (f32[3,256,1536]{2,1,0:T(8,128)}, f32[3,154,1536]{2,1,0:T(8,128)}, f32[768,1536]{1,0:T(8,128)}, ...) | async-done | bytes 15114256 | tf_op jit(solution)/shard_map/psum | solution.py:305
  897.1 8.2 copy.176
  920.9 7.0 convolution_bitcast_fusion.4
  933.1 10.9 pad_maximum_fusion.2
  993.0 628.5 %all-reduce.14.cloned.1.call-done = (f32[24,1536]{1,0:T(8,128)}, f32[2,384,1536]{1,0,2:T(2,128)}, f32[2,1536,1536]{1,0,2:T(2,128)}) async-done(((f32[24,1536]{1,0:T(8,128)}, f32[2,384,1536]{1,0,2:T(2,128)}, f32[2,1536,1536]{1,0,2:T(2,128)}), (f32[24,1536]{1,0:T(8,128)}, f32[2,384,1536]{1,0,2:T(2,128)}, f32[2,1536,1536]{1,0,2:T(2,128)})) %all-reduce.14.cloned.1.call-update) | async-done | bytes 23740432
  1622.3 10.9 all-reduce.5
  1633.2 38.8 %all-reduce.3 = (f32[2,3,384]{2,1,0:T(4,128)S(1)}, f32[2,2,64]{2,1,0:T(2,128)}, f32[2,1536]{1,0:T(2,128)}, f32[2,1536]{1,0:T(2,128)}, f32[2,1536]{1,0:T(2,128)}) all-reduce(f32[2,3,384]{2,1,0:T(4,128)S(1)} %pad_maximum_fusion.20, f32[2,2,64]{2,1,0:T(2,128)S(1)} %get-tuple-element.149, ...), channel_id=1, replica_groups=mesh['dp'=8,'tensor'=4] {'dp'}, use_global_device_ids=true, to_apply=%region_53.0 | all-reduce | flops 11776 | bytes 94208 | tf_op jit(solution)/shard_map/psum | solution.py:420
  1679.7 175.5 %reduce-scatter.3.cloned.1.call-done = f32[2,192,3,384]{3,1,2,0:T(8,128)} async-done(((f32[2,1536,3,384]{3,1,2,0:T(8,128)}), f32[2,192,3,384]{3,1,2,0:T(8,128)}) %reduce-scatter.3.cloned.1.call-update) | async-done | bytes 1769488 | tf_op jit(solution)/shard_map/reduce_scatter | solution.py:415
  1855.2 313.1 %reduce-scatter.5.cloned.1.call-done = f32[2,192,1536]{2,1,0:T(8,128)} async-done(((f32[2,1536,1536]{2,1,0:T(8,128)}), f32[2,192,1536]{2,1,0:T(8,128)}) %reduce-scatter.5.cloned.1.call-update) | async-done | bytes 2359312 | tf_op jit(solution)/shard_map/reduce_scatter | solution.py:417
  (534 shorter events, 359.8 us)
Async XLA Ops:
  11.9 29.5 %all-to-all-start = ((f32[24,2,288]{2,1,0:T(2,128)}), f32[24,2,288]{2,1,0:T(2,128)S(1)}, u32[]{:S(2)}, u32[]{:S(2)}) async-start(f32[24,2,288]{2,1,0:T(2,128)} %copy.145), calls=%async_computation | async-start | bytes 147456 | tf_op jit(solution)/shard_map/all_to_all | solution.py:264
  19.2 263.0 %all-reduce.20.cloned.1.call-start = ((), (), s32[]{:S(2)}) async-start(), calls=%async_computation.9 | async-start | bytes 15335424 | tf_op jit(solution)/shard_map/psum | solution.py:286
  19.7 52.9 %copy-start.96 = (f32[3,256]{1,0:T(4,128)}, f32[3,256]{1,0:T(4,128)S(1)}, u32[]{:S(2)}) copy-start(f32[3,256]{1,0:T(4,128)S(1)} %broadcast_multiply_fusion.13) | copy-start | bytes 9220
  20.4 52.1 %copy-start.112 = (f32[3,256]{1,0:T(4,128)}, f32[3,256]{1,0:T(4,128)S(1)}, u32[]{:S(2)}) copy-start(f32[3,256]{1,0:T(4,128)S(1)} %add_rsqrt_fusion.7) | copy-start | bytes 9220
  27.6 58.9 %copy-start.94 = (f32[3,154]{1,0:T(4,128)}, f32[3,154]{1,0:T(4,128)S(1)}, u32[]{:S(2)}) copy-start(f32[3,154]{1,0:T(4,128)S(1)} %broadcast_multiply_fusion.9) | copy-start | bytes 5548
  28.2 58.3 %copy-start.110 = (f32[3,154]{1,0:T(4,128)}, f32[3,154]{1,0:T(4,128)S(1)}, u32[]{:S(2)}) copy-start(f32[3,154]{1,0:T(4,128)S(1)} %add_rsqrt_fusion.6) | copy-start | bytes 5548
  29.3 73.6 %copy-start.122 = (f32[64]{0:T(128)}, f32[64]{0:T(128)S(1)}, u32[]{:S(2)}) copy-start(f32[64]{0:T(128)S(1)} %get-tuple-element.202) | copy-start | bytes 772
  29.3 73.6 %copy-start.124 = (f32[64]{0:T(128)}, f32[64]{0:T(128)S(1)}, u32[]{:S(2)}) copy-start(f32[64]{0:T(128)S(1)} %get-tuple-element.205) | copy-start | bytes 772
  84.0 18.9 copy-start.8
  100.3 18.9 copy-start.43
  139.7 332.0 %all-reduce.18.cloned.1.call-start = ((), (), s32[]{:S(2)}) async-start(), calls=%async_computation.8 | async-start | bytes 15138816 | tf_op jit(solution)/shard_map/psum | solution.py:323
  146.2 136.1 %copy-start.80 = (f32[3,1536]{1,0:T(4,128)S(1)}, f32[3,1536]{1,0:T(4,128)}, u32[]{:S(2)}) copy-start(f32[3,1536]{1,0:T(4,128)} %get-tuple-element.181) | copy-start | bytes 55300
  285.1 224.7 %copy-start.1 = (f32[3,154,1536]{2,1,0:T(8,128)}, f32[3,154,1536]{2,1,0:T(8,128)S(1)}, u32[]{:S(2)}) copy-start(f32[3,154,1536]{2,1,0:T(8,128)S(1)} %get-tuple-element.161) | copy-start | bytes 8515588
  330.9 529.2 %all-reduce.16.cloned.1.call-start = ((), (), s32[]{:S(2)}) async-start(), calls=%async_computation.7 | async-start | bytes 30474240 | tf_op jit(solution)/shard_map/psum | solution.py:305
  615.4 28.5 %copy-start.53 = (bf16[462,384]{0,1:T(8,128)(2,1)S(1)}, bf16[462,384]{0,1:T(8,128)(2,1)}, u32[]{:S(2)}) copy-start(bf16[462,384]{0,1:T(8,128)(2,1)} %copy-done.52) | copy-start | bytes 1064452
  615.4 28.5 %copy-start.70 = (bf16[462,1536]{1,0:T(8,128)(2,1)S(1)}, bf16[462,1536]{1,0:T(8,128)(2,1)}, u32[]{:S(2)}) copy-start(bf16[462,1536]{1,0:T(8,128)(2,1)} %copy-done.69) | copy-start | bytes 4257796
  648.6 215.3 %copy-start.7 = (bf16[3,154,1536]{2,1,0:T(8,128)(2,1)S(1)}, bf16[3,154,1536]{2,1,0:T(8,128)(2,1)}, u32[]{:S(2)}) copy-start(bf16[3,154,1536]{2,1,0:T(8,128)(2,1)} %param.17) | copy-start | bytes 4257796
  648.6 215.3 %copy-start.76 = (f32[3,1536]{1,0:T(4,128)S(1)}, f32[3,1536]{1,0:T(4,128)}, u32[]{:S(2)}) copy-start(f32[3,1536]{1,0:T(4,128)} %copy-done.75) | copy-start | bytes 55300
  648.6 215.3 %copy-start.95 = (f32[3,154]{1,0:T(4,128)S(1)}, f32[3,154]{1,0:T(4,128)}, u32[]{:S(2)}) copy-start(f32[3,154]{1,0:T(4,128)} %copy-done.94) | copy-start | bytes 5548
  648.6 215.3 %copy-start.111 = (f32[3,154]{1,0:T(4,128)S(1)}, f32[3,154]{1,0:T(4,128)}, u32[]{:S(2)}) copy-start(f32[3,154]{1,0:T(4,128)} %copy-done.110) | copy-start | bytes 5548
  886.7 18.6 all-to-all-start.1
  892.2 729.2 %all-reduce.14.cloned.1.call-start = ((), (), s32[]{:S(2)}) async-start(), calls=%async_computation.6 | async-start | bytes 47480832
  918.0 937.2 %reduce-scatter.3.cloned.1.call-start = ((), (), s32[]{:S(2)}) async-start(), calls=%async_computation.4 | async-start | bytes 15925248 | tf_op jit(solution)/shard_map/reduce_scatter | solution.py:415
  944.1 1224.2 %reduce-scatter.5.cloned.1.call-start = ((), (), s32[]{:S(2)}) async-start(), calls=%async_computation.5 | async-start | bytes 21233664 | tf_op jit(solution)/shard_map/reduce_scatter | solution.py:417
  (140 other events, 629.5 us)
Sparse Core Ops, SparseCore 0:
  139.8 142.3 all-reduce.19
  331.0 140.6 all-reduce.17
  595.9 264.1 all-reduce.15
  918.1 703.2 all-reduce.13
  1625.5 229.6 reduce-scatter.2
  1859.5 308.7 reduce-scatter.4
where the time goes:
time: 2180 us
  waiting for transfers between devices  1580 us (72%)
  local copies, waits for them, and re-layouts  180 us (8%)
  matrix products  161 us (7%)
  other arithmetic  154 us (7%)
  blocking collectives  74.1 us (3%)
    unnamed x7, waiting for transfers between devices  629 us
    reduce_scatter x1, waiting for transfers between devices, on_device(): lax.psum_scatter(grad_up_w, 'dp', scatter_dimension=1, tiled=True)  313 us
    psum x1, waiting for transfers between devices, on_device(): lax.psum((dot_plain(states[0]['active'], down_weight[0]), dot_plain(state...  211 us
    reduce_scatter x1, waiting for transfers between devices, on_device(): lax.psum_scatter(grad_qkv_w, 'dp', scatter_dimension=1, tiled=True)  176 us
    psum x1, waiting for transfers between devices, on_device(): lax.psum((dot_plain(attn_parts[0].reshape(-1, local_width), proj_weight[0...  134 us
    psum x1, waiting for transfers between devices, on_device(): lax.psum((dot_right_t(mlp_backs[0]['up_low'], up_weight[0]), dot_right_t(...  112 us
    unnamed x336, local copies, waits for them, and re-layouts  57.5 us
    dot_general x10, matrix products, dot_plain(): return jnp.dot(first_op, second_op, preferred_element_type=jnp.float32)  43.7 us
  transfers between devices with their start and end apart: 8, of which 6 were waited for; matrix products, arithmetic and copies ran while one was open for 9% of the time, Pallas kernels for 0%

commit v1 on v0

v1 whole, which is shorter than its diff:
```python
import functools

import jax
import jax.numpy as jnp
from jax import lax
from jax.experimental import pallas as pl
from jax.experimental.pallas import tpu as pltpu
from jax.sharding import PartitionSpec as P

epsilon = 1e-06
GELU_C = 0.7978845608028654
GELU_A = 0.044715
ROW_TILE = 16
NEG = -1e30


def dot_plain(first_op, second_op):
    return jnp.dot(first_op, second_op, preferred_element_type=jnp.float32)


def dot_right_t(first_op, second_op):
    return lax.dot_general(
        first_op, second_op, (((1,), (1,)), ((), ())), preferred_element_type=jnp.float32
    )


def dot_left_t(first_op, second_op):
    return lax.dot_general(
        first_op, second_op, (((0,), (0,)), ((), ())), preferred_element_type=jnp.float32
    )


def layer_norm(values):
    center = values - jnp.mean(values, axis=-1, keepdims=True)
    inverse = lax.rsqrt(jnp.mean(center * center, axis=-1, keepdims=True) + epsilon)
    return (center * inverse, inverse)


def norm_back(grad_normed, normed, inverse):
    return inverse * (
        grad_normed
        - jnp.mean(grad_normed, axis=-1, keepdims=True)
        - normed * jnp.mean(grad_normed * normed, axis=-1, keepdims=True)
    )


def gelu_both(values):
    inner = jnp.tanh(GELU_C * (values + GELU_A * values * values * values))
    active = 0.5 * values * (1.0 + inner)
    slope = 0.5 * (1.0 + inner) + 0.5 * values * (1.0 - inner * inner) * GELU_C * (
        1.0 + 3.0 * GELU_A * values * values
    )
    return active, slope


def head_norm(values, gain):
    head_dim = values.shape[1] // 2
    lower = lax.broadcasted_iota(jnp.int32, values.shape, 1) < head_dim
    square = values * values
    first = jnp.sum(jnp.where(lower, square, 0.0), axis=-1, keepdims=True) / head_dim
    second = jnp.sum(jnp.where(lower, 0.0, square), axis=-1, keepdims=True) / head_dim
    factor = jnp.where(lower, lax.rsqrt(first + epsilon), lax.rsqrt(second + epsilon))
    return values * factor * gain, factor


def rows_of(img_ref, txt_ref, cols):
    return jnp.concatenate(
        [img_ref[0, 0, :, cols], img_ref[1, 0, :, cols], txt_ref[0, 0, :, cols], txt_ref[1, 0, :, cols]],
        axis=0,
    )


def put_rows(img_ref, txt_ref, cols, values):
    img, txt = img_ref.shape[2], txt_ref.shape[2]
    img_ref[0, 0, :, cols] = values[:img]
    img_ref[1, 0, :, cols] = values[img : 2 * img]
    txt_ref[0, 0, :, cols] = values[2 * img : 2 * img + txt]
    txt_ref[1, 0, :, cols] = values[2 * img + txt :]


def gain_rows(gain_ref, which, img, txt):
    width = gain_ref.shape[2]
    return jnp.concatenate(
        [
            jnp.broadcast_to(gain_ref[0, which : which + 1, :], (2 * img, width)),
            jnp.broadcast_to(gain_ref[1, which : which + 1, :], (2 * txt, width)),
        ],
        axis=0,
    )


def key_bias(img, txt, real):
    where = lax.broadcasted_iota(jnp.int32, (1, 2 * (img + txt)), 1)
    first = where - 2 * img
    gone = ((first >= real) & (first < txt)) | (first >= txt + real)
    return jnp.where(gone, NEG, 0.0).astype(jnp.float32)


def probs(q_head, k_low, bias):
    scores = dot_right_t(q_head, k_low) + bias
    top = jnp.max(scores, axis=-1, keepdims=True)
    weights = jnp.exp(scores - top)
    return weights * (1.0 / jnp.sum(weights, axis=-1, keepdims=True))


def attn_forward_kernel(real, gain_ref, img_ref, txt_ref, out_img_ref, out_txt_ref):
    img, txt = img_ref.shape[2], txt_ref.shape[2]
    local = img_ref.shape[3] // 3
    pair = gain_ref.shape[2]
    q_gain, k_gain = gain_rows(gain_ref, 0, img, txt), gain_rows(gain_ref, 1, img, txt)
    bias = key_bias(img, txt, real)
    scale = (pair // 2) ** (-0.5)
    for start in range(0, local, pair):
        q_raw, k_raw, v_raw = (
            rows_of(img_ref, txt_ref, slice(part * local + start, part * local + start + pair))
            for part in range(3)
        )
        q_low = head_norm(q_raw, q_gain)[0].astype(jnp.bfloat16) * jnp.bfloat16(scale)
        k_low = head_norm(k_raw, k_gain)[0].astype(jnp.bfloat16)
        v_low = v_raw.astype(jnp.bfloat16)
        lower = lax.broadcasted_iota(jnp.int32, q_raw.shape, 1) < pair // 2
        results = []
        for head in range(2):
            mine = lower if head == 0 else jnp.logical_not(lower)
            q_head = jnp.where(mine, q_low, jnp.bfloat16(0))
            results.append(dot_plain(probs(q_head, k_low, bias).astype(jnp.bfloat16), v_low))
        out = jnp.where(lower, results[0], results[1]).astype(jnp.bfloat16)
        put_rows(out_img_ref, out_txt_ref, slice(start, start + pair), out)


def attn_backward_kernel(
    real, gain_ref, img_ref, txt_ref, d_img_ref, d_txt_ref, o_img_ref, o_txt_ref, bias_ref, dgain_ref
):
    img, txt = img_ref.shape[2], txt_ref.shape[2]
    local = img_ref.shape[3] // 3
    pair = gain_ref.shape[2]
    head_dim = pair // 2
    q_gain, k_gain = gain_rows(gain_ref, 0, img, txt), gain_rows(gain_ref, 1, img, txt)
    bias = key_bias(img, txt, real)
    scale = head_dim ** (-0.5)
    gain_sums = [[None, None], [None, None]]
    for start in range(0, local, pair):
        q_raw, k_raw, v_raw = (
            rows_of(img_ref, txt_ref, slice(part * local + start, part * local + start + pair))
            for part in range(3)
        )
        q_wide, q_factor = head_norm(q_raw, q_gain)
        k_wide, k_factor = head_norm(k_raw, k_gain)
        q_low = q_wide.astype(jnp.bfloat16) * jnp.bfloat16(scale)
        k_low = k_wide.astype(jnp.bfloat16)
        v_low = v_raw.astype(jnp.bfloat16)
        grad_out = rows_of(d_img_ref, d_txt_ref, slice(start, start + pair))
        lower = lax.broadcasted_iota(jnp.int32, q_raw.shape, 1) < head_dim
        parts = []
        for head in range(2):
            mine = lower if head == 0 else jnp.logical_not(lower)
            prob = probs(jnp.where(mine, q_low, jnp.bfloat16(0)), k_low, bias)
            grad_v = dot_left_t(prob.astype(jnp.bfloat16), grad_out)
            grad_prob = dot_right_t(jnp.where(mine, grad_out, jnp.bfloat16(0)), v_low)
            delta = jnp.sum(prob * grad_prob, axis=-1, keepdims=True)
            grad_scores = (prob * (grad_prob - delta)).astype(jnp.bfloat16)
            parts.append((dot_plain(grad_scores, k_low), dot_left_t(grad_scores, q_low), grad_v))
        grad_qn = jnp.where(lower, parts[0][0], parts[1][0]) * scale
        grad_kn = jnp.where(lower, parts[0][1], parts[1][1])
        grad_vn = jnp.where(lower, parts[0][2], parts[1][2])

        def raw_grad(grad_normed, raw, factor, gain, which):
            gained = grad_normed * gain
            product = gained * raw
            first = jnp.sum(jnp.where(lower, product, 0.0), axis=-1, keepdims=True) / head_dim
            second = jnp.sum(jnp.where(lower, 0.0, product), axis=-1, keepdims=True) / head_dim
            inner = jnp.where(lower, first, second)
            terms = grad_normed * raw * factor
            for stream, rows in enumerate((slice(0, 2 * img), slice(2 * img, 2 * (img + txt)))):
                total = jnp.sum(terms[rows], axis=0, keepdims=True)
                old = gain_sums[stream][which]
                gain_sums[stream][which] = total if old is None else old + total
            return factor * gained - raw * (factor * factor * factor) * inner

        grads = (
            raw_grad(grad_qn, q_raw, q_factor, q_gain, 0),
            raw_grad(grad_kn, k_raw, k_factor, k_gain, 1),
            grad_vn,
        )
        for part, grad in enumerate(grads):
            cols = slice(part * local + start, part * local + start + pair)
            bias_ref[0, 0:1, cols] = jnp.sum(grad[: 2 * img], axis=0, keepdims=True)
            bias_ref[0, 1:2, cols] = jnp.sum(grad[2 * img :], axis=0, keepdims=True)
            put_rows(o_img_ref, o_txt_ref, cols, grad.astype(jnp.bfloat16))
    for stream in range(2):
        for which in range(2):
            row = stream * 2 + which
            dgain_ref[0, row : row + 1, :] = gain_sums[stream][which]


def block_of(array):
    shape = array.shape
    return pl.BlockSpec((shape[0], 1) + shape[2:], lambda seq: (0, seq, 0, 0))


def whole_of(array):
    return pl.BlockSpec(array.shape, lambda seq: (0,) * array.ndim)


def attn_forward(gain_pair, packed_img, packed_txt, real):
    seqs = packed_img.shape[1]
    local = packed_img.shape[3] // 3
    outs = [
        jax.ShapeDtypeStruct(packed.shape[:3] + (local,), jnp.bfloat16)
        for packed in (packed_img, packed_txt)
    ]
    rows = 2 * (packed_img.shape[2] + packed_txt.shape[2])
    return pl.pallas_call(
        functools.partial(attn_forward_kernel, real),
        grid=(seqs,),
        out_shape=outs,
        in_specs=[whole_of(gain_pair), block_of(packed_img), block_of(packed_txt)],
        out_specs=[block_of(out) for out in outs],
        compiler_params=pltpu.CompilerParams(vmem_limit_bytes=48 << 20),
        cost_estimate=pl.CostEstimate(
            flops=seqs * rows * rows * local * 4,
            bytes_accessed=seqs * rows * local * 14,
            transcendentals=seqs * rows * rows * (local // 64),
        ),
        name="attn_forward",
    )(gain_pair, packed_img, packed_txt)


def attn_backward(gain_pair, packed_img, packed_txt, grad_img, grad_txt, real):
    seqs = packed_img.shape[1]
    local = packed_img.shape[3] // 3
    outs = [
        jax.ShapeDtypeStruct(packed_img.shape, jnp.bfloat16),
        jax.ShapeDtypeStruct(packed_txt.shape, jnp.bfloat16),
        jax.ShapeDtypeStruct((seqs, 2, 3 * local), jnp.float32),
        jax.ShapeDtypeStruct((seqs, 4, gain_pair.shape[2]), jnp.float32),
    ]
    rows = 2 * (packed_img.shape[2] + packed_txt.shape[2])
    return pl.pallas_call(
        functools.partial(attn_backward_kernel, real),
        grid=(seqs,),
        out_shape=outs,
        in_specs=[whole_of(gain_pair)]
        + [block_of(each) for each in (packed_img, packed_txt, grad_img, grad_txt)],
        out_specs=[
            block_of(outs[0]),
            block_of(outs[1]),
            pl.BlockSpec((1, 2, 3 * local), lambda seq: (seq, 0, 0)),
            pl.BlockSpec((1, 4, gain_pair.shape[2]), lambda seq: (seq, 0, 0)),
        ],
        compiler_params=pltpu.CompilerParams(vmem_limit_bytes=56 << 20),
        cost_estimate=pl.CostEstimate(
            flops=seqs * rows * rows * local * 10,
            bytes_accessed=seqs * rows * local * 20,
            transcendentals=seqs * rows * rows * (local // 64),
        ),
        name="attn_backward",
    )(gain_pair, packed_img, packed_txt, grad_img, grad_txt)


def xor_index(index, distance):
    return index + distance - 2 * distance * ((index // distance) % 2)


def peers_of(data_size, tensor_size):
    row, col = lax.axis_index("dp"), lax.axis_index("tensor")
    around = [(lax.rem(row + step, data_size), col) for step in range(1, data_size)]
    across = []
    distance = 1
    while distance < tensor_size:
        across.append((row, xor_index(col, distance)))
        distance *= 2
    return row, col, around, across


def greet(partners):
    barrier = pltpu.get_barrier_semaphore()
    for partner in partners:
        pl.semaphore_signal(barrier, inc=1, device_id=partner, device_id_type=pl.DeviceIdType.MESH)
    pl.semaphore_wait(barrier, len(partners))


def remote(source, target, sems, index, partner):
    copy = pltpu.make_async_remote_copy(
        src_ref=source,
        dst_ref=target,
        send_sem=sems.at[0, index],
        recv_sem=sems.at[1, index],
        device_id=partner,
        device_id_type=pl.DeviceIdType.MESH,
    )
    copy.start()
    return copy


def silu_of(cond_ref):
    wide = cond_ref[...].astype(jnp.float32)
    return (wide * (1.0 / (1.0 + jnp.exp(-wide)))).astype(jnp.bfloat16)


def mod_forward_kernel(
    data_size, tensor_size, cond_ref, weight_ref, bias_ref, out_ref, outgoing, blocks, sems
):
    row, col, around, across = peers_of(data_size, tensor_size)
    seqs, feat = out_ref.shape[1], out_ref.shape[2]
    silu_cond = silu_of(cond_ref)
    for stream in range(2):
        values = dot_plain(silu_cond, weight_ref[stream]) + bias_ref[stream : stream + 1].astype(
            jnp.float32
        )
        for index in range(data_size):
            outgoing[index, stream * seqs : (stream + 1) * seqs] = values[
                index * seqs : (index + 1) * seqs
            ]
    blocks[col, row] = outgoing[row]
    greet(around + across)
    copies = [
        remote(outgoing.at[partner[0]], blocks.at[col, row], sems, index, partner)
        for index, partner in enumerate(around)
    ]
    for copy in copies:
        copy.wait()
    held, used = [0], len(around)
    for level in reversed(range(len(across))):
        distance = 1 << level
        copies = []
        for offset in held:
            index = col
            for bit in range(len(across)):
                if offset >> bit & 1:
                    index = xor_index(index, 1 << bit)
            copies.append(remote(blocks.at[index], blocks.at[index], sems, used, across[level]))
            used += 1
        for copy in copies:
            copy.wait()
        held = held + [offset | distance for offset in held]
    for stream in range(2):
        full = jnp.concatenate(
            [
                blocks[second, first, stream * seqs : (stream + 1) * seqs]
                for first in range(data_size)
                for second in range(tensor_size)
            ],
            axis=1,
        )
        for index in range(6):
            out_ref[stream * 6 + index] = full[:, index * feat : (index + 1) * feat]


def mod_forward(conditioning, ada_weight, ada_bias, seqs, feat, data_size, tensor_size):
    cols = ada_weight.shape[2]
    vmem = pl.BlockSpec(memory_space=pltpu.VMEM)
    return pl.pallas_call(
        functools.partial(mod_forward_kernel, data_size, tensor_size),
        out_shape=jax.ShapeDtypeStruct((12, seqs, feat), jnp.float32),
        in_specs=[vmem] * 3,
        out_specs=vmem,
        scratch_shapes=[
            pltpu.VMEM((data_size, 2 * seqs, cols), jnp.float32),
            pltpu.VMEM((tensor_size, data_size, 2 * seqs, cols), jnp.float32),
            pltpu.SemaphoreType.DMA((2, data_size + tensor_size)),
        ],
        compiler_params=pltpu.CompilerParams(
            collective_id=0, has_side_effects=True, vmem_limit_bytes=32 << 20
        ),
        name="mod_forward",
    )(conditioning, ada_weight, ada_bias)


def mod_backward_kernel(
    data_size,
    tensor_size,
    mod_ref,
    cond_ref,
    weight_ref,
    group_ref,
    all_ref,
    weight_out,
    bias_out,
    silu_out,
    group_out,
    all_out,
    blocks,
    core_in,
    outgoing,
    cols_in,
    group_in,
    all_in,
    group_own,
    all_own,
    silu_blocks,
    silu_in,
    silu_send,
    silu_recv,
    all_send,
    all_recv,
    sems,
):
    row, col, around, across = peers_of(data_size, tensor_size)
    seqs, feat = silu_out.shape
    cols = bias_out.shape[1]
    for stream in range(2):
        full = jnp.concatenate([mod_ref[stream * 6 + index] for index in range(6)], axis=1)
        for first in range(data_size):
            for second in range(tensor_size):
                start = (first * tensor_size + second) * cols
                blocks[second, first, stream * seqs : (stream + 1) * seqs] = full[
                    :, start : start + cols
                ]
    silu_cond = silu_of(cond_ref)
    greet(around + across)

    used = 0
    copy = remote(blocks.at[xor_index(col, 1)], core_in, sems, used, across[0])
    used += 1
    copy.wait()
    for first in range(data_size):
        outgoing[first] = blocks[col, first] + core_in[first]

    cols_in[row] = outgoing[row]
    group_in[row] = group_ref[row]
    all_in[row] = all_ref[row]
    copies = []
    for partner in around:
        for source, target in ((group_ref, group_in), (all_ref, all_in), (outgoing, cols_in)):
            copies.append(
                remote(source.at[partner[0]], target.at[row], sems, used, partner)
            )
            used += 1
    for copy in copies:
        copy.wait()
    group_own[...] = functools.reduce(jnp.add, [group_in[index] for index in range(data_size)])
    all_own[...] = functools.reduce(jnp.add, [all_in[index] for index in range(data_size)])
    low = []
    for stream in range(2):
        wide = jnp.concatenate(
            [cols_in[index, stream * seqs : (stream + 1) * seqs] for index in range(data_size)],
            axis=0,
        )
        bias_out[stream : stream + 1] = jnp.sum(wide, axis=0, keepdims=True)
        low.append(wide.astype(jnp.bfloat16))
    silu_grad = dot_right_t(low[0], weight_ref[0]) + dot_right_t(low[1], weight_ref[1])
    for index in range(data_size):
        silu_blocks[index] = silu_grad[index * seqs : (index + 1) * seqs]
    for stream in range(2):
        weight_out[stream] = dot_left_t(silu_cond, low[stream])

    silu_in[row] = silu_blocks[row]
    group_out[row] = group_own[...]
    all_send[0, row] = all_own[...]
    copies = []
    for partner in around:
        for source, target in (
            (silu_blocks.at[partner[0]], silu_in.at[row]),
            (group_own, group_out.at[row]),
            (all_own, all_send.at[0, row]),
        ):
            copies.append(remote(source, target, sems, used, partner))
            used += 1
    for copy in copies:
        copy.wait()
    silu_send[0] = functools.reduce(jnp.add, [silu_in[index] for index in range(data_size)])

    for level, partner in enumerate(across):
        copies = [
            remote(silu_send.at[level], silu_recv.at[level], sems, used, partner),
            remote(all_send.at[level], all_recv.at[level], sems, used + 1, partner),
        ]
        used += 2
        for copy in copies:
            copy.wait()
        silu_send[level + 1] = silu_send[level] + silu_recv[level]
        all_send[level + 1] = all_send[level] + all_recv[level]
    silu_out[...] = silu_send[len(across)]
    all_out[...] = all_send[len(across)]


def mod_backward(mod_grads, conditioning, ada_weight, group, every, data_size, tensor_size):
    _, seqs, feat = mod_grads.shape
    cols = ada_weight.shape[2]
    levels = tensor_size.bit_length() - 1
    group_size, every_size = group.shape[-1], every.shape[-1]
    vmem = pl.BlockSpec(memory_space=pltpu.VMEM)

    def wide(*shape):
        return pltpu.VMEM(shape, jnp.float32)

    return pl.pallas_call(
        functools.partial(mod_backward_kernel, data_size, tensor_size),
        out_shape=[
            jax.ShapeDtypeStruct(ada_weight.shape, jnp.float32),
            jax.ShapeDtypeStruct((2, cols), jnp.float32),
            jax.ShapeDtypeStruct((seqs, feat), jnp.float32),
            jax.ShapeDtypeStruct(group.shape, jnp.float32),
            jax.ShapeDtypeStruct(every.shape, jnp.float32),
        ],
        in_specs=[vmem] * 5,
        out_specs=[vmem] * 5,
        scratch_shapes=[
            wide(tensor_size, data_size, 2 * seqs, cols),
            wide(data_size, 2 * seqs, cols),
            wide(data_size, 2 * seqs, cols),
            wide(data_size, 2 * seqs, cols),
            wide(*group.shape),
            wide(*every.shape),
            wide(1, group_size),
            wide(1, every_size),
            wide(data_size, seqs, feat),
            wide(data_size, seqs, feat),
            wide(levels + 1, seqs, feat),
            wide(levels, seqs, feat),
            wide(levels + 1, *every.shape),
            wide(levels, *every.shape),
            pltpu.SemaphoreType.DMA((2, 1 + 6 * (data_size - 1) + 2 * levels)),
        ],
        compiler_params=pltpu.CompilerParams(
            collective_id=1, has_side_effects=True, vmem_limit_bytes=48 << 20
        ),
        name="mod_backward",
    )(mod_grads, conditioning, ada_weight, group, every)


def swap_pairs(size, distance):
    return [(index, index ^ distance) for index in range(size)]


def tensor_sum(own_part, other_part, tensor_size):
    total = own_part + lax.ppermute(other_part, "tensor", swap_pairs(tensor_size, 1))
    distance = 2
    while distance < tensor_size:
        total = total + lax.ppermute(total, "tensor", swap_pairs(tensor_size, distance))
        distance *= 2
    return total


def share(own_rows, tensor_size):
    other = lax.ppermute(own_rows, "tensor", swap_pairs(tensor_size, 1))
    return jnp.stack([own_rows, other])


def ring_order(mesh):
    size = mesh.shape["dp"]
    fallback = list(range(0, size, 2)) + list(range(1, size, 2))[::-1]
    axis = list(mesh.axis_names).index("dp")
    devices = mesh.devices
    line = [devices[(slice(None),) * axis + (index,)].flatten()[0] for index in range(size)]
    coords = [getattr(device, "coords", None) for device in line]
    if any(place is None for place in coords):
        return fallback
    near = [
        [
            other
            for other in range(size)
            if sum(abs(a - b) for a, b in zip(coords[index], coords[other])) == 1
        ]
        for index in range(size)
    ]
    path, seen, budget = [0], {0}, [200000]

    def extend():
        budget[0] -= 1
        if budget[0] < 0:
            return False
        if len(path) == size:
            return path[0] in near[path[-1]]
        choices = [index for index in near[path[-1]] if index not in seen]
        choices.sort(key=lambda index: (sum(o not in seen for o in near[index]), index))
        for index in choices:
            path.append(index)
            seen.add(index)
            if extend():
                return True
            path.pop()
            seen.remove(index)
        return False

    return path if extend() else fallback


def ring_scatter(grad, order):
    size = len(order)
    ahead = [(order[index], order[(index + 1) % size]) for index in range(size)]
    back = [(second, first) for first, second in ahead]
    place = jnp.array([order.index(index) for index in range(size)], jnp.int32)[lax.axis_index("dp")]
    blocks = jnp.array(order, jnp.int32)
    halves = grad.reshape(size, 2, grad.shape[0] // (2 * size), grad.shape[1])

    def block(offset, way):
        index = blocks[(place + offset) % size]
        return lax.dynamic_slice(
            halves, (index, way, 0, 0), (1, 1) + halves.shape[2:]
        ).reshape(halves.shape[2:])

    first, second = block(size - 1, 0), block(1, 1)
    for step in range(size - 1):
        first = lax.ppermute(first, "dp", ahead) + block(2 * size - 2 - step, 0)
        second = lax.ppermute(second, "dp", back) + block(2 + step, 1)
    return jnp.concatenate([first, second], axis=0)


def on_device(
    order,
    tensor_size,
    input_img,
    input_txt,
    conditioning,
    ada_weight,
    ada_bias,
    qkv_weight,
    qkv_bias,
    norm_gain,
    proj_weight,
    proj_bias,
    up_weight,
    up_bias,
    down_weight,
    down_bias,
    cotangent_img,
    cotangent_txt,
):
    data_size = len(order)
    seqs, _, feat = input_img.shape
    core = lax.axis_index("tensor") % 2
    reals = (input_img.shape[1] // 2, input_txt.shape[1] // 2)

    def split_rows(array):
        half = array.shape[1] // 2
        pad = -half % ROW_TILE
        lower, upper = (
            jnp.pad(part, ((0, 0), (0, pad), (0, 0))) for part in (array[:, :half], array[:, half:])
        )
        first = core == 0
        return jnp.stack([jnp.where(first, lower, upper), jnp.where(first, upper, lower)])

    def join_rows(halves, real):
        own, other = halves.astype(jnp.bfloat16)
        first = core == 0
        lower, upper = jnp.where(first, own, other), jnp.where(first, other, own)
        return jnp.concatenate([lower[:, :real], upper[:, :real]], axis=1)

    modulate = mod_forward(
        conditioning, ada_weight, ada_bias, seqs, feat, data_size, tensor_size
    )
    piece = [
        [modulate[stream * 6 + index][:, None, :] for index in range(6)] for stream in range(2)
    ]

    inputs = [split_rows(input_img), split_rows(input_txt)]
    cotangents = [split_rows(cotangent_img), split_rows(cotangent_txt)]
    shapes = [array.shape for array in inputs]
    gain_pair = jnp.concatenate([norm_gain, norm_gain], axis=2)

    hidden1, packed, stats1 = [], [], []
    weights_in = [qkv_weight[stream].reshape(feat, -1) for stream in range(2)]
    for stream in range(2):
        normed, inverse = layer_norm(inputs[stream].astype(jnp.float32))
        hidden = (normed * (1.0 + piece[stream][1]) + piece[stream][0]).astype(jnp.bfloat16)
        hidden = hidden.reshape(-1, feat)
        flat = dot_plain(hidden, weights_in[stream]) + qkv_bias[stream].reshape(-1).astype(
            jnp.float32
        )
        hidden1.append(hidden)
        packed.append(flat.reshape(shapes[stream][:3] + (-1,)))
        stats1.append((normed[0], inverse[0]))
    attn = attn_forward(gain_pair, packed[0], packed[1], reals[1])
    local = attn[0].shape[3]

    down_rings, up_rings = [None, None], [None, None]
    state = [None, None]
    hidden_sums, mlp_sums = [None, None], [None, None]
    up_bias_sums = [None, None]
    for stream in (1, 0):
        rows = attn[stream].reshape(2, -1, local)
        other_part = dot_plain(rows[1], proj_weight[stream])
        own_part = dot_plain(rows[0], proj_weight[stream])
        total = tensor_sum(own_part, other_part, tensor_size).reshape(shapes[stream][1:])
        branch = total + proj_bias[stream]
        residual = inputs[stream][0].astype(jnp.float32) + piece[stream][2] * branch
        normed, inverse = layer_norm(residual)
        hidden = share(normed, tensor_size) * (1.0 + piece[stream][4]) + piece[stream][3]
        hidden = hidden.astype(jnp.bfloat16).reshape(-1, feat)
        upward = dot_plain(hidden, up_weight[stream]) + up_bias[stream].astype(jnp.float32)
        active, slope = gelu_both(upward)
        active = active.astype(jnp.bfloat16)
        grad_mlp = cotangents[stream].astype(jnp.float32) * piece[stream][5]
        grad_mlp_low = grad_mlp.astype(jnp.bfloat16).reshape(-1, feat)
        grad_up = dot_right_t(grad_mlp_low, down_weight[stream]) * slope
        grad_up_low = grad_up.astype(jnp.bfloat16)
        up_bias_sums[stream] = jnp.sum(grad_up, axis=0)
        half = grad_up_low.shape[0] // 2
        down_rings[stream] = ring_scatter(dot_left_t(grad_mlp_low, active), order)
        up_rings[stream] = ring_scatter(dot_left_t(hidden, grad_up_low), order)
        other_part = dot_right_t(grad_up_low[half:], up_weight[stream])
        own_part = dot_right_t(grad_up_low[:half], up_weight[stream])
        hidden_sums[stream] = tensor_sum(own_part, other_part, tensor_size)
        other_part = dot_plain(active[half:], down_weight[stream])
        own_part = dot_plain(active[:half], down_weight[stream])
        mlp_sums[stream] = tensor_sum(own_part, other_part, tensor_size)
        state[stream] = (branch, normed, inverse, jnp.sum(grad_mlp[0], axis=(0, 1)))

    grad_attn, proj_rings, proj_sums, resid_grads, mod_grads = (
        [None, None],
        [None, None],
        [None, None],
        [None, None],
        [None, None],
    )
    outputs = [None, None]
    for stream in (1, 0):
        branch, normed, inverse, _ = state[stream]
        grad_out = cotangents[stream][0].astype(jnp.float32)
        grad_hidden = hidden_sums[stream].reshape(normed.shape)
        through = norm_back(grad_hidden * (1.0 + piece[stream][4]), normed, inverse)
        grad_resid = grad_out + through
        grad_branch = share(grad_resid, tensor_size) * piece[stream][2]
        branch_low = grad_branch.astype(jnp.bfloat16).reshape(-1, feat)
        grad_attn[stream] = (
            dot_right_t(branch_low, proj_weight[stream])
            .astype(jnp.bfloat16)
            .reshape(attn[stream].shape)
        )
        proj_rings[stream] = ring_scatter(
            dot_left_t(branch_low, attn[stream].reshape(-1, local)), order
        )
        proj_sums[stream] = jnp.sum(grad_resid * piece[stream][2], axis=(0, 1))
        resid_grads[stream] = through
        mod_grads[stream] = [
            None,
            None,
            jnp.sum(grad_resid * branch, axis=1),
            jnp.sum(grad_hidden, axis=1),
            jnp.sum(grad_hidden * normed, axis=1),
            None,
        ]
    grad_packed = attn_backward(gain_pair, packed[0], packed[1], grad_attn[0], grad_attn[1], reals[1])
    qkv_bias_sums = jnp.sum(grad_packed[2], axis=0)
    gain_sums = jnp.sum(grad_packed[3], axis=0)
    head_dim = norm_gain.shape[2]
    gain_sums = gain_sums[:, :head_dim] + gain_sums[:, head_dim:]
    qkv_rings, first_sums = [None, None], [None, None]
    for stream in (1, 0):
        packed_low = grad_packed[stream].reshape(-1, 3 * local)
        half = packed_low.shape[0] // 2
        other_part = dot_right_t(packed_low[half:], weights_in[stream])
        own_part = dot_right_t(packed_low[:half], weights_in[stream])
        first_sums[stream] = tensor_sum(own_part, other_part, tensor_size)
        qkv_rings[stream] = ring_scatter(dot_left_t(hidden1[stream], packed_low), order)

    grad_inputs = [None, None]
    for stream in (1, 0):
        branch = state[stream][0]
        grad_out = cotangents[stream][0].astype(jnp.float32)
        mlp_out = mlp_sums[stream].reshape(branch.shape) + down_bias[stream]
        added = piece[stream][2] * branch + piece[stream][5] * mlp_out
        outputs[stream] = join_rows(
            inputs[stream].astype(jnp.float32) + share(added, tensor_size), reals[stream]
        )
        mod_grads[stream][5] = jnp.sum(grad_out * mlp_out, axis=1)
        normed, inverse = stats1[stream]
        grad_hidden = first_sums[stream].reshape(normed.shape)
        added = resid_grads[stream] + norm_back(
            grad_hidden * (1.0 + piece[stream][1]), normed, inverse
        )
        grad_inputs[stream] = join_rows(
            cotangents[stream].astype(jnp.float32) + share(added, tensor_size), reals[stream]
        )
        mod_grads[stream][0] = jnp.sum(grad_hidden, axis=1)
        mod_grads[stream][1] = jnp.sum(grad_hidden * normed, axis=1)

    row_share = 2.0 / tensor_size
    parts = (
        (qkv_bias_sums, jnp.stack(up_bias_sums)),
        (
            gain_sums,
            jnp.stack(proj_sums) * row_share,
            jnp.stack([state[0][3], state[1][3]]) * row_share,
        ),
    )
    vectors = [
        jnp.concatenate([each.reshape(-1) for each in group]).reshape(data_size, 1, -1)
        for group in parts
    ]
    grad_ada_weight, grad_ada_bias, silu_rows, *vectors = mod_backward(
        jnp.stack(mod_grads[0] + mod_grads[1]),
        conditioning,
        ada_weight,
        vectors[0],
        vectors[1],
        data_size,
        tensor_size,
    )
    sums = []
    for group, vector in zip(parts, vectors):
        flat, start = vector.reshape(-1), 0
        for each in group:
            sums.append(flat[start : start + each.size].reshape(each.shape))
            start += each.size
    qkv_bias_sums, up_bias_sums, gain_sums, proj_sums, down_sums = sums
    own_cond = lax.dynamic_slice_in_dim(
        conditioning, lax.axis_index("dp") * seqs, seqs, axis=0
    ).astype(jnp.float32)
    own_sig = jax.nn.sigmoid(own_cond)
    grad_conditioning = silu_rows * own_sig * (1.0 + own_cond * (1.0 - own_sig))
    return (
        outputs[0],
        outputs[1],
        grad_inputs[0],
        grad_inputs[1],
        grad_conditioning,
        grad_ada_weight,
        grad_ada_bias,
        jnp.stack([ring.reshape(ring.shape[0], 3, -1) for ring in qkv_rings]),
        qkv_bias_sums.reshape(2, 3, -1),
        gain_sums.reshape(norm_gain.shape),
        jnp.stack([ring.T for ring in proj_rings]),
        proj_sums,
        jnp.stack(up_rings),
        up_bias_sums,
        jnp.stack([ring.T for ring in down_rings]),
        down_sums,
    )


def solution(mesh):
    in_specs = (
        P("dp", None, None),
        P("dp", None, None),
        P(),
        P(None, None, ("dp", "tensor")),
        P(None, ("dp", "tensor")),
        P(None, None, None, "tensor"),
        P(None, None, "tensor"),
        P(),
        P(None, "tensor", None),
        P(),
        P(None, None, "tensor"),
        P(None, "tensor"),
        P(None, "tensor", None),
        P(),
        P("dp", None, None),
        P("dp", None, None),
    )
    out_specs = (
        P("dp", None, None),
        P("dp", None, None),
        P("dp", None, None),
        P("dp", None, None),
        P("dp", None),
        P(None, None, ("dp", "tensor")),
        P(None, ("dp", "tensor")),
        P(None, "dp", None, "tensor"),
        P(None, None, "tensor"),
        P(),
        P(None, "tensor", "dp"),
        P(),
        P(None, "dp", "tensor"),
        P(None, "tensor"),
        P(None, "tensor", "dp"),
        P(),
    )
    return jax.shard_map(
        functools.partial(on_device, ring_order(mesh), mesh.shape["tensor"]),
        mesh=mesh,
        in_specs=in_specs,
        out_specs=out_specs,
        check_vma=False,
    )
```

time: 2180 us -> 1090 us (0.50)
  waiting for transfers between devices: 1580 us -> 465 us
  starting transfers between devices: 13.9 us -> 122 us
  Pallas kernels: 0 us -> 81.3 us
  local copies, waits for them, and re-layouts: 180 us -> 103 us
  blocking collectives: 74.1 us -> 0 us
  matrix products: 161 us -> 118 us
  between operations: 17.7 us -> 39.6 us
    unnamed x7 -> x0, waiting for transfers between devices: 629 us -> none
    reduce_scatter x2 -> x0, waiting for transfers between devices: 489 us -> none  [the longest x1 313 us: on_device(): lax.psum_scatter(grad_up_w, 'dp', scatter_dimension=1, tiled=True)]
    ppermute x0 -> x136, waiting for transfers between devices: none -> 465 us  [the longest x56 214 us: ring_scatter(): first = lax.ppermute(first, 'dp', ahead) + block(2 * size - 2 - step, 0)]
    psum x3 -> x0, waiting for transfers between devices: 458 us -> none  [the longest x1 211 us: on_device(): lax.psum((dot_plain(states[0]['active'], down_weight[0]), dot_plain(state...]
    ppermute x0 -> x136, starting transfers between devices: none -> 122 us  [the longest x56 72.7 us: ring_scatter(): first = lax.ppermute(first, 'dp', ahead) + block(2 * size - 2 - step, 0)]
    pallas_call x0 -> x4, Pallas kernels: none -> 81.3 us  [the longest x1 25.4 us: mod_backward(): pl.pallas_call(functools.partial(mod_backward_kernel, data_size, tensor_s...]
    psum x2 -> x0, blocking collectives: 49.7 us -> none  [the longest x1 38.8 us: on_device(): lax.psum((paired(qkv_backs, 'qkv_b'), gain_sum, paired(resid_backs, 'proj...]
    add x3 -> x63, other arithmetic: 0.92 us -> 45.5 us  [the longest x53 28.5 us: ring_scatter(): first = lax.ppermute(first, 'dp', ahead) + block(2 * size - 2 - step, 0)]
  transfers between devices with their start and end apart: 8 -> 136, of which waited for: 6 -> 86; matrix products, arithmetic and copies ran while one was open for 9% -> 26% of each run, Pallas kernels for 0% -> 4%
where the time goes in v1:
time: 1090 us; the launch traced here: 1080 us
  waiting for transfers between devices  465 us (43%)
  other arithmetic  150 us (14%)
  starting transfers between devices  122 us (11%)
  matrix products  118 us (11%)
  local copies, waits for them, and re-layouts  103 us (9%)
  Pallas kernels  81.3 us (7%)
  between operations  39.6 us (4%)
    ppermute x56, waiting for transfers between devices, ring_scatter(): first = lax.ppermute(first, 'dp', ahead) + block(2 * size - 2 - step, 0)  214 us
    ppermute x56, waiting for transfers between devices, ring_scatter(): second = lax.ppermute(second, 'dp', back) + block(2 + step, 1)  127 us
    ppermute x8, waiting for transfers between devices, tensor_sum(): lax.ppermute(total, 'tensor', swap_pairs(tensor_size, distance))  120 us
    ppermute x56, starting transfers between devices, ring_scatter(): first = lax.ppermute(first, 'dp', ahead) + block(2 * size - 2 - step, 0)  72.7 us
    dot_general x12, matrix products, dot_plain(): return jnp.dot(first_op, second_op, preferred_element_type=jnp.float32)  44.7 us
    unnamed x408, local copies, waits for them, and re-layouts  42.9 us
    dot_general x12, matrix products, dot_right_t(): lax.dot_general(first_op, second_op, (((1,), (1,)), ((), ())), preferred_...  41 us
    ppermute x56, starting transfers between devices, ring_scatter(): second = lax.ppermute(second, 'dp', back) + block(2 + step, 1)  41 us
  transfers between devices with their start and end apart: 136, of which 86 were waited for; matrix products, arithmetic and copies ran while one was open for 26% of the time, Pallas kernels for 4%

profile of v1, /device:TPU:0, one launch (start us, length us, event | category | flops | bytes accessed | tf_op | source)
XLA Modules:
  0.0 1079.8 jit_solution(9357004512478193292)
XLA Ops:
  3.6 14.9 %mod_forward.1 = f32[12,3,1536]{2,1,0:T(4,128)S(1)} custom-call(bf16[24,1536]{1,0:T(8,128)(2,1)S(1)} %copy-done.2, bf16[2,1536,288]{2,1,0:T(8,128)(2,1)S(1)} %copy.59.weight_ref, bf16[2,288]{1,0:T(2,128)(2,1)S(1)} %copy-done.5), custom_call_target="tpu_custom_call" | custom-call | tf_op jit(solution)/shard_map/mod_forward/pallas_call | solution.py:353
  59.2 19.0 %attn_forward.1 = (bf16[2,3,128,384]{3,2,1,0:T(8,128)(2,1)S(1)}, bf16[2,3,80,384]{3,2,1,0:T(8,128)(2,1)S(1)}) custom-call(f32[2,2,128]{2,1,0:T(2,128)S(1)} %pad_maximum_fusion.17.gain_ref, f32[2,3,128,1152]{3,2,1,0:T(8,128)} %bitcast.766, f32[2,3,80,1152]{3,2,1,0:T(8,128)S(1)} %bitcast.656), custom_call_target="tpu_custom_call" | custom-call | flops 797442048 | bytes 6709248 | tf_op jit(solution)/shard_map/attn_forward/pallas_call | solution.py:213
  84.8 32.5 %collective-permute-done.7 = f32[240,1536]{1,0:T(8,128)S(1)} collective-permute-done((f32[240,1536]{1,0:T(8,128)S(1)}, f32[240,1536]{1,0:T(8,128)S(1)}, u32[]{:S(2)}, u32[]{:S(2)}) %collective-permute-start.7) | collective-permute-done | bytes 1474592 | tf_op jit(solution)/shard_map/ppermute | solution.py:531
  127.4 46.2 %collective-permute-done.1 = f32[384,1536]{1,0:T(8,128)S(1)} collective-permute-done((f32[384,1536]{1,0:T(8,128)S(1)}, f32[384,1536]{1,0:T(8,128)S(1)}, u32[]{:S(2)}, u32[]{:S(2)}) %collective-permute-start.1) | collective-permute-done | bytes 2359328 | tf_op jit(solution)/shard_map/ppermute | solution.py:531
  262.6 10.0 multiply_convert_fusion
  279.2 8.7 collective-permute-done.10
  353.6 9.9 collective-permute-done.123
  558.7 10.1 collective-permute-done.74
  574.7 10.2 collective-permute-done.115
  590.9 10.2 collective-permute-done.88
  604.6 9.1 collective-permute-done.116
  620.8 9.1 collective-permute-done.89
  632.8 9.8 collective-permute-done.117
  657.5 9.7 collective-permute-done.118
  671.7 11.9 %collective-permute-done.112 = f32[96,1536]{1,0:T(8,128)S(1)} collective-permute-done((f32[96,1536]{1,0:T(8,128)S(1)}, f32[96,1536]{1,0:T(8,128)S(1)}, u32[]{:S(2)}, u32[]{:S(2)}) %collective-permute-start.112) | collective-permute-done | bytes 589856 | tf_op jit(solution)/shard_map/ppermute | solution.py:596
  686.0 10.3 collective-permute-done.84
  702.2 10.3 collective-permute-done.113
  715.5 9.6 collective-permute-done.85
  739.7 11.5 %collective-permute-done.121 = f32[96,1536]{1,0:T(8,128)S(1)} collective-permute-done((f32[96,1536]{1,0:T(8,128)}, f32[96,1536]{1,0:T(8,128)S(1)}, u32[]{:S(2)}, u32[]{:S(2)}) %collective-permute-start.121) | collective-permute-done | bytes 589856 | tf_op jit(solution)/shard_map/ppermute | solution.py:597
  768.3 22.0 %attn_backward.1 = (bf16[2,3,128,1152]{3,2,1,0:T(8,128)(2,1)}, bf16[2,3,80,1152]{3,2,1,0:T(8,128)(2,1)}, f32[3,2,1152]{2,1,0:T(2,128)}, f32[3,4,128]{2,1,0:T(4,128)}) custom-call(f32[2,2,128]{2,1,0:T(2,128)} %copy-done.4, f32[2,3,128,1152]{3,2,1,0:T(8,128)} %bitcast.767, f32[2,3,80,1152]{3,2,1,0:T(8,128)} %bitcast.657, bf16[2,3,128,384]{3,2,1,0:T(8,128)(2,1)} %bitcast.768, ...), custom_call_target="tpu_custom_call" | custom-call | flops 1993605120 | bytes 9584640 | tf_op jit(solution)/shard_map/attn_backward/pallas_call | solution.py:239
  838.0 8.2 collective-permute-done.55
  850.4 9.2 collective-permute-done.56
  995.8 32.8 %collective-permute-done.19 = f32[384,1536]{1,0:T(8,128)} collective-permute-done((f32[384,1536]{1,0:T(8,128)}, f32[384,1536]{1,0:T(8,128)}, u32[]{:S(2)}, u32[]{:S(2)}) %collective-permute-start.19) | collective-permute-done | bytes 2359328 | tf_op jit(solution)/shard_map/ppermute | solution.py:531
  1036.9 25.4 %mod_backward.1 = (f32[2,1536,288]{2,1,0:T(8,128)}, f32[2,288]{1,0:T(2,128)S(1)}, f32[3,1536]{1,0:T(4,128)S(1)}, f32[8,1,672]{2,1,0:T(1,128)S(1)}, f32[8,1,800]{2,1,0:T(1,128)S(1)}) custom-call(f32[12,3,1536]{2,1,0:T(4,128)S(1)} %constant_dynamic-update-slice_fusion.mod_ref, bf16[24,1536]{1,0:T(8,128)(2,1)S(1)} %copy-done.3, ...), custom_call_target="tpu_custom_call" | custom-call | tf_op jit(solution)/shard_map/mod_backward/pallas_call | solution.py:488
  (919 shorter events, 679.6 us)
Async XLA Ops:
  119.9 53.7 %collective-permute-start.1 = (f32[384,1536]{1,0:T(8,128)S(1)}, f32[384,1536]{1,0:T(8,128)S(1)}, u32[]{:S(2)}, u32[]{:S(2)}) collective-permute-start(f32[384,1536]{1,0:T(8,128)S(1)} %convolution_add_fusion.2), channel_id=1, source_target_pairs={{0,2},{1,3},{2,0},{3,1},{4,6},{5,7},{6,4},{7,5},{8,10},{9,11},{10,... | collective-permute-start | bytes 7077896 | tf_op jit(solution)/shard_map/ppermute | solution.py:531
  177.4 76.5 %collective-permute-start.2 = (f32[3,128,1536]{2,1,0:T(8,128)}, f32[3,128,1536]{2,1,0:T(8,128)}, u32[]{:S(2)}, u32[]{:S(2)}) collective-permute-start(f32[3,128,1536]{2,1,0:T(8,128)} %subtract_multiply_fusion.3), channel_id=1, source_target_pairs={{0,1},{1,0},{2,3},{3,2},{4,5},{5,4},{6,7},{7,6},{8,9},{9,8},{10,11... | collective-permute-start | bytes 7077896 | tf_op jit(solution)/shard_map/ppermute | solution.py:537
  181.5 65.9 %collective-permute-start.9 = (f32[240,1536]{1,0:T(8,128)}, f32[240,1536]{1,0:T(8,128)}, u32[]{:S(2)}, u32[]{:S(2)}) collective-permute-start(f32[240,1536]{1,0:T(8,128)} %fusion.15), channel_id=1, source_target_pairs={{0,1},{1,0},{2,3},{3,2},{4,5},{5,4},{6,7},{7,6},{8,9},{9,8},{10,11... | collective-permute-start | bytes 4423688 | tf_op jit(solution)/shard_map/ppermute | solution.py:528
  252.9 35.0 %collective-permute-start.10 = (f32[240,1536]{1,0:T(8,128)}, f32[240,1536]{1,0:T(8,128)}, u32[]{:S(2)}, u32[]{:S(2)}) collective-permute-start(f32[240,1536]{1,0:T(8,128)} %fusion.78), channel_id=1, source_target_pairs={{0,2},{1,3},{2,0},{3,1},{4,6},{5,7},{6,4},{7,5},{8,10},{9,11},{10,... | collective-permute-start | bytes 4423688 | tf_op jit(solution)/shard_map/ppermute | solution.py:531
  301.8 63.9 %collective-permute-start.15 = (f32[240,1536]{1,0:T(8,128)}, f32[240,1536]{1,0:T(8,128)}, u32[]{:S(2)}, u32[]{:S(2)}) collective-permute-start(f32[240,1536]{1,0:T(8,128)} %fusion.19), channel_id=1, source_target_pairs={{0,1},{1,0},{2,3},{3,2},{4,5},{5,4},{6,7},{7,6},{8,9},{9,8},{10,11... | collective-permute-start | bytes 4423688 | tf_op jit(solution)/shard_map/ppermute | solution.py:528
  350.8 41.5 %collective-permute-start.3 = (f32[384,1536]{1,0:T(8,128)S(1)}, f32[384,1536]{1,0:T(8,128)S(1)}, u32[]{:S(2)}, u32[]{:S(2)}) collective-permute-start(f32[384,1536]{1,0:T(8,128)S(1)} %copy-done.157), channel_id=1, source_target_pairs={{0,1},{1,0},{2,3},{3,2},{4,5},{5,4},{6,7},{7,6},{8,9},{9,8},{10,11... | collective-permute-start | bytes 7077896 | tf_op jit(solution)/shard_map/ppermute | solution.py:528
  376.1 42.5 %collective-permute-start.16 = (f32[240,1536]{1,0:T(8,128)S(1)}, f32[240,1536]{1,0:T(8,128)S(1)}, u32[]{:S(2)}, u32[]{:S(2)}) collective-permute-start(f32[240,1536]{1,0:T(8,128)S(1)} %fusion.75), channel_id=1, source_target_pairs={{0,2},{1,3},{2,0},{3,1},{4,6},{5,7},{6,4},{7,5},{8,10},{9,11},{10,... | collective-permute-start | bytes 4423688 | tf_op jit(solution)/shard_map/ppermute | solution.py:531
  401.3 80.3 %collective-permute-start.4 = (f32[384,1536]{1,0:T(8,128)}, f32[384,1536]{1,0:T(8,128)}, u32[]{:S(2)}, u32[]{:S(2)}) collective-permute-start(f32[384,1536]{1,0:T(8,128)} %fusion.60), channel_id=1, source_target_pairs={{0,2},{1,3},{2,0},{3,1},{4,6},{5,7},{6,4},{7,5},{8,10},{9,11},{10,... | collective-permute-start | bytes 7077896 | tf_op jit(solution)/shard_map/ppermute | solution.py:531
  464.5 72.0 %collective-permute-start.17 = (f32[3,80,1536]{2,1,0:T(8,128)}, f32[3,80,1536]{2,1,0:T(8,128)}, u32[]{:S(2)}, u32[]{:S(2)}) collective-permute-start(f32[3,80,1536]{2,1,0:T(8,128)} %get-tuple-element.96), channel_id=1, source_target_pairs={{0,1},{1,0},{2,3},{3,2},{4,5},{5,4},{6,7},{7,6},{8,9},{9,8},{10,11... | collective-permute-start | bytes 4423688 | tf_op jit(solution)/shard_map/ppermute | solution.py:537
  468.1 85.3 %collective-permute-start.11 = (f32[3,80,1536]{2,1,0:T(8,128)}, f32[3,80,1536]{2,1,0:T(8,128)}, u32[]{:S(2)}, u32[]{:S(2)}) collective-permute-start(f32[3,80,1536]{2,1,0:T(8,128)} %get-tuple-element.257), channel_id=1, source_target_pairs={{0,1},{1,0},{2,3},{3,2},{4,5},{5,4},{6,7},{7,6},{8,9},{9,8},{10,11... | collective-permute-start | bytes 4423688 | tf_op jit(solution)/shard_map/ppermute | solution.py:537
  501.2 142.6 %collective-permute-start.12 = (f32[384,1536]{1,0:T(8,128)}, f32[384,1536]{1,0:T(8,128)}, u32[]{:S(2)}, u32[]{:S(2)}) collective-permute-start(f32[384,1536]{1,0:T(8,128)} %fusion.31), channel_id=1, source_target_pairs={{0,1},{1,0},{2,3},{3,2},{4,5},{5,4},{6,7},{7,6},{8,9},{9,8},{10,11... | collective-permute-start | bytes 7077896 | tf_op jit(solution)/shard_map/ppermute | solution.py:528
  518.5 50.7 %collective-permute-start.80 = (f32[96,1536]{1,0:T(8,128)}, f32[96,1536]{1,0:T(8,128)}, u32[]{:S(2)}, u32[]{:S(2)}) collective-permute-start(f32[96,1536]{1,0:T(8,128)} %get-tuple-element.154), channel_id=1, source_target_pairs={{0,4},{4,12},{12,20},{20,28},{28,24},{24,16},{16,8},{8,0},{1,5},{5... | collective-permute-start | bytes 1769480 | tf_op jit(solution)/shard_map/ppermute | solution.py:596
  619.2 50.3 %collective-permute-start.70 = (f32[96,384]{1,0:T(8,128)S(1)}, f32[96,384]{1,0:T(8,128)S(1)}, u32[]{:S(2)}, u32[]{:S(2)}) collective-permute-start(f32[96,384]{1,0:T(8,128)S(1)} %get-tuple-element.237), channel_id=1, source_target_pairs={{0,4},{4,12},{12,20},{20,28},{28,24},{24,16},{16,8},{8,0},{1,5},{5... | collective-permute-start | bytes 442376 | tf_op jit(solution)/shard_map/ppermute | solution.py:596
  630.2 37.2 %collective-permute-start.83 = (f32[96,1536]{1,0:T(8,128)S(1)}, f32[96,1536]{1,0:T(8,128)S(1)}, u32[]{:S(2)}, u32[]{:S(2)}) collective-permute-start(f32[96,1536]{1,0:T(8,128)S(1)} %get-tuple-element.148), channel_id=1, source_target_pairs={{0,4},{4,12},{12,20},{20,28},{28,24},{24,16},{16,8},{8,0},{1,5},{5... | collective-permute-start | bytes 1769480 | tf_op jit(solution)/shard_map/ppermute | solution.py:596
  631.9 36.0 %collective-permute-start.90 = (f32[96,1536]{1,0:T(8,128)S(1)}, f32[96,1536]{1,0:T(8,128)S(1)}, u32[]{:S(2)}, u32[]{:S(2)}) collective-permute-start(f32[96,1536]{1,0:T(8,128)S(1)} %get-tuple-element.149), channel_id=1, source_target_pairs={{4,0},{12,4},{20,12},{28,20},{24,28},{16,24},{8,16},{0,8},{5,1},{1... | collective-permute-start | bytes 1769480 | tf_op jit(solution)/shard_map/ppermute | solution.py:597
  667.2 60.1 %collective-permute-start.13 = (f32[384,1536]{1,0:T(8,128)S(1)}, f32[384,1536]{1,0:T(8,128)S(1)}, u32[]{:S(2)}, u32[]{:S(2)}) collective-permute-start(f32[384,1536]{1,0:T(8,128)S(1)} %fusion.57), channel_id=1, source_target_pairs={{0,2},{1,3},{2,0},{3,1},{4,6},{5,7},{6,4},{7,5},{8,10},{9,11},{10,... | collective-permute-start | bytes 7077896 | tf_op jit(solution)/shard_map/ppermute | solution.py:531
  725.1 150.7 %collective-permute-start.72 = (f32[96,384]{1,0:T(8,128)}, f32[96,384]{1,0:T(8,128)}, u32[]{:S(2)}, u32[]{:S(2)}) collective-permute-start(f32[96,384]{1,0:T(8,128)} %get-tuple-element.233), channel_id=1, source_target_pairs={{0,4},{4,12},{12,20},{20,28},{28,24},{24,16},{16,8},{8,0},{1,5},{5... | collective-permute-start | bytes 442376 | tf_op jit(solution)/shard_map/ppermute | solution.py:596
  762.9 49.5 %collective-permute-start.5 = (f32[3,128,1536]{2,1,0:T(8,128)}, f32[3,128,1536]{2,1,0:T(8,128)}, u32[]{:S(2)}, u32[]{:S(2)}) collective-permute-start(f32[3,128,1536]{2,1,0:T(8,128)} %get-tuple-element.210), channel_id=1, source_target_pairs={{0,1},{1,0},{2,3},{3,2},{4,5},{5,4},{6,7},{7,6},{8,9},{9,8},{10,11... | collective-permute-start | bytes 7077896 | tf_op jit(solution)/shard_map/ppermute | solution.py:537
  797.2 37.5 %collective-permute-start.38 = (f32[96,1152]{1,0:T(8,128)}, f32[96,1152]{1,0:T(8,128)S(1)}, u32[]{:S(2)}, u32[]{:S(2)}) collective-permute-start(f32[96,1152]{1,0:T(8,128)} %get-tuple-element.202), channel_id=1, source_target_pairs={{0,4},{4,12},{12,20},{20,28},{28,24},{24,16},{16,8},{8,0},{1,5},{5... | collective-permute-start | bytes 1327112 | tf_op jit(solution)/shard_map/ppermute | solution.py:596
  798.2 38.1 %collective-permute-start.45 = (f32[96,1152]{1,0:T(8,128)}, f32[96,1152]{1,0:T(8,128)}, u32[]{:S(2)}, u32[]{:S(2)}) collective-permute-start(f32[96,1152]{1,0:T(8,128)} %get-tuple-element.203), channel_id=1, source_target_pairs={{4,0},{12,4},{20,12},{28,20},{24,28},{16,24},{8,16},{0,8},{5,1},{1... | collective-permute-start | bytes 1327112 | tf_op jit(solution)/shard_map/ppermute | solution.py:597
  873.5 96.4 %collective-permute-start.18 = (f32[384,1536]{1,0:T(8,128)}, f32[384,1536]{1,0:T(8,128)}, u32[]{:S(2)}, u32[]{:S(2)}) collective-permute-start(f32[384,1536]{1,0:T(8,128)} %fusion.133), channel_id=1, source_target_pairs={{0,1},{1,0},{2,3},{3,2},{4,5},{5,4},{6,7},{7,6},{8,9},{9,8},{10,11... | collective-permute-start | bytes 7077896 | tf_op jit(solution)/shard_map/ppermute | solution.py:528
  909.8 50.4 %collective-permute-start.22 = (f32[240,1536]{1,0:T(8,128)S(1)}, f32[240,1536]{1,0:T(8,128)S(1)}, u32[]{:S(2)}, u32[]{:S(2)}) collective-permute-start(f32[240,1536]{1,0:T(8,128)S(1)} %convolution_add_fusion.5), channel_id=1, source_target_pairs={{0,2},{1,3},{2,0},{3,1},{4,6},{5,7},{6,4},{7,5},{8,10},{9,11},{10,... | collective-permute-start | bytes 4423688 | tf_op jit(solution)/shard_map/ppermute | solution.py:531
  974.7 54.0 %collective-permute-start.19 = (f32[384,1536]{1,0:T(8,128)}, f32[384,1536]{1,0:T(8,128)}, u32[]{:S(2)}, u32[]{:S(2)}) collective-permute-start(f32[384,1536]{1,0:T(8,128)} %convolution_add_fusion.3), channel_id=1, source_target_pairs={{0,2},{1,3},{2,0},{3,1},{4,6},{5,7},{6,4},{7,5},{8,10},{9,11},{10,... | collective-permute-start | bytes 7077896 | tf_op jit(solution)/shard_map/ppermute | solution.py:531
  1036.6 35.6 %collective-permute-start.20 = (f32[3,128,1536]{2,1,0:T(8,128)}, f32[3,128,1536]{2,1,0:T(8,128)}, u32[]{:S(2)}, u32[]{:S(2)}) collective-permute-start(f32[3,128,1536]{2,1,0:T(8,128)} %multiply_add_fusion.2), channel_id=1, source_target_pairs={{0,1},{1,0},{2,3},{3,2},{4,5},{5,4},{6,7},{7,6},{8,9},{9,8},{10,11... | collective-permute-start | bytes 7077896 | tf_op jit(solution)/shard_map/ppermute | solution.py:537
  (307 other events, 4981.4 us)

commit v2 on v1

--- a/solution.py
+++ b/solution.py
@@ -103,16 +103,17 @@
     return weights * (1.0 / jnp.sum(weights, axis=-1, keepdims=True))
 
 
-def attn_forward_kernel(real, gain_ref, img_ref, txt_ref, out_img_ref, out_txt_ref):
-    img, txt = img_ref.shape[2], txt_ref.shape[2]
-    local = img_ref.shape[3] // 3
+def attn_forward_kernel(real, gain_ref, *refs):
+    raw_refs, (out_img_ref, out_txt_ref) = (refs[:3], refs[3:6]), refs[6:]
+    img, txt = out_img_ref.shape[2], out_txt_ref.shape[2]
+    local = out_img_ref.shape[3]
     pair = gain_ref.shape[2]
     q_gain, k_gain = gain_rows(gain_ref, 0, img, txt), gain_rows(gain_ref, 1, img, txt)
     bias = key_bias(img, txt, real)
     scale = (pair // 2) ** (-0.5)
     for start in range(0, local, pair):
         q_raw, k_raw, v_raw = (
-            rows_of(img_ref, txt_ref, slice(part * local + start, part * local + start + pair))
+            rows_of(raw_refs[0][part], raw_refs[1][part], slice(start, start + pair))
             for part in range(3)
         )
         q_low = head_norm(q_raw, q_gain)[0].astype(jnp.bfloat16) * jnp.bfloat16(scale)
@@ -128,11 +129,11 @@
         put_rows(out_img_ref, out_txt_ref, slice(start, start + pair), out)
 
 
-def attn_backward_kernel(
-    real, gain_ref, img_ref, txt_ref, d_img_ref, d_txt_ref, o_img_ref, o_txt_ref, bias_ref, dgain_ref
-):
-    img, txt = img_ref.shape[2], txt_ref.shape[2]
-    local = img_ref.shape[3] // 3
+def attn_backward_kernel(real, gain_ref, *refs):
+    raw_refs = (refs[:3], refs[3:6])
+    d_img_ref, d_txt_ref, o_img_ref, o_txt_ref, bias_ref, dgain_ref = refs[6:]
+    img, txt = d_img_ref.shape[2], d_txt_ref.shape[2]
+    local = d_img_ref.shape[3]
     pair = gain_ref.shape[2]
     head_dim = pair // 2
     q_gain, k_gain = gain_rows(gain_ref, 0, img, txt), gain_rows(gain_ref, 1, img, txt)
@@ -141,7 +142,7 @@
     gain_sums = [[None, None], [None, None]]
     for start in range(0, local, pair):
         q_raw, k_raw, v_raw = (
-            rows_of(img_ref, txt_ref, slice(part * local + start, part * local + start + pair))
+            rows_of(raw_refs[0][part], raw_refs[1][part], slice(start, start + pair))
             for part in range(3)
         )
         q_wide, q_factor = head_norm(q_raw, q_gain)
@@ -202,19 +203,15 @@
     return pl.BlockSpec(array.shape, lambda seq: (0,) * array.ndim)
 
 
-def attn_forward(gain_pair, packed_img, packed_txt, real):
-    seqs = packed_img.shape[1]
-    local = packed_img.shape[3] // 3
-    outs = [
-        jax.ShapeDtypeStruct(packed.shape[:3] + (local,), jnp.bfloat16)
-        for packed in (packed_img, packed_txt)
-    ]
-    rows = 2 * (packed_img.shape[2] + packed_txt.shape[2])
+def attn_forward(gain_pair, raw_img, raw_txt, real):
+    seqs, local = raw_img[0].shape[1], raw_img[0].shape[3]
+    outs = [jax.ShapeDtypeStruct(raw[0].shape, jnp.bfloat16) for raw in (raw_img, raw_txt)]
+    rows = 2 * (raw_img[0].shape[2] + raw_txt[0].shape[2])
     return pl.pallas_call(
         functools.partial(attn_forward_kernel, real),
         grid=(seqs,),
         out_shape=outs,
-        in_specs=[whole_of(gain_pair), block_of(packed_img), block_of(packed_txt)],
+        in_specs=[whole_of(gain_pair)] + [block_of(raw) for raw in raw_img + raw_txt],
         out_specs=[block_of(out) for out in outs],
         compiler_params=pltpu.CompilerParams(vmem_limit_bytes=48 << 20),
         cost_estimate=pl.CostEstimate(
@@ -223,25 +220,24 @@
             transcendentals=seqs * rows * rows * (local // 64),
         ),
         name="attn_forward",
-    )(gain_pair, packed_img, packed_txt)
-
-
-def attn_backward(gain_pair, packed_img, packed_txt, grad_img, grad_txt, real):
-    seqs = packed_img.shape[1]
-    local = packed_img.shape[3] // 3
+    )(gain_pair, *raw_img, *raw_txt)
+
+
+def attn_backward(gain_pair, raw_img, raw_txt, grad_img, grad_txt, real):
+    seqs, local = raw_img[0].shape[1], raw_img[0].shape[3]
     outs = [
-        jax.ShapeDtypeStruct(packed_img.shape, jnp.bfloat16),
-        jax.ShapeDtypeStruct(packed_txt.shape, jnp.bfloat16),
+        jax.ShapeDtypeStruct(raw_img[0].shape[:3] + (3 * local,), jnp.bfloat16),
+        jax.ShapeDtypeStruct(raw_txt[0].shape[:3] + (3 * local,), jnp.bfloat16),
         jax.ShapeDtypeStruct((seqs, 2, 3 * local), jnp.float32),
         jax.ShapeDtypeStruct((seqs, 4, gain_pair.shape[2]), jnp.float32),
     ]
-    rows = 2 * (packed_img.shape[2] + packed_txt.shape[2])
+    rows = 2 * (raw_img[0].shape[2] + raw_txt[0].shape[2])
     return pl.pallas_call(
         functools.partial(attn_backward_kernel, real),
         grid=(seqs,),
         out_shape=outs,
         in_specs=[whole_of(gain_pair)]
-        + [block_of(each) for each in (packed_img, packed_txt, grad_img, grad_txt)],
+        + [block_of(each) for each in raw_img + raw_txt + [grad_img, grad_txt]],
         out_specs=[
             block_of(outs[0]),
             block_of(outs[1]),
@@ -255,7 +251,7 @@
             transcendentals=seqs * rows * rows * (local // 64),
         ),
         name="attn_backward",
-    )(gain_pair, packed_img, packed_txt, grad_img, grad_txt)
+    )(gain_pair, *raw_img, *raw_txt, grad_img, grad_txt)
 
 
 def xor_index(index, distance):
@@ -305,7 +301,7 @@
     seqs, feat = out_ref.shape[1], out_ref.shape[2]
     silu_cond = silu_of(cond_ref)
     for stream in range(2):
-        values = dot_plain(silu_cond, weight_ref[stream]) + bias_ref[stream : stream + 1].astype(
+        values = dot_right_t(silu_cond, weight_ref[stream]) + bias_ref[stream : stream + 1].astype(
             jnp.float32
         )
         for index in range(data_size):
@@ -348,7 +344,7 @@
 
 
 def mod_forward(conditioning, ada_weight, ada_bias, seqs, feat, data_size, tensor_size):
-    cols = ada_weight.shape[2]
+    cols = ada_weight.shape[1]
     vmem = pl.BlockSpec(memory_space=pltpu.VMEM)
     return pl.pallas_call(
         functools.partial(mod_forward_kernel, data_size, tensor_size),
@@ -373,29 +369,20 @@
     mod_ref,
     cond_ref,
     weight_ref,
-    group_ref,
-    all_ref,
-    weight_out,
-    bias_out,
-    silu_out,
-    group_out,
-    all_out,
-    blocks,
-    core_in,
-    outgoing,
-    cols_in,
-    group_in,
-    all_in,
-    group_own,
-    all_own,
-    silu_blocks,
-    silu_in,
-    silu_send,
-    silu_recv,
-    all_send,
-    all_recv,
-    sems,
+    *refs,
 ):
+    refs = list(refs)
+
+    def take(number):
+        taken = refs[:number]
+        del refs[:number]
+        return taken
+
+    group_refs, all_refs = take(2), take(3)
+    weight_out, bias_out, silu_out = take(3)
+    group_outs, all_outs = take(2), take(3)
+    blocks, core_in, outgoing, cols_in, lines, lines_in, lines_own, lines_all = take(8)
+    silu_blocks, silu_in, silu_send, silu_recv, all_send, all_recv, sems = take(7)
     row, col, around, across = peers_of(data_size, tensor_size)
     seqs, feat = silu_out.shape
     cols = bias_out.shape[1]
@@ -408,6 +395,21 @@
                     :, start : start + cols
                 ]
     silu_cond = silu_of(cond_ref)
+    half = lines.shape[1] // 2
+    width = lines.shape[2]
+
+    def line_up(sources):
+        padded = [
+            jnp.pad(ref[...], ((0, 0), (0, feat - ref.shape[1]))) for ref in sources
+        ]
+        short = half - sum(ref.shape[0] for ref in sources)
+        if short:
+            padded.append(jnp.zeros((short, feat), jnp.float32))
+        return jnp.concatenate(padded, axis=0)
+
+    every_line = jnp.concatenate([line_up(group_refs), line_up(all_refs)], axis=0)
+    for index in range(data_size):
+        lines[index] = every_line[:, index * width : (index + 1) * width]
     greet(around + across)
 
     used = 0
@@ -418,19 +420,17 @@
         outgoing[first] = blocks[col, first] + core_in[first]
 
     cols_in[row] = outgoing[row]
-    group_in[row] = group_ref[row]
-    all_in[row] = all_ref[row]
+    lines_in[row] = lines[row]
     copies = []
     for partner in around:
-        for source, target in ((group_ref, group_in), (all_ref, all_in), (outgoing, cols_in)):
+        for source, target in ((lines, lines_in), (outgoing, cols_in)):
             copies.append(
                 remote(source.at[partner[0]], target.at[row], sems, used, partner)
             )
             used += 1
     for copy in copies:
         copy.wait()
-    group_own[...] = functools.reduce(jnp.add, [group_in[index] for index in range(data_size)])
-    all_own[...] = functools.reduce(jnp.add, [all_in[index] for index in range(data_size)])
+    lines_own[...] = functools.reduce(jnp.add, [lines_in[index] for index in range(data_size)])
     low = []
     for stream in range(2):
         wide = jnp.concatenate(
@@ -439,27 +439,36 @@
         )
         bias_out[stream : stream + 1] = jnp.sum(wide, axis=0, keepdims=True)
         low.append(wide.astype(jnp.bfloat16))
-    silu_grad = dot_right_t(low[0], weight_ref[0]) + dot_right_t(low[1], weight_ref[1])
+    silu_grad = dot_plain(low[0], weight_ref[0]) + dot_plain(low[1], weight_ref[1])
     for index in range(data_size):
         silu_blocks[index] = silu_grad[index * seqs : (index + 1) * seqs]
     for stream in range(2):
-        weight_out[stream] = dot_left_t(silu_cond, low[stream])
+        weight_out[stream] = dot_left_t(low[stream], silu_cond)
 
     silu_in[row] = silu_blocks[row]
-    group_out[row] = group_own[...]
-    all_send[0, row] = all_own[...]
+    lines_all[row] = lines_own[...]
     copies = []
     for partner in around:
         for source, target in (
             (silu_blocks.at[partner[0]], silu_in.at[row]),
-            (group_own, group_out.at[row]),
-            (all_own, all_send.at[0, row]),
+            (lines_own, lines_all.at[row]),
         ):
             copies.append(remote(source, target, sems, used, partner))
             used += 1
     for copy in copies:
         copy.wait()
     silu_send[0] = functools.reduce(jnp.add, [silu_in[index] for index in range(data_size)])
+    every_line = jnp.concatenate([lines_all[index] for index in range(data_size)], axis=1)
+    all_send[0] = every_line[half:]
+
+    def hand_out(values, targets):
+        start = 0
+        for target in targets:
+            count, size = target.shape
+            target[...] = values[start : start + count, :size]
+            start += count
+
+    hand_out(every_line[:half], group_outs)
 
     for level, partner in enumerate(across):
         copies = [
@@ -472,15 +481,15 @@
         silu_send[level + 1] = silu_send[level] + silu_recv[level]
         all_send[level + 1] = all_send[level] + all_recv[level]
     silu_out[...] = silu_send[len(across)]
-    all_out[...] = all_send[len(across)]
+    hand_out(all_send[len(across)], all_outs)
 
 
 def mod_backward(mod_grads, conditioning, ada_weight, group, every, data_size, tensor_size):
     _, seqs, feat = mod_grads.shape
-    cols = ada_weight.shape[2]
+    cols = ada_weight.shape[1]
     levels = tensor_size.bit_length() - 1
-    group_size, every_size = group.shape[-1], every.shape[-1]
     vmem = pl.BlockSpec(memory_space=pltpu.VMEM)
+    lines, width = 16, feat // data_size
 
     def wide(*shape):
         return pltpu.VMEM(shape, jnp.float32)
@@ -491,44 +500,48 @@
             jax.ShapeDtypeStruct(ada_weight.shape, jnp.float32),
             jax.ShapeDtypeStruct((2, cols), jnp.float32),
             jax.ShapeDtypeStruct((seqs, feat), jnp.float32),
-            jax.ShapeDtypeStruct(group.shape, jnp.float32),
-            jax.ShapeDtypeStruct(every.shape, jnp.float32),
-        ],
-        in_specs=[vmem] * 5,
-        out_specs=[vmem] * 5,
+        ]
+        + [jax.ShapeDtypeStruct(each.shape, jnp.float32) for each in group + every],
+        in_specs=[vmem] * (3 + len(group) + len(every)),
+        out_specs=[vmem] * (3 + len(group) + len(every)),
         scratch_shapes=[
             wide(tensor_size, data_size, 2 * seqs, cols),
             wide(data_size, 2 * seqs, cols),
             wide(data_size, 2 * seqs, cols),
             wide(data_size, 2 * seqs, cols),
-            wide(*group.shape),
-            wide(*every.shape),
-            wide(1, group_size),
-            wide(1, every_size),
+            wide(data_size, lines, width),
+            wide(data_size, lines, width),
+            wide(lines, width),
+            wide(data_size, lines, width),
             wide(data_size, seqs, feat),
             wide(data_size, seqs, feat),
             wide(levels + 1, seqs, feat),
             wide(levels, seqs, feat),
-            wide(levels + 1, *every.shape),
-            wide(levels, *every.shape),
-            pltpu.SemaphoreType.DMA((2, 1 + 6 * (data_size - 1) + 2 * levels)),
+            wide(levels + 1, lines // 2, feat),
+            wide(levels, lines // 2, feat),
+            pltpu.SemaphoreType.DMA((2, 1 + 4 * (data_size - 1) + 2 * levels)),
         ],
         compiler_params=pltpu.CompilerParams(
             collective_id=1, has_side_effects=True, vmem_limit_bytes=48 << 20
         ),
         name="mod_backward",
-    )(mod_grads, conditioning, ada_weight, group, every)
+    )(mod_grads, conditioning, ada_weight, *group, *every)
 
 
 def swap_pairs(size, distance):
     return [(index, index ^ distance) for index in range(size)]
 
 
-def tensor_sum(own_part, other_part, tensor_size):
-    total = own_part + lax.ppermute(other_part, "tensor", swap_pairs(tensor_size, 1))
+def core_sum(own_part, other_part, tensor_size):
+    return own_part + lax.ppermute(other_part, "tensor", swap_pairs(tensor_size, 1))
+
+
+def chip_sum(total, swapped, tensor_size):
     distance = 2
     while distance < tensor_size:
-        total = total + lax.ppermute(total, "tensor", swap_pairs(tensor_size, distance))
+        if swapped is None or distance > 2:
+            swapped = lax.ppermute(total, "tensor", swap_pairs(tensor_size, distance))
+        total = total + swapped
         distance *= 2
     return total
 
@@ -577,25 +590,125 @@
     return path if extend() else fallback
 
 
-def ring_scatter(grad, order):
+def entry_of(table, index):
+    value = jnp.int32(table[0])
+    for place in range(1, len(table)):
+        value = jnp.where(index == place, jnp.int32(table[place]), value)
+    return value
+
+
+def grad_ring_kernel(order, count, swaps, *refs):
+    refs = list(refs)
+
+    def take(number):
+        taken = refs[:number]
+        del refs[:number]
+        return taken
+
+    lefts, rights, gives = take(count), take(count), take(swaps)
+    outs, gets = take(count), take(swaps)
+    slots, terms, turned = take(count), take(count), take(count)
+    (sems,) = take(1)
+    swap_sems = refs[0] if swaps else None
     size = len(order)
-    ahead = [(order[index], order[(index + 1) % size]) for index in range(size)]
-    back = [(second, first) for first, second in ahead]
-    place = jnp.array([order.index(index) for index in range(size)], jnp.int32)[lax.axis_index("dp")]
-    blocks = jnp.array(order, jnp.int32)
-    halves = grad.reshape(size, 2, grad.shape[0] // (2 * size), grad.shape[1])
-
-    def block(offset, way):
-        index = blocks[(place + offset) % size]
-        return lax.dynamic_slice(
-            halves, (index, way, 0, 0), (1, 1) + halves.shape[2:]
-        ).reshape(halves.shape[2:])
-
-    first, second = block(size - 1, 0), block(1, 1)
-    for step in range(size - 1):
-        first = lax.ppermute(first, "dp", ahead) + block(2 * size - 2 - step, 0)
-        second = lax.ppermute(second, "dp", back) + block(2 + step, 1)
-    return jnp.concatenate([first, second], axis=0)
+    row, col = lax.axis_index("dp"), lax.axis_index("tensor")
+    place = entry_of([order.index(index) for index in range(size)], row)
+    after = entry_of(order, lax.rem(place + 1, size))
+    before = entry_of(order, lax.rem(place + size - 1, size))
+    targets = ((after, col), (before, col))
+    half = slots[0].shape[2]
+    facing = (row, xor_index(col, 2))
+
+    greet(targets + ((facing,) if swaps else ()))
+    swapped = [
+        remote(gives[index], gets[index], swap_sems, index, facing) for index in range(swaps)
+    ]
+    for left, flipped in zip(lefts, turned):
+        flipped[...] = left[...].T
+
+    def work_out(which, way, index):
+        start = pl.multiple_of((2 * index + way) * half, 8)
+        terms[which][way] = dot_plain(turned[which][pl.ds(start, half), :], rights[which][...])
+
+    def copy_of(which, way, step, source, target):
+        return pltpu.make_async_remote_copy(
+            src_ref=source,
+            dst_ref=slots[which].at[way, target],
+            send_sem=sems.at[0, which, way, step],
+            recv_sem=sems.at[1, which, way, step],
+            device_id=targets[way],
+            device_id_type=pl.DeviceIdType.MESH,
+        )
+
+    chains = [(which, way) for which in range(count) for way in range(2)]
+    for which, way in chains:
+        work_out(which, way, (before, after)[way])
+        slots[which][way, size - 1] = terms[which][way]
+        copy_of(which, way, 0, slots[which].at[way, size - 1], 0).start()
+
+    def arrive(which, way, step):
+        copy_of(which, way, step, slots[which].at[way, step], step).wait_recv()
+
+    def round_of(step, carry):
+        ahead = entry_of(order, lax.rem(place + 2 * size - 2 - step, size))
+        back = entry_of(order, lax.rem(place + 2 + step, size))
+        for which, way in chains:
+            work_out(which, way, (ahead, back)[way])
+        for which, way in chains:
+            arrive(which, way, step)
+            slots[which][way, step] = slots[which][way, step] + terms[which][way]
+            copy_of(which, way, step + 1, slots[which].at[way, step], step + 1).start()
+        return carry
+
+    lax.fori_loop(0, size - 2, round_of, 0)
+    for which, way in chains:
+        work_out(which, way, row)
+    for which, way in chains:
+        arrive(which, way, size - 2)
+        total = slots[which][way, size - 2] + terms[which][way]
+        parts, _, width = outs[which].shape
+        for part in range(parts):
+            outs[which][part, way * half : (way + 1) * half] = total[
+                :, part * width : (part + 1) * width
+            ]
+
+    def sent(step, carry):
+        for which, way in chains:
+            copy_of(which, way, step, slots[which].at[way, size - 1], step).wait_send()
+        return carry
+
+    lax.fori_loop(0, size - 1, sent, 0)
+    for copy in swapped:
+        copy.wait()
+
+
+def grad_ring(pairs, gives, order, collective_id, name):
+    size, count, swaps = len(order), len(pairs), len(gives)
+    vmem = pl.BlockSpec(memory_space=pltpu.VMEM)
+    anywhere = pl.BlockSpec(memory_space=pl.ANY)
+    halves = [(left.shape[1] // (2 * size), right.shape[1]) for left, right, _ in pairs]
+    moved = sum(4 * 2 * (size - 1) * rows * cols for rows, cols in halves)
+    results = pl.pallas_call(
+        functools.partial(grad_ring_kernel, order, count, swaps),
+        out_shape=[
+            jax.ShapeDtypeStruct((parts, 2 * rows, cols // parts), jnp.float32)
+            for (rows, cols), (_, _, parts) in zip(halves, pairs)
+        ]
+        + [jax.ShapeDtypeStruct(give.shape, give.dtype) for give in gives],
+        in_specs=[vmem] * (2 * count) + [anywhere] * swaps,
+        out_specs=[vmem] * count + [anywhere] * swaps,
+        scratch_shapes=[pltpu.VMEM((2, size) + half, jnp.float32) for half in halves]
+        + [pltpu.VMEM((2,) + half, jnp.float32) for half in halves]
+        + [pltpu.VMEM(left.shape[::-1], left.dtype) for left, _, _ in pairs]
+        + [pltpu.SemaphoreType.DMA((2, count, 2, size - 1))]
+        + [pltpu.SemaphoreType.DMA((2, swaps))] * bool(swaps),
+        compiler_params=pltpu.CompilerParams(
+            collective_id=collective_id, has_side_effects=True, vmem_limit_bytes=58 << 20
+        ),
+        cost_estimate=pl.CostEstimate(flops=moved * 10000, bytes_accessed=moved, transcendentals=0),
+        name=name,
+    )(*[left for left, _, _ in pairs], *[right for _, right, _ in pairs], *gives)
+    return results[:count], results[count:]
 
 
 def on_device(
@@ -638,6 +751,7 @@
         lower, upper = jnp.where(first, own, other), jnp.where(first, other, own)
         return jnp.concatenate([lower[:, :real], upper[:, :real]], axis=1)
 
+    ada_weight = ada_weight.transpose(0, 2, 1)
     modulate = mod_forward(
         conditioning, ada_weight, ada_bias, seqs, feat, data_size, tensor_size
     )
@@ -650,31 +764,23 @@
     shapes = [array.shape for array in inputs]
     gain_pair = jnp.concatenate([norm_gain, norm_gain], axis=2)
 
-    hidden1, packed, stats1 = [], [], []
-    weights_in = [qkv_weight[stream].reshape(feat, -1) for stream in range(2)]
+    hidden1, raw, stats1 = [], [], []
     for stream in range(2):
         normed, inverse = layer_norm(inputs[stream].astype(jnp.float32))
         hidden = (normed * (1.0 + piece[stream][1]) + piece[stream][0]).astype(jnp.bfloat16)
         hidden = hidden.reshape(-1, feat)
-        flat = dot_plain(hidden, weights_in[stream]) + qkv_bias[stream].reshape(-1).astype(
-            jnp.float32
-        )
+        flat = [
+            dot_plain(hidden, qkv_weight[stream, :, part]) + qkv_bias[stream, part].astype(jnp.float32)
+            for part in range(3)
+        ]
         hidden1.append(hidden)
-        packed.append(flat.reshape(shapes[stream][:3] + (-1,)))
+        raw.append([each.reshape(shapes[stream][:3] + (-1,)) for each in flat])
         stats1.append((normed[0], inverse[0]))
-    attn = attn_forward(gain_pair, packed[0], packed[1], reals[1])
+    attn = attn_forward(gain_pair, raw[0], raw[1], reals[1])
     local = attn[0].shape[3]
 
-    down_rings, up_rings = [None, None], [None, None]
-    state = [None, None]
-    hidden_sums, mlp_sums = [None, None], [None, None]
-    up_bias_sums = [None, None]
-    for stream in (1, 0):
-        rows = attn[stream].reshape(2, -1, local)
-        other_part = dot_plain(rows[1], proj_weight[stream])
-        own_part = dot_plain(rows[0], proj_weight[stream])
-        total = tensor_sum(own_part, other_part, tensor_size).reshape(shapes[stream][1:])
-        branch = total + proj_bias[stream]
+    def mlp_stage(stream, total):
+        branch = total.reshape(shapes[stream][1:]) + proj_bias[stream]
         residual = inputs[stream][0].astype(jnp.float32) + piece[stream][2] * branch
         normed, inverse = layer_norm(residual)
         hidden = share(normed, tensor_size) * (1.0 + piece[stream][4]) + piece[stream][3]
@@ -686,28 +792,51 @@
         grad_mlp_low = grad_mlp.astype(jnp.bfloat16).reshape(-1, feat)
         grad_up = dot_right_t(grad_mlp_low, down_weight[stream]) * slope
         grad_up_low = grad_up.astype(jnp.bfloat16)
-        up_bias_sums[stream] = jnp.sum(grad_up, axis=0)
         half = grad_up_low.shape[0] // 2
-        down_rings[stream] = ring_scatter(dot_left_t(grad_mlp_low, active), order)
-        up_rings[stream] = ring_scatter(dot_left_t(hidden, grad_up_low), order)
-        other_part = dot_right_t(grad_up_low[half:], up_weight[stream])
-        own_part = dot_right_t(grad_up_low[:half], up_weight[stream])
-        hidden_sums[stream] = tensor_sum(own_part, other_part, tensor_size)
-        other_part = dot_plain(active[half:], down_weight[stream])
-        own_part = dot_plain(active[:half], down_weight[stream])
-        mlp_sums[stream] = tensor_sum(own_part, other_part, tensor_size)
-        state[stream] = (branch, normed, inverse, jnp.sum(grad_mlp[0], axis=(0, 1)))
-
-    grad_attn, proj_rings, proj_sums, resid_grads, mod_grads = (
-        [None, None],
-        [None, None],
-        [None, None],
-        [None, None],
-        [None, None],
-    )
+        hidden_sum = core_sum(
+            dot_right_t(grad_up_low[:half], up_weight[stream]),
+            dot_right_t(grad_up_low[half:], up_weight[stream]),
+            tensor_size,
+        )
+        mlp_sum = core_sum(
+            dot_plain(active[:half], down_weight[stream]),
+            dot_plain(active[half:], down_weight[stream]),
+            tensor_size,
+        )
+        return {
+            "branch": branch,
+            "normed": normed,
+            "inverse": inverse,
+            "pairs": [(grad_mlp_low, active, 1), (hidden, grad_up_low, 1)],
+            "hidden_sum": hidden_sum,
+            "mlp_sum": mlp_sum,
+            "up_bias": jnp.sum(grad_up, axis=0),
+            "down_bias": jnp.sum(grad_mlp[0], axis=(0, 1)),
+        }
+
+    branch_sums = [None, None]
+    for stream in (1, 0):
+        rows = attn[stream].reshape(2, -1, local)
+        branch_sums[stream] = core_sum(
+            dot_plain(rows[0], proj_weight[stream]),
+            dot_plain(rows[1], proj_weight[stream]),
+            tensor_size,
+        )
+    state, mlp_rings = [None, None], [None, None]
+    state[1] = mlp_stage(1, chip_sum(branch_sums[1], None, tensor_size))
+    mlp_rings[1], (swapped,) = grad_ring(
+        state[1]["pairs"], [branch_sums[0]], order, 2, "ring_mlp_txt"
+    )
+    state[0] = mlp_stage(0, chip_sum(branch_sums[0], swapped, tensor_size))
+    gives = [state[stream][key] for key in ("hidden_sum", "mlp_sum") for stream in (1, 0)]
+    mlp_rings[0], swapped = grad_ring(state[0]["pairs"], gives, order, 3, "ring_mlp_img")
+    gives = [chip_sum(give, get, tensor_size) for give, get in zip(gives, swapped)]
+    hidden_sums, mlp_sums = gives[1::-1], gives[:1:-1]
+
+    grad_attn, proj_pairs, proj_sums, resid_grads, mod_grads = ([None, None] for _ in range(5))
     outputs = [None, None]
     for stream in (1, 0):
-        branch, normed, inverse, _ = state[stream]
+        branch, normed, inverse = (state[stream][key] for key in ("branch", "normed", "inverse"))
         grad_out = cotangents[stream][0].astype(jnp.float32)
         grad_hidden = hidden_sums[stream].reshape(normed.shape)
         through = norm_back(grad_hidden * (1.0 + piece[stream][4]), normed, inverse)
@@ -719,9 +848,7 @@
             .astype(jnp.bfloat16)
             .reshape(attn[stream].shape)
         )
-        proj_rings[stream] = ring_scatter(
-            dot_left_t(branch_low, attn[stream].reshape(-1, local)), order
-        )
+        proj_pairs[stream] = (branch_low, attn[stream].reshape(-1, local), 1)
         proj_sums[stream] = jnp.sum(grad_resid * piece[stream][2], axis=(0, 1))
         resid_grads[stream] = through
         mod_grads[stream] = [
@@ -732,23 +859,35 @@
             jnp.sum(grad_hidden * normed, axis=1),
             None,
         ]
-    grad_packed = attn_backward(gain_pair, packed[0], packed[1], grad_attn[0], grad_attn[1], reals[1])
+    grad_packed = attn_backward(gain_pair, raw[0], raw[1], grad_attn[0], grad_attn[1], reals[1])
     qkv_bias_sums = jnp.sum(grad_packed[2], axis=0)
     gain_sums = jnp.sum(grad_packed[3], axis=0)
     head_dim = norm_gain.shape[2]
     gain_sums = gain_sums[:, :head_dim] + gain_sums[:, head_dim:]
-    qkv_rings, first_sums = [None, None], [None, None]
+    qkv_pairs, first_sums = [None, None], [None, None]
     for stream in (1, 0):
         packed_low = grad_packed[stream].reshape(-1, 3 * local)
         half = packed_low.shape[0] // 2
-        other_part = dot_right_t(packed_low[half:], weights_in[stream])
-        own_part = dot_right_t(packed_low[:half], weights_in[stream])
-        first_sums[stream] = tensor_sum(own_part, other_part, tensor_size)
-        qkv_rings[stream] = ring_scatter(dot_left_t(hidden1[stream], packed_low), order)
+
+        def through_weights(rows):
+            return sum(
+                dot_right_t(
+                    packed_low[rows, part * local : (part + 1) * local], qkv_weight[stream, :, part]
+                )
+                for part in range(3)
+            )
+
+        first_sums[stream] = core_sum(
+            through_weights(slice(None, half)), through_weights(slice(half, None)), tensor_size
+        )
+        qkv_pairs[stream] = (hidden1[stream], packed_low, 3)
+    rings, swapped = grad_ring(qkv_pairs + proj_pairs, first_sums, order, 4, "ring_attn")
+    qkv_rings, proj_rings = rings[:2], rings[2:]
+    first_sums = [chip_sum(give, get, tensor_size) for give, get in zip(first_sums, swapped)]
 
     grad_inputs = [None, None]
     for stream in (1, 0):
-        branch = state[stream][0]
+        branch = state[stream]["branch"]
         grad_out = cotangents[stream][0].astype(jnp.float32)
         mlp_out = mlp_sums[stream].reshape(branch.shape) + down_bias[stream]
         added = piece[stream][2] * branch + piece[stream][5] * mlp_out
@@ -768,55 +907,43 @@
         mod_grads[stream][1] = jnp.sum(grad_hidden * normed, axis=1)
 
     row_share = 2.0 / tensor_size
-    parts = (
-        (qkv_bias_sums, jnp.stack(up_bias_sums)),
-        (
-            gain_sums,
-            jnp.stack(proj_sums) * row_share,
-            jnp.stack([state[0][3], state[1][3]]) * row_share,
-        ),
-    )
-    vectors = [
-        jnp.concatenate([each.reshape(-1) for each in group]).reshape(data_size, 1, -1)
-        for group in parts
-    ]
-    grad_ada_weight, grad_ada_bias, silu_rows, *vectors = mod_backward(
+    sums = mod_backward(
         jnp.stack(mod_grads[0] + mod_grads[1]),
         conditioning,
         ada_weight,
-        vectors[0],
-        vectors[1],
+        [qkv_bias_sums, jnp.stack([state[0]["up_bias"], state[1]["up_bias"]])],
+        [
+            gain_sums,
+            jnp.stack(proj_sums) * row_share,
+            jnp.stack([state[0]["down_bias"], state[1]["down_bias"]]) * row_share,
+        ],
         data_size,
         tensor_size,
     )
-    sums = []
-    for group, vector in zip(parts, vectors):
-        flat, start = vector.reshape(-1), 0
-        for each in group:
-            sums.append(flat[start : start + each.size].reshape(each.shape))
-            start += each.size
-    qkv_bias_sums, up_bias_sums, gain_sums, proj_sums, down_sums = sums
+    grad_ada_weight, grad_ada_bias, silu_rows, qkv_bias_sums, up_bias_sums = sums[:5]
+    gain_sums, proj_sums, down_sums = sums[5:]
     own_cond = lax.dynamic_slice_in_dim(
         conditioning, lax.axis_index("dp") * seqs, seqs, axis=0
     ).astype(jnp.float32)
     own_sig = jax.nn.sigmoid(own_cond)
     grad_conditioning = silu_rows * own_sig * (1.0 + own_cond * (1.0 - own_sig))
+    down_rings, up_rings = ([mlp_rings[0][index], mlp_rings[1][index]] for index in range(2))
     return (
         outputs[0],
         outputs[1],
         grad_inputs[0],
         grad_inputs[1],
         grad_conditioning,
-        grad_ada_weight,
+        grad_ada_weight.transpose(0, 2, 1),
         grad_ada_bias,
-        jnp.stack([ring.reshape(ring.shape[0], 3, -1) for ring in qkv_rings]),
+        jnp.stack(qkv_rings).transpose(0, 2, 1, 3),
         qkv_bias_sums.reshape(2, 3, -1),
         gain_sums.reshape(norm_gain.shape),
-        jnp.stack([ring.T for ring in proj_rings]),
+        jnp.concatenate(proj_rings).transpose(0, 2, 1),
         proj_sums,
-        jnp.stack(up_rings),
+        jnp.concatenate(up_rings),
         up_bias_sums,
-        jnp.stack([ring.T for ring in down_rings]),
+        jnp.concatenate(down_rings).transpose(0, 2, 1),
         down_sums,
     )
 

time: 1090 us -> 902 us (0.83)
  Pallas kernels: 81.3 us -> 637 us
  waiting for transfers between devices: 465 us -> 33.6 us
  starting transfers between devices: 122 us -> 4.16 us
  local copies, waits for them, and re-layouts: 103 us -> 31 us
  other arithmetic: 150 us -> 94.7 us
  between operations: 39.6 us -> 3.14 us
  matrix products: 118 us -> 92.4 us
    pallas_call x0 -> x3, Pallas kernels: none -> 565 us  [grad_ring(): pl.pallas_call(functools.partial(grad_ring_kernel, order, count, swaps),...]
    ppermute x128 -> x9, waiting for transfers between devices: 465 us -> 33.6 us  [the longest x1 30.6 us: chip_sum(): swapped = lax.ppermute(total, 'tensor', swap_pairs(tensor_size, distance))]
    ppermute x128 -> x9, starting transfers between devices: 122 us -> 2.94 us  [the longest x8 1.92 us: core_sum(): lax.ppermute(other_part, 'tensor', swap_pairs(tensor_size, 1))]
    dot_general x8 -> x0, matrix products: 32.8 us -> none  [dot_left_t(): lax.dot_general(first_op, second_op, (((0,), (0,)), ((), ())), preferred_...]
    add x58 -> x5, other arithmetic: 34.7 us -> 4.87 us  [the longest x4 4.25 us: chip_sum(): total = total + swapped]
    dot_general x8 -> x0, local copies, waits for them, and re-layouts: 27.7 us -> none  [dot_left_t(): lax.dot_general(first_op, second_op, (((0,), (0,)), ((), ())), preferred_...]
    unnamed x408 -> x378, local copies, waits for them, and re-layouts: 42.9 us -> 23.2 us
    dot_general x12 -> x20, matrix products: 41 us -> 51.3 us  [dot_right_t(): lax.dot_general(first_op, second_op, (((1,), (1,)), ((), ())), preferred_...]
  transfers between devices with their start and end apart: 136 -> 17, of which waited for: 86 -> 2; matrix products, arithmetic and copies ran while one was open for 26% -> 13% of each run, Pallas kernels for 4% -> 5%
where the time goes in v2:
time: 902 us; the launch traced here: 896 us
  Pallas kernels  637 us (71%)
  other arithmetic  94.7 us (10%)
  matrix products  92.4 us (10%)
  waiting for transfers between devices  33.6 us (4%)
  local copies, waits for them, and re-layouts  31 us (3%)
    pallas_call x3, Pallas kernels, grad_ring(): pl.pallas_call(functools.partial(grad_ring_kernel, order, count, swaps),...  565 us
    dot_general x20, matrix products, dot_right_t(): lax.dot_general(first_op, second_op, (((1,), (1,)), ((), ())), preferred_...  51.3 us
    dot_general x16, matrix products, dot_plain(): return jnp.dot(first_op, second_op, preferred_element_type=jnp.float32)  41.1 us
    ppermute x1, waiting for transfers between devices, chip_sum(): swapped = lax.ppermute(total, 'tensor', swap_pairs(tensor_size, distance))  30.6 us
    pallas_call x1, Pallas kernels, mod_backward(): pl.pallas_call(functools.partial(mod_backward_kernel, data_size, tensor_s...  24 us
    unnamed x378, local copies, waits for them, and re-layouts  23.2 us
    pallas_call x1, Pallas kernels, attn_backward(): pl.pallas_call(functools.partial(attn_backward_kernel, real), grid=(seqs,...  22.6 us
  transfers between devices with their start and end apart: 17, of which 2 were waited for; matrix products, arithmetic and copies ran while one was open for 13% of the time, Pallas kernels for 5%

profile of v2, /device:TPU:0, one launch (start us, length us, event | category | flops | bytes accessed | tf_op | source)
XLA Modules:
  0.0 895.5 jit_solution(10799972834310472546)
XLA Ops:
  5.3 15.0 %mod_forward.1 = f32[12,3,1536]{2,1,0:T(4,128)S(1)} custom-call(bf16[24,1536]{1,0:T(8,128)(2,1)S(1)} %copy-done.4, bf16[2,288,1536]{2,1,0:T(8,128)(2,1)S(1)} %bitcast.326, bf16[2,288]{1,0:T(2,128)(2,1)S(1)} %copy-done.7), custom_call_target="tpu_custom_call" | custom-call | tf_op jit(solution)/shard_map/mod_forward/pallas_call | solution.py:349
  33.5 3.5 subtract_multiply_fusion
  42.3 9.8 %attn_forward.1 = (bf16[2,3,128,384]{3,2,1,0:T(8,128)(2,1)S(1)}, bf16[2,3,80,384]{3,2,1,0:T(8,128)(2,1)S(1)}) custom-call(f32[2,2,128]{2,1,0:T(2,128)S(1)} %pad_maximum_fusion.10.gain_ref, f32[2,3,128,384]{3,2,1,0:T(8,128)S(1)} %bitcast.335, f32[2,3,128,384]{3,2,1,0:T(8,128)S(1)} %bitcast.333, f32[2,3,128,384]{3,2,1,0:T(8,128)} %bitcast.445, ...), custom_call_target="tpu_custom_call" | custom-call | flops 797442048 | bytes 6709248 | tf_op jit(solution)/shard_map/attn_forward/pallas_call | solution.py:210
  60.6 30.6 %collective-permute-done.2 = f32[240,1536]{1,0:T(8,128)S(1)} collective-permute-done((f32[240,1536]{1,0:T(8,128)S(1)}, f32[240,1536]{1,0:T(8,128)S(1)}, u32[]{:S(2)}, u32[]{:S(2)}) %collective-permute-start.2) | collective-permute-done | bytes 1474592 | tf_op jit(solution)/shard_map/ppermute | solution.py:543
  97.8 3.8 convolution_add_fusion.4.refs_4_
  103.5 7.0 multiply_convert_fusion.1
  110.6 5.4 fusion.171
  116.0 186.9 %ring_mlp_txt.1 = (f32[1,192,1536]{2,1,0:T(8,128)}, f32[1,192,1536]{2,1,0:T(8,128)}, f32[384,1536]{1,0:T(8,128)}) custom-call(bf16[480,1536]{1,0:T(8,128)(2,1)} %bitcast.420, bf16[480,1536]{1,0:T(8,128)(2,1)} %bitcast.422, bf16[480,1536]{1,0:T(8,128)(2,1)} %get-tuple-element.194.refs_2_, bf16[480,1536]{1,0:T(8,128)(2,1)} %get-tuple-element.147.refs_3_, ...), custom_call_target="tpu_custom_call" | custom-call | flops 165150720000 | bytes 16515072 | tf_op jit(solution)/shard_map/ring_mlp_txt/pallas_call | solution.py:691
  316.0 3.8 fusion.11.refs_0_
  320.4 4.9 fusion.25
  325.3 3.8 fusion.31
  332.9 6.1 multiply_convert_fusion
  341.6 8.3 fusion.170
  360.9 3.4 fusion.61.refs_7_
  364.3 3.5 fusion.58.refs_5_
  367.8 189.1 %ring_mlp_img.1 = (f32[1,192,1536]{2,1,0:T(8,128)}, f32[1,192,1536]{2,1,0:T(8,128)}, f32[240,1536]{1,0:T(8,128)}, f32[384,1536]{1,0:T(8,128)}, f32[240,1536]{1,0:T(8,128)}, /*index=5*/f32[384,1536]{1,0:T(8,128)}) custom-call(bf16[768,1536]{1,0:T(8,128)(2,1)} %bitcast.398, bf16[768,1536]{1,0:T(8,128)(2,1)} %bitcast.397, bf16[768,1536]{1,0:T(8,128)(2,1)} %copy-done.161, ...), custom_call_target="tpu_custom_call" | custom-call | flops 165150720000 | bytes 16515072 | tf_op jit(solution)/shard_map/ring_mlp_img/pallas_call | solution.py:691
  566.9 3.8 multiply_reduce_fusion.3
  575.3 5.7 multiply_reduce_fusion.2
  594.8 22.6 %attn_backward.1 = (bf16[2,3,128,1152]{3,2,1,0:T(8,128)(2,1)}, bf16[2,3,80,1152]{3,2,1,0:T(8,128)(2,1)}, f32[3,2,1152]{2,1,0:T(2,128)}, f32[3,4,128]{2,1,0:T(4,128)}) custom-call(f32[2,2,128]{2,1,0:T(2,128)} %copy-done.6, f32[2,3,128,384]{3,2,1,0:T(8,128)} %bitcast.336, f32[2,3,128,384]{3,2,1,0:T(8,128)} %bitcast.334, f32[2,3,128,384]{3,2,1,0:T(8,128)} %bitcast.446, ...), custom_call_target="tpu_custom_call" | custom-call | flops 1993605120 | bytes 9584640 | tf_op jit(solution)/shard_map/attn_backward/pallas_call | solution.py:235
  631.0 4.8 fusion.9
  641.1 3.9 fusion.57.refs_8_
  645.1 189.2 %ring_attn.1 = (f32[3,192,384]{2,1,0:T(8,128)}, f32[3,192,384]{2,1,0:T(8,128)}, f32[1,192,384]{2,1,0:T(8,128)}, f32[1,192,384]{2,1,0:T(8,128)}, f32[384,1536]{1,0:T(8,128)}, /*index=5*/f32[240,1536]{1,0:T(8,128)}) custom-call(bf16[768,1536]{1,0:T(8,128)(2,1)} %fusion.11.refs_0_, bf16[480,1536]{1,0:T(8,128)(2,1)} %fusion.74.refs_1_, ...), custom_call_target="tpu_custom_call" | custom-call | flops 165150720000 | bytes 16515072 | tf_op jit(solution)/shard_map/ring_attn/pallas_call | solution.py:691
  848.4 3.5 multiply_add_fusion.2
  852.3 24.0 %mod_backward.1 = (f32[2,288,1536]{2,1,0:T(8,128)S(1)}, f32[2,288]{1,0:T(2,128)S(1)}, f32[3,1536]{1,0:T(4,128)S(1)}, f32[2,1152]{1,0:T(2,128)S(1)}, f32[2,1536]{...) custom-call(f32[12,3,1536]{2,1,0:T(4,128)S(1)} %constant_dynamic-update-slice_fusion.mod_ref, ...), custom_call_target="tpu_custom_call" | custom-call | tf_op jit(solution)/shard_map/mod_backward/pallas_call | solution.py:497
  (542 shorter events, 149.9 us)
Async XLA Ops:
  21.1 74.5 %copy-start.97 = (f32[3,1536]{1,0:T(4,128)}, f32[3,1536]{1,0:T(4,128)S(1)}, u32[]{:S(2)}) copy-start(f32[3,1536]{1,0:T(4,128)S(1)} %get-tuple-element.186) | copy-start | bytes 55300
  21.1 80.5 %copy-start.88 = (f32[3,1536]{1,0:T(4,128)}, f32[3,1536]{1,0:T(4,128)S(1)}, u32[]{:S(2)}) copy-start(f32[3,1536]{1,0:T(4,128)S(1)} %get-tuple-element.184) | copy-start | bytes 55300
  23.5 72.1 %copy-start.41 = (bf16[3,80,1536]{2,1,0:T(8,128)(2,1)}, bf16[3,80,1536]{2,1,0:T(8,128)(2,1)S(1)}, u32[]{:S(2)}) copy-start(bf16[3,80,1536]{2,1,0:T(8,128)(2,1)S(1)} %get-tuple-element.162) | copy-start | bytes 2211844
  52.7 3.3 collective-permute-start.1
  56.6 34.6 %collective-permute-start.2 = (f32[240,1536]{1,0:T(8,128)S(1)}, f32[240,1536]{1,0:T(8,128)S(1)}, u32[]{:S(2)}, u32[]{:S(2)}) collective-permute-start(f32[240,1536]{1,0:T(8,128)S(1)} %convolution_add_fusion.9), channel_id=1, source_target_pairs={{0,2},{1,3},{2,0},{3,1},{4,6},{5,7},{6,4},{7,5},{8,10},{9,11},{10,... | collective-permute-start | bytes 4423688 | tf_op jit(solution)/shard_map/ppermute | solution.py:543
  59.9 37.5 %collective-permute-start = (f32[384,1536]{1,0:T(8,128)}, f32[384,1536]{1,0:T(8,128)}, u32[]{:S(2)}, u32[]{:S(2)}) collective-permute-start(f32[384,1536]{1,0:T(8,128)} %fusion.96), channel_id=1, source_target_pairs={{0,1},{1,0},{2,3},{3,2},{4,5},{5,4},{6,7},{7,6},{8,9},{9,8},{10,11... | collective-permute-start | bytes 7077896 | tf_op jit(solution)/shard_map/ppermute | solution.py:536
  92.9 8.8 collective-permute-start.3
  116.0 186.9 %copy-start.47 = (f32[384,1536]{1,0:T(8,128)S(1)}, f32[384,1536]{1,0:T(8,128)}, u32[]{:S(2)}) copy-start(f32[384,1536]{1,0:T(8,128)} %convolution_add_fusion.4.refs_4_) | copy-start | bytes 7077892
  308.5 21.1 %collective-permute-start.4 = (f32[3,128,1536]{2,1,0:T(8,128)}, f32[3,128,1536]{2,1,0:T(8,128)}, u32[]{:S(2)}, u32[]{:S(2)}) collective-permute-start(f32[3,128,1536]{2,1,0:T(8,128)} %subtract_multiply_fusion.3), channel_id=1, source_target_pairs={{0,1},{1,0},{2,3},{3,2},{4,5},{5,4},{6,7},{7,6},{8,9},{9,8},{10,11... | collective-permute-start | bytes 7077896 | tf_op jit(solution)/shard_map/ppermute | solution.py:550
  325.3 30.1 %collective-permute-start.8 = (f32[240,1536]{1,0:T(8,128)}, f32[240,1536]{1,0:T(8,128)S(1)}, u32[]{:S(2)}, u32[]{:S(2)}) collective-permute-start(f32[240,1536]{1,0:T(8,128)} %fusion.25), channel_id=1, source_target_pairs={{0,1},{1,0},{2,3},{3,2},{4,5},{5,4},{6,7},{7,6},{8,9},{9,8},{10,11... | collective-permute-start | bytes 4423688 | tf_op jit(solution)/shard_map/ppermute | solution.py:536
  329.2 28.6 %collective-permute-start.6 = (f32[240,1536]{1,0:T(8,128)S(1)}, f32[240,1536]{1,0:T(8,128)S(1)}, u32[]{:S(2)}, u32[]{:S(2)}) collective-permute-start(f32[240,1536]{1,0:T(8,128)S(1)} %fusion.31), channel_id=1, source_target_pairs={{0,1},{1,0},{2,3},{3,2},{4,5},{5,4},{6,7},{7,6},{8,9},{9,8},{10,11... | collective-permute-start | bytes 4423688 | tf_op jit(solution)/shard_map/ppermute | solution.py:536
  341.1 19.8 %collective-permute-start.5 = (f32[384,1536]{1,0:T(8,128)S(1)}, f32[384,1536]{1,0:T(8,128)S(1)}, u32[]{:S(2)}, u32[]{:S(2)}) collective-permute-start(f32[384,1536]{1,0:T(8,128)S(1)} %fusion.15), channel_id=1, source_target_pairs={{0,1},{1,0},{2,3},{3,2},{4,5},{5,4},{6,7},{7,6},{8,9},{9,8},{10,11... | collective-permute-start | bytes 7077896 | tf_op jit(solution)/shard_map/ppermute | solution.py:536
  353.4 11.0 %collective-permute-start.7 = (f32[384,1536]{1,0:T(8,128)S(1)}, f32[384,1536]{1,0:T(8,128)S(1)}, u32[]{:S(2)}, u32[]{:S(2)}) collective-permute-start(f32[384,1536]{1,0:T(8,128)S(1)} %fusion.19), channel_id=1, source_target_pairs={{0,1},{1,0},{2,3},{3,2},{4,5},{5,4},{6,7},{7,6},{8,9},{9,8},{10,11... | collective-permute-start | bytes 7077896 | tf_op jit(solution)/shard_map/ppermute | solution.py:536
  367.8 189.1 %copy-start.89 = (f32[3,1536]{1,0:T(4,128)S(1)}, f32[3,1536]{1,0:T(4,128)}, u32[]{:S(2)}) copy-start(f32[3,1536]{1,0:T(4,128)} %copy-done.88) | copy-start | bytes 55300
  574.6 11.8 %collective-permute-start.10 = (f32[3,80,1536]{2,1,0:T(8,128)S(1)}, f32[3,80,1536]{2,1,0:T(8,128)S(1)}, u32[]{:S(2)}, u32[]{:S(2)}) collective-permute-start(f32[3,80,1536]{2,1,0:T(8,128)S(1)} %get-tuple-element.166), channel_id=1, source_target_pairs={{0,1},{1,0},{2,3},{3,2},{4,5},{5,4},{6,7},{7,6},{8,9},{9,8},{10,11... | collective-permute-start | bytes 4423688 | tf_op jit(solution)/shard_map/ppermute | solution.py:550
  574.7 13.4 %collective-permute-start.12 = (f32[3,80,1536]{2,1,0:T(8,128)S(1)}, f32[3,80,1536]{2,1,0:T(8,128)S(1)}, u32[]{:S(2)}, u32[]{:S(2)}) collective-permute-start(f32[3,80,1536]{2,1,0:T(8,128)S(1)} %get-tuple-element.134), channel_id=1, source_target_pairs={{0,1},{1,0},{2,3},{3,2},{4,5},{5,4},{6,7},{7,6},{8,9},{9,8},{10,11... | collective-permute-start | bytes 4423688 | tf_op jit(solution)/shard_map/ppermute | solution.py:550
  581.0 50.0 %collective-permute-start.9 = (f32[3,128,1536]{2,1,0:T(8,128)}, f32[3,128,1536]{2,1,0:T(8,128)}, u32[]{:S(2)}, u32[]{:S(2)}) collective-permute-start(f32[3,128,1536]{2,1,0:T(8,128)} %get-tuple-element.148), channel_id=1, source_target_pairs={{0,1},{1,0},{2,3},{3,2},{4,5},{5,4},{6,7},{7,6},{8,9},{9,8},{10,11... | collective-permute-start | bytes 7077896 | tf_op jit(solution)/shard_map/ppermute | solution.py:550
  581.1 10.9 %collective-permute-start.11 = (f32[3,128,1536]{2,1,0:T(8,128)S(1)}, f32[3,128,1536]{2,1,0:T(8,128)S(1)}, u32[]{:S(2)}, u32[]{:S(2)}) collective-permute-start(f32[3,128,1536]{2,1,0:T(8,128)S(1)} %get-tuple-element.135), channel_id=1, source_target_pairs={{0,1},{1,0},{2,3},{3,2},{4,5},{5,4},{6,7},{7,6},{8,9},{9,8},{10,11... | collective-permute-start | bytes 7077896 | tf_op jit(solution)/shard_map/ppermute | solution.py:550
  625.3 15.8 %collective-permute-start.13 = (f32[384,1536]{1,0:T(8,128)}, f32[384,1536]{1,0:T(8,128)}, u32[]{:S(2)}, u32[]{:S(2)}) collective-permute-start(f32[384,1536]{1,0:T(8,128)} %convolution_add_fusion), channel_id=1, source_target_pairs={{0,1},{1,0},{2,3},{3,2},{4,5},{5,4},{6,7},{7,6},{8,9},{9,8},{10,11... | collective-permute-start | bytes 7077896 | tf_op jit(solution)/shard_map/ppermute | solution.py:536
  628.4 11.0 %collective-permute-start.14 = (f32[240,1536]{1,0:T(8,128)}, f32[240,1536]{1,0:T(8,128)S(1)}, u32[]{:S(2)}, u32[]{:S(2)}) collective-permute-start(f32[240,1536]{1,0:T(8,128)} %convolution_add_fusion.5), channel_id=1, source_target_pairs={{0,1},{1,0},{2,3},{3,2},{4,5},{5,4},{6,7},{7,6},{8,9},{9,8},{10,11... | collective-permute-start | bytes 4423688 | tf_op jit(solution)/shard_map/ppermute | solution.py:536
  645.1 189.2 %copy-start.51 = (f32[384,1536]{1,0:T(8,128)S(1)}, f32[384,1536]{1,0:T(8,128)}, u32[]{:S(2)}) copy-start(f32[384,1536]{1,0:T(8,128)} %fusion.57.refs_8_) | copy-start | bytes 7077892
  645.1 189.2 %copy-start.87 = (f32[3,1536]{1,0:T(4,128)S(1)}, f32[3,1536]{1,0:T(4,128)}, u32[]{:S(2)}) copy-start(f32[3,1536]{1,0:T(4,128)} %copy-done.85) | copy-start | bytes 55300
  846.7 32.4 %collective-permute-start.16 = (f32[3,80,1536]{2,1,0:T(8,128)}, f32[3,80,1536]{2,1,0:T(8,128)S(1)}, u32[]{:S(2)}, u32[]{:S(2)}) collective-permute-start(f32[3,80,1536]{2,1,0:T(8,128)} %multiply_add_fusion.5), channel_id=1, source_target_pairs={{0,1},{1,0},{2,3},{3,2},{4,5},{5,4},{6,7},{7,6},{8,9},{9,8},{10,11... | collective-permute-start | bytes 4423688 | tf_op jit(solution)/shard_map/ppermute | solution.py:550
  851.9 32.0 %collective-permute-start.15 = (f32[3,128,1536]{2,1,0:T(8,128)}, f32[3,128,1536]{2,1,0:T(8,128)S(1)}, u32[]{:S(2)}, u32[]{:S(2)}) collective-permute-start(f32[3,128,1536]{2,1,0:T(8,128)} %multiply_add_fusion.2), channel_id=1, source_target_pairs={{0,1},{1,0},{2,3},{3,2},{4,5},{5,4},{6,7},{7,6},{8,9},{9,8},{10,11... | collective-permute-start | bytes 7077896 | tf_op jit(solution)/shard_map/ppermute | solution.py:550
  (173 other events, 1256.1 us)

commit v3 on v2

--- a/solution.py
+++ b/solution.py
@@ -7,11 +7,13 @@
 from jax.experimental.pallas import tpu as pltpu
 from jax.sharding import PartitionSpec as P
 
+
 epsilon = 1e-06
 GELU_C = 0.7978845608028654
 GELU_A = 0.044715
 ROW_TILE = 16
 NEG = -1e30
+RESTS = (1, 2, 2)
 
 
 def dot_plain(first_op, second_op):
@@ -528,22 +530,18 @@
     )(mod_grads, conditioning, ada_weight, *group, *every)
 
 
+def norm_of(values):
+    center = values - jnp.mean(values, axis=-1, keepdims=True)
+    inverse = lax.rsqrt(jnp.mean(center * center, axis=-1, keepdims=True) + epsilon)
+    return center * inverse, inverse
+
+
 def swap_pairs(size, distance):
     return [(index, index ^ distance) for index in range(size)]
 
 
 def core_sum(own_part, other_part, tensor_size):
     return own_part + lax.ppermute(other_part, "tensor", swap_pairs(tensor_size, 1))
-
-
-def chip_sum(total, swapped, tensor_size):
-    distance = 2
-    while distance < tensor_size:
-        if swapped is None or distance > 2:
-            swapped = lax.ppermute(total, "tensor", swap_pairs(tensor_size, distance))
-        total = total + swapped
-        distance *= 2
-    return total
 
 
 def share(own_rows, tensor_size):
@@ -597,7 +595,92 @@
     return value
 
 
-def grad_ring_kernel(order, count, swaps, *refs):
+class Ring:
+    def __init__(self, order, rest, lefts, rights, slots, terms, turned, sems):
+        self.order, self.size, self.rest = order, len(order), rest
+        self.lefts, self.rights, self.slots, self.terms = lefts, rights, slots, terms
+        self.turned, self.sems = turned, sems
+        row, col = lax.axis_index("dp"), lax.axis_index("tensor")
+        size = self.size
+        self.place = entry_of([order.index(index) for index in range(size)], row)
+        self.after = entry_of(order, lax.rem(self.place + 1, size))
+        self.before = entry_of(order, lax.rem(self.place + size - 1, size))
+        self.targets = ((self.after, col), (self.before, col))
+        self.half = slots[0].shape[2]
+        self.chains = [(which, way) for which in range(len(lefts)) for way in range(2)]
+        self.last = size - 2 - rest
+
+    def term(self, which, way, index):
+        start = pl.multiple_of((2 * index + way) * self.half, 8)
+        return dot_plain(
+            self.turned[which][pl.ds(start, self.half), :], self.rights[which][...]
+        )
+
+    def work_out(self, indices):
+        for which, way in self.chains:
+            self.terms[which][way] = self.term(which, way, indices[way])
+
+    def copy_of(self, which, way, step, source, target):
+        return pltpu.make_async_remote_copy(
+            src_ref=source,
+            dst_ref=self.slots[which].at[way, target],
+            send_sem=self.sems.at[0, which, way, step],
+            recv_sem=self.sems.at[1, which, way, step],
+            device_id=self.targets[way],
+            device_id_type=pl.DeviceIdType.MESH,
+        )
+
+    def blocks_at(self, step):
+        size = self.size
+        return (
+            entry_of(self.order, lax.rem(self.place + 2 * size - 2 - step, size)),
+            entry_of(self.order, lax.rem(self.place + 2 + step, size)),
+        )
+
+    def arrive(self, which, way, step):
+        slot = self.slots[which].at[way, step]
+        self.copy_of(which, way, step, slot, step).wait_recv()
+
+    def begin(self):
+        for which, left in enumerate(self.lefts):
+            self.turned[which][...] = left[...].T
+            for way in range(2):
+                first = self.slots[which].at[way, self.size - 1]
+                first[...] = self.term(which, way, (self.before, self.after)[way])
+                self.copy_of(which, way, 0, first, 0).start()
+
+    def rounds(self):
+        def round_of(step, carry):
+            self.work_out(self.blocks_at(step))
+            for which, way in self.chains:
+                self.arrive(which, way, step)
+                slot = self.slots[which].at[way, step]
+                slot[...] = slot[...] + self.terms[which][way]
+                self.copy_of(which, way, step + 1, slot, step + 1).start()
+            return carry
+
+        lax.fori_loop(0, self.last, round_of, 0)
+
+    def finish(self, put_later, put_total):
+        for later in range(self.rest):
+            indices = self.blocks_at(self.last + 1 + later)
+            for which, way in self.chains:
+                put_later(later, which, way, self.term(which, way, indices[way]))
+        self.work_out(self.blocks_at(self.last))
+        for which, way in self.chains:
+            self.arrive(which, way, self.last)
+            put_total(which, way, self.slots[which][way, self.last] + self.terms[which][way])
+
+        def sent(step, carry):
+            for which, way in self.chains:
+                slot = self.slots[which].at[way, self.size - 1]
+                self.copy_of(which, way, step, slot, step).wait_send()
+            return carry
+
+        lax.fori_loop(0, self.last + 1, sent, 0)
+
+
+def taker(refs):
     refs = list(refs)
 
     def take(number):
@@ -605,110 +688,361 @@
         del refs[:number]
         return taken
 
+    return take
+
+
+def ring_scratch(size, halves, lefts, count_kind=jnp.bfloat16):
+    return (
+        [pltpu.VMEM((2, size) + half, jnp.float32) for half in halves]
+        + [pltpu.VMEM((2,) + half, jnp.float32) for half in halves]
+        + [pltpu.VMEM(shape[::-1], count_kind) for shape in lefts]
+        + [pltpu.SemaphoreType.DMA((2, len(halves), 2, size - 1))]
+    )
+
+
+def grad_ring_kernel(order, count, swaps, rest, *refs):
+    take = taker(refs)
     lefts, rights, gives = take(count), take(count), take(swaps)
-    outs, gets = take(count), take(swaps)
+    outs = take(2 * (rest + 1)) if rest else take(count)
+    gets = take(swaps)
     slots, terms, turned = take(count), take(count), take(count)
-    (sems,) = take(1)
-    swap_sems = refs[0] if swaps else None
-    size = len(order)
-    row, col = lax.axis_index("dp"), lax.axis_index("tensor")
-    place = entry_of([order.index(index) for index in range(size)], row)
-    after = entry_of(order, lax.rem(place + 1, size))
-    before = entry_of(order, lax.rem(place + size - 1, size))
-    targets = ((after, col), (before, col))
-    half = slots[0].shape[2]
-    facing = (row, xor_index(col, 2))
-
-    greet(targets + ((facing,) if swaps else ()))
+    sems, swap_sems = take(2)
+    ring = Ring(order, rest, lefts, rights, slots, terms, turned, sems)
+    facing = (lax.axis_index("dp"), xor_index(lax.axis_index("tensor"), 2))
+    greet(ring.targets + (facing,))
     swapped = [
         remote(gives[index], gets[index], swap_sems, index, facing) for index in range(swaps)
     ]
-    for left, flipped in zip(lefts, turned):
-        flipped[...] = left[...].T
-
-    def work_out(which, way, index):
-        start = pl.multiple_of((2 * index + way) * half, 8)
-        terms[which][way] = dot_plain(turned[which][pl.ds(start, half), :], rights[which][...])
-
-    def copy_of(which, way, step, source, target):
-        return pltpu.make_async_remote_copy(
-            src_ref=source,
-            dst_ref=slots[which].at[way, target],
-            send_sem=sems.at[0, which, way, step],
-            recv_sem=sems.at[1, which, way, step],
-            device_id=targets[way],
-            device_id_type=pl.DeviceIdType.MESH,
-        )
-
-    chains = [(which, way) for which in range(count) for way in range(2)]
-    for which, way in chains:
-        work_out(which, way, (before, after)[way])
-        slots[which][way, size - 1] = terms[which][way]
-        copy_of(which, way, 0, slots[which].at[way, size - 1], 0).start()
-
-    def arrive(which, way, step):
-        copy_of(which, way, step, slots[which].at[way, step], step).wait_recv()
-
-    def round_of(step, carry):
-        ahead = entry_of(order, lax.rem(place + 2 * size - 2 - step, size))
-        back = entry_of(order, lax.rem(place + 2 + step, size))
-        for which, way in chains:
-            work_out(which, way, (ahead, back)[way])
-        for which, way in chains:
-            arrive(which, way, step)
-            slots[which][way, step] = slots[which][way, step] + terms[which][way]
-            copy_of(which, way, step + 1, slots[which].at[way, step], step + 1).start()
-        return carry
-
-    lax.fori_loop(0, size - 2, round_of, 0)
-    for which, way in chains:
-        work_out(which, way, row)
-    for which, way in chains:
-        arrive(which, way, size - 2)
-        total = slots[which][way, size - 2] + terms[which][way]
+    widths = [right.shape[1] for right in rights]
+    starts = [sum(widths[:which]) for which in range(count)]
+
+    def put_later(later, which, way, values):
+        columns = slice(starts[which], starts[which] + widths[which])
+        outs[2 * (later + 1) + way][:, columns] = values
+
+    def put_total(which, way, values):
+        if rest:
+            outs[way][:, starts[which] : starts[which] + widths[which]] = values
+            return
         parts, _, width = outs[which].shape
         for part in range(parts):
-            outs[which][part, way * half : (way + 1) * half] = total[
+            outs[which][part, way * ring.half : (way + 1) * ring.half] = values[
                 :, part * width : (part + 1) * width
             ]
 
-    def sent(step, carry):
-        for which, way in chains:
-            copy_of(which, way, step, slots[which].at[way, size - 1], step).wait_send()
-        return carry
-
-    lax.fori_loop(0, size - 1, sent, 0)
+    ring.begin()
+    ring.rounds()
+    ring.finish(put_later, put_total)
     for copy in swapped:
         copy.wait()
 
 
-def grad_ring(pairs, gives, order, collective_id, name):
+def mlp_ring_kernel(order, stream, seqs, block, swaps, rest, *refs):
+    take = taker(refs)
+    mod_ref, proj_bias_ref, up_bias_ref = take(3)
+    mine_hbm, got_hbm, input_hbm, cot_hbm, up_hbm, down_hbm = take(6)
+    gives = take(swaps)
+    outs = take(2 * (rest + 1)) if rest else take(2)
+    gets = take(swaps)
+    inverse_ref, up_sum_ref, down_sum_ref = take(3)
+    branch_hbm, normed_hbm, hidden_sum_hbm, hidden_got_hbm, mlp_sum_hbm, mlp_got_hbm = take(6)
+    slots, terms, turned = take(2), take(2), take(2)
+    (ring_sems,) = take(1)
+    up_ref, down_ref, input_ref, hidden_ref, active_ref, grad_up_ref, grad_mlp_ref = take(7)
+    mine_ref, got_ref, branch_ref, normed_ref, normed_in, spare = take(6)
+    load_sems, core_sems, swap_sems, out_sems = take(4)
+    rows, feat = mine_ref.shape
+    units = active_ref.shape[1]
+    length = rows // seqs
+    ring = Ring(
+        order, rest, (grad_mlp_ref, hidden_ref), (active_ref, grad_up_ref), slots, terms, turned, ring_sems
+    )
+    partner = (lax.axis_index("dp"), xor_index(lax.axis_index("tensor"), 1))
+    facing = (lax.axis_index("dp"), xor_index(lax.axis_index("tensor"), 2))
+
+    loads = []
+    for source, target in (
+        (mine_hbm, mine_ref),
+        (got_hbm, got_ref),
+        (input_hbm, input_ref),
+        (cot_hbm, grad_mlp_ref),
+        (up_hbm.at[stream], up_ref),
+        (down_hbm.at[stream], down_ref),
+    ):
+        loads.append(pltpu.make_async_copy(source, target, load_sems.at[len(loads)]))
+        loads[-1].start()
+    greet(ring.targets + (facing, partner))
+    swapped = [
+        remote(gives[index], gets[index], swap_sems, index, facing) for index in range(swaps)
+    ]
+
+    def mod(index, seq):
+        return mod_ref[stream * 6 + index, seq : seq + 1, :]
+
+    stored = []
+
+    def store(source, target):
+        copy = pltpu.make_async_copy(source, target, out_sems.at[len(stored)])
+        copy.start()
+        stored.append(copy)
+        return copy
+
+    for load in loads[:3]:
+        load.wait()
+    copies = []
+    for seq in range(seqs):
+        span = slice(seq * length, (seq + 1) * length)
+        branch = mine_ref[span] + got_ref[span] + proj_bias_ref[stream : stream + 1].astype(jnp.float32)
+        branch_ref[span] = branch
+        normed, inverse = norm_of(input_ref[span].astype(jnp.float32) + mod(2, seq) * branch)
+        normed_ref[span] = normed
+        inverse_ref[span] = inverse
+        hidden_ref[span] = (normed * (1.0 + mod(4, seq)) + mod(3, seq)).astype(jnp.bfloat16)
+        copies.append(remote(normed_ref.at[span], normed_in.at[span], core_sems, seq, partner))
+    kept = [store(branch_ref, branch_hbm), store(normed_ref, normed_hbm)]
+    loads[3].wait()
+    down_total = None
+    for half in range(2):
+        for seq in range(seqs):
+            span = slice(half * rows + seq * length, half * rows + (seq + 1) * length)
+            grad_mlp = grad_mlp_ref[span].astype(jnp.float32) * mod(5, seq)
+            grad_mlp_ref[span] = grad_mlp.astype(jnp.bfloat16)
+            if half == 0:
+                total = jnp.sum(grad_mlp, axis=0, keepdims=True)
+                down_total = total if down_total is None else down_total + total
+    down_sum_ref[...] = down_total
+    for seq, copy in enumerate(copies):
+        copy.wait()
+        span = slice(seq * length, (seq + 1) * length)
+        hidden_ref[rows + seq * length : rows + (seq + 1) * length] = (
+            normed_in[span] * (1.0 + mod(4, seq)) + mod(3, seq)
+        ).astype(jnp.bfloat16)
+    for load in loads[4:]:
+        load.wait()
+
+    def unit_block(index, carry):
+        cols = pl.ds(pl.multiple_of(index * block, block), block)
+        upward = dot_plain(hidden_ref[...], up_ref[:, cols]) + up_bias_ref[
+            stream : stream + 1, cols
+        ].astype(jnp.float32)
+        active, slope = gelu_both(upward)
+        active_ref[:, cols] = active.astype(jnp.bfloat16)
+        grad_up = dot_right_t(grad_mlp_ref[...], down_ref[cols, :]) * slope
+        up_sum_ref[:, cols] = jnp.sum(grad_up, axis=0, keepdims=True)
+        grad_up_ref[:, cols] = grad_up.astype(jnp.bfloat16)
+        return carry
+
+    lax.fori_loop(0, units // block, unit_block, 0)
+    ring.begin()
+
+    for copy in kept:
+        copy.wait()
+    count = feat // block
+    sums = ((branch_ref, mine_ref, normed_in), (normed_ref, got_ref, spare))
+    copies = []
+    for kind, (outgoing, incoming, own) in enumerate(sums):
+        for index in range(count):
+            cols = slice(index * block, (index + 1) * block)
+            if kind == 0:
+                both = dot_right_t(grad_up_ref[...], up_ref[cols, :])
+            else:
+                both = dot_plain(active_ref[...], down_ref[:, cols])
+            own[:, cols] = both[:rows]
+            outgoing[:, cols] = both[rows:]
+            copies.append(
+                remote(
+                    outgoing.at[:, cols],
+                    incoming.at[:, cols],
+                    core_sems,
+                    seqs + kind * count + index,
+                    partner,
+                )
+            )
+    for kind, (target, swap) in enumerate(
+        ((hidden_sum_hbm, hidden_got_hbm), (mlp_sum_hbm, mlp_got_hbm))
+    ):
+        _, incoming, own = sums[kind]
+        for copy in copies[kind * count : (kind + 1) * count]:
+            copy.wait()
+        own[...] = own[...] + incoming[...]
+        store(own, target)
+        swapped.append(remote(own, swap, swap_sems, swaps + kind, facing))
+    ring.rounds()
+
+    buffers = (mine_ref, got_ref, branch_ref, normed_ref)
+    each = rows // (2 * ring.half)
+
+    def piece_of(index):
+        start = index % each * 2 * ring.half
+        return buffers[index // each].at[start : start + 2 * ring.half]
+
+    def put_later(later, which, way, values):
+        piece_of(2 * (later + 1) + way)[which * ring.half : (which + 1) * ring.half] = values
+
+    def put_total(which, way, values):
+        if rest:
+            piece_of(way)[which * ring.half : (which + 1) * ring.half] = values
+        else:
+            outs[which][0, way * ring.half : (way + 1) * ring.half] = values
+
+    ring.finish(put_later, put_total)
+    if rest:
+        for index, out in enumerate(outs):
+            store(piece_of(index), out)
+    for copy in swapped:
+        copy.wait()
+    for copy in stored[len(kept) :]:
+        copy.wait()
+
+
+def mlp_ring(
+    stream, mine, got, inputs, cots, modulate, proj_bias, up_bias, up_weight, down_weight, gives, order, rest,
+    collective_id,
+):
+    _, seqs, length, feat = inputs.shape
+    rows, units, size, swaps = seqs * length, up_weight.shape[2], len(order), len(gives)
+    block = 256
+    half = feat // (2 * size)
+    vmem = pl.BlockSpec(memory_space=pltpu.VMEM)
+    anywhere = pl.BlockSpec(memory_space=pl.ANY)
+
+    def shape(kind, *dims):
+        return jax.ShapeDtypeStruct(dims, kind)
+
+    def low(*dims):
+        return pltpu.VMEM(dims, jnp.bfloat16)
+
+    ring_outs = (
+        [shape(jnp.float32, 2 * half, units)] * (2 * (rest + 1))
+        if rest
+        else [shape(jnp.float32, 1, 2 * half, units)] * 2
+    )
+    gets = [shape(give.dtype, *give.shape) for give in gives]
+    small = [
+        shape(jnp.float32, rows, 1),
+        shape(jnp.float32, 1, units),
+        shape(jnp.float32, 1, feat),
+    ]
+    large = [shape(jnp.float32, rows, feat)] * 6
+    moved = 4 * 2 * 2 * (size - 1) * half * units
+    blocks = 2 * feat // block
+    results = pl.pallas_call(
+        functools.partial(mlp_ring_kernel, order, stream, seqs, block, swaps, rest),
+        out_shape=ring_outs + gets + small + large,
+        in_specs=[vmem] * 3 + [anywhere] * (6 + swaps),
+        out_specs=[anywhere if rest else vmem] * len(ring_outs)
+        + [anywhere] * swaps
+        + [vmem] * 3
+        + [anywhere] * 6,
+        scratch_shapes=ring_scratch(size, [(half, units)] * 2, [(2 * rows, feat)] * 2)
+        + [
+            low(feat, units),
+            low(units, feat),
+            low(rows, feat),
+            low(2 * rows, feat),
+            low(2 * rows, units),
+            low(2 * rows, units),
+            low(2 * rows, feat),
+        ]
+        + [pltpu.VMEM((rows, feat), jnp.float32)] * 6
+        + [
+            pltpu.SemaphoreType.DMA((6,)),
+            pltpu.SemaphoreType.DMA((2, seqs + blocks)),
+            pltpu.SemaphoreType.DMA((2, swaps + 2)),
+            pltpu.SemaphoreType.DMA((4 + len(ring_outs),)),
+        ],
+        compiler_params=pltpu.CompilerParams(
+            collective_id=collective_id, has_side_effects=True, vmem_limit_bytes=67043328
+        ),
+        cost_estimate=pl.CostEstimate(flops=moved * 10000, bytes_accessed=moved, transcendentals=0),
+        name="mlp_ring",
+    )(
+        modulate,
+        proj_bias,
+        up_bias,
+        mine,
+        got,
+        inputs[0].reshape(rows, feat),
+        cots.reshape(2 * rows, feat),
+        up_weight,
+        down_weight,
+        *gives,
+    )
+    ring_parts, results = results[: len(ring_outs)], results[len(ring_outs) :]
+    names = ("inverse", "up_bias", "down_bias", "branch", "normed", "hidden_sum", "hidden_got", "mlp_sum", "mlp_got")
+    made = dict(zip(names, results[swaps:]))
+    for name in ("inverse", "branch", "normed"):
+        made[name] = made[name].reshape(seqs, length, -1)
+    made["ring"], made["gets"] = ring_parts, results[:swaps]
+    return made
+
+
+def grad_ring(pairs, gives, order, rest, collective_id):
     size, count, swaps = len(order), len(pairs), len(gives)
     vmem = pl.BlockSpec(memory_space=pltpu.VMEM)
     anywhere = pl.BlockSpec(memory_space=pl.ANY)
     halves = [(left.shape[1] // (2 * size), right.shape[1]) for left, right, _ in pairs]
     moved = sum(4 * 2 * (size - 1) * rows * cols for rows, cols in halves)
+    if rest:
+        whole = (halves[0][0], sum(cols for _, cols in halves))
+        shapes = [whole] * (2 * (rest + 1))
+    else:
+        shapes = [
+            (parts, 2 * rows, cols // parts) for (rows, cols), (_, _, parts) in zip(halves, pairs)
+        ]
     results = pl.pallas_call(
-        functools.partial(grad_ring_kernel, order, count, swaps),
-        out_shape=[
-            jax.ShapeDtypeStruct((parts, 2 * rows, cols // parts), jnp.float32)
-            for (rows, cols), (_, _, parts) in zip(halves, pairs)
-        ]
+        functools.partial(grad_ring_kernel, order, count, swaps, rest),
+        out_shape=[jax.ShapeDtypeStruct(shape, jnp.float32) for shape in shapes]
         + [jax.ShapeDtypeStruct(give.shape, give.dtype) for give in gives],
         in_specs=[vmem] * (2 * count) + [anywhere] * swaps,
-        out_specs=[vmem] * count + [anywhere] * swaps,
-        scratch_shapes=[pltpu.VMEM((2, size) + half, jnp.float32) for half in halves]
-        + [pltpu.VMEM((2,) + half, jnp.float32) for half in halves]
-        + [pltpu.VMEM(left.shape[::-1], left.dtype) for left, _, _ in pairs]
-        + [pltpu.SemaphoreType.DMA((2, count, 2, size - 1))]
-        + [pltpu.SemaphoreType.DMA((2, swaps))] * bool(swaps),
+        out_specs=[vmem] * len(shapes) + [anywhere] * swaps,
+        scratch_shapes=ring_scratch(size, halves, [left.shape for left, _, _ in pairs])
+        + [pltpu.SemaphoreType.DMA((2, swaps))],
         compiler_params=pltpu.CompilerParams(
             collective_id=collective_id, has_side_effects=True, vmem_limit_bytes=58 << 20
         ),
         cost_estimate=pl.CostEstimate(flops=moved * 10000, bytes_accessed=moved, transcendentals=0),
-        name=name,
     )(*[left for left, _, _ in pairs], *[right for _, right, _ in pairs], *gives)
-    return results[:count], results[count:]
+    return results[: len(shapes)], results[len(shapes) :]
+
+
+def ring_rest(parts, order, rest):
+    size = len(order)
+    ahead = [(order[index], order[(index + 1) % size]) for index in range(size)]
+    ways = (ahead, [(second, first) for first, second in ahead])
+    totals = list(parts[:2])
+    for later in range(rest):
+        for way in range(2):
+            totals[way] = lax.ppermute(totals[way], "dp", ways[way])
+        for way in range(2):
+            totals[way] = totals[way] + parts[2 * (later + 1) + way]
+    return totals
+
+
+def by_columns(totals, pairs):
+    blocks, start = [], 0
+    for _, right, split in pairs:
+        width = right.shape[1] // split
+        blocks.append(
+            jnp.stack(
+                [
+                    jnp.concatenate(
+                        [total[:, start + part * width : start + (part + 1) * width] for total in totals]
+                    )
+                    for part in range(split)
+                ]
+            )
+        )
+        start += right.shape[1]
+    return blocks
+
+
+def by_rows(totals):
+    half = totals[0].shape[0] // 2
+    return [
+        jnp.concatenate([total[which * half : (which + 1) * half] for total in totals])[None]
+        for which in range(2)
+    ]
 
 
 def on_device(
@@ -779,40 +1113,26 @@
     attn = attn_forward(gain_pair, raw[0], raw[1], reals[1])
     local = attn[0].shape[3]
 
-    def mlp_stage(stream, total):
-        branch = total.reshape(shapes[stream][1:]) + proj_bias[stream]
-        residual = inputs[stream][0].astype(jnp.float32) + piece[stream][2] * branch
-        normed, inverse = layer_norm(residual)
-        hidden = share(normed, tensor_size) * (1.0 + piece[stream][4]) + piece[stream][3]
-        hidden = hidden.astype(jnp.bfloat16).reshape(-1, feat)
-        upward = dot_plain(hidden, up_weight[stream]) + up_bias[stream].astype(jnp.float32)
-        active, slope = gelu_both(upward)
-        active = active.astype(jnp.bfloat16)
-        grad_mlp = cotangents[stream].astype(jnp.float32) * piece[stream][5]
-        grad_mlp_low = grad_mlp.astype(jnp.bfloat16).reshape(-1, feat)
-        grad_up = dot_right_t(grad_mlp_low, down_weight[stream]) * slope
-        grad_up_low = grad_up.astype(jnp.bfloat16)
-        half = grad_up_low.shape[0] // 2
-        hidden_sum = core_sum(
-            dot_right_t(grad_up_low[:half], up_weight[stream]),
-            dot_right_t(grad_up_low[half:], up_weight[stream]),
-            tensor_size,
-        )
-        mlp_sum = core_sum(
-            dot_plain(active[:half], down_weight[stream]),
-            dot_plain(active[half:], down_weight[stream]),
-            tensor_size,
-        )
-        return {
-            "branch": branch,
-            "normed": normed,
-            "inverse": inverse,
-            "pairs": [(grad_mlp_low, active, 1), (hidden, grad_up_low, 1)],
-            "hidden_sum": hidden_sum,
-            "mlp_sum": mlp_sum,
-            "up_bias": jnp.sum(grad_up, axis=0),
-            "down_bias": jnp.sum(grad_mlp[0], axis=(0, 1)),
-        }
+    def mlp_stage(stream, got, gives, rest, collective_id):
+        made = mlp_ring(
+            stream,
+            branch_sums[stream],
+            got,
+            inputs[stream],
+            cotangents[stream],
+            modulate,
+            proj_bias,
+            up_bias,
+            up_weight,
+            down_weight,
+            gives,
+            order,
+            rest,
+            collective_id,
+        )
+        if rest:
+            made["ring"] = by_rows(ring_rest(made["ring"], order, rest))
+        return made
 
     branch_sums = [None, None]
     for stream in (1, 0):
@@ -822,16 +1142,13 @@
             dot_plain(rows[1], proj_weight[stream]),
             tensor_size,
         )
-    state, mlp_rings = [None, None], [None, None]
-    state[1] = mlp_stage(1, chip_sum(branch_sums[1], None, tensor_size))
-    mlp_rings[1], (swapped,) = grad_ring(
-        state[1]["pairs"], [branch_sums[0]], order, 2, "ring_mlp_txt"
-    )
-    state[0] = mlp_stage(0, chip_sum(branch_sums[0], swapped, tensor_size))
-    gives = [state[stream][key] for key in ("hidden_sum", "mlp_sum") for stream in (1, 0)]
-    mlp_rings[0], swapped = grad_ring(state[0]["pairs"], gives, order, 3, "ring_mlp_img")
-    gives = [chip_sum(give, get, tensor_size) for give, get in zip(gives, swapped)]
-    hidden_sums, mlp_sums = gives[1::-1], gives[:1:-1]
+    state = [None, None]
+    got = lax.ppermute(branch_sums[1], "tensor", swap_pairs(tensor_size, 2))
+    state[1] = mlp_stage(1, got, [branch_sums[0]], RESTS[0], 2)
+    state[0] = mlp_stage(0, state[1]["gets"][0], [], RESTS[1], 3)
+    mlp_rings = [state[stream]["ring"] for stream in range(2)]
+    hidden_sums = [state[stream]["hidden_sum"] + state[stream]["hidden_got"] for stream in range(2)]
+    mlp_sums = [state[stream]["mlp_sum"] + state[stream]["mlp_got"] for stream in range(2)]
 
     grad_attn, proj_pairs, proj_sums, resid_grads, mod_grads = ([None, None] for _ in range(5))
     outputs = [None, None]
@@ -878,12 +1195,17 @@
             )
 
         first_sums[stream] = core_sum(
-            through_weights(slice(None, half)), through_weights(slice(half, None)), tensor_size
+            through_weights(slice(None, half)),
+            through_weights(slice(half, None)),
+            tensor_size,
         )
         qkv_pairs[stream] = (hidden1[stream], packed_low, 3)
-    rings, swapped = grad_ring(qkv_pairs + proj_pairs, first_sums, order, 4, "ring_attn")
+    pairs = qkv_pairs + proj_pairs
+    rings, swapped = grad_ring(pairs, first_sums, order, RESTS[2], 4)
+    if RESTS[2]:
+        rings = by_columns(ring_rest(rings, order, RESTS[2]), pairs)
     qkv_rings, proj_rings = rings[:2], rings[2:]
-    first_sums = [chip_sum(give, get, tensor_size) for give, get in zip(first_sums, swapped)]
+    first_sums = [give + get for give, get in zip(first_sums, swapped)]
 
     grad_inputs = [None, None]
     for stream in (1, 0):
@@ -911,11 +1233,11 @@
         jnp.stack(mod_grads[0] + mod_grads[1]),
         conditioning,
         ada_weight,
-        [qkv_bias_sums, jnp.stack([state[0]["up_bias"], state[1]["up_bias"]])],
+        [qkv_bias_sums, jnp.concatenate([state[0]["up_bias"], state[1]["up_bias"]])],
         [
             gain_sums,
             jnp.stack(proj_sums) * row_share,
-            jnp.stack([state[0]["down_bias"], state[1]["down_bias"]]) * row_share,
+            jnp.concatenate([state[0]["down_bias"], state[1]["down_bias"]]) * row_share,
         ],
         data_size,
         tensor_size,
@@ -985,10 +1307,8 @@
         P(None, "tensor", "dp"),
         P(),
     )
-    return jax.shard_map(
-        functools.partial(on_device, ring_order(mesh), mesh.shape["tensor"]),
-        mesh=mesh,
-        in_specs=in_specs,
-        out_specs=out_specs,
-        check_vma=False,
-    )
+
+    def step(*arrays):
+        return on_device(ring_order(mesh), mesh.shape["tensor"], *arrays)
+
+    return jax.shard_map(step, mesh=mesh, in_specs=in_specs, out_specs=out_specs, check_vma=False)

time: 902 us -> 798 us (0.88)
  Pallas kernels: 637 us -> 548 us
  matrix products: 92.4 us -> 38.3 us
  waiting for transfers between devices: 33.6 us -> 55 us
  starting transfers between devices: 4.16 us -> 13.4 us
    pallas_call x3, Pallas kernels: 565 us -> 468 us  [the longest x2 329 us: mlp_ring(): pl.pallas_call(functools.partial(mlp_ring_kernel, order, stream, seqs, bl...]
    dot_general x20 -> x14, matrix products: 51.3 us -> 20.5 us  [dot_right_t(): lax.dot_general(first_op, second_op, (((1,), (1,)), ((), ())), preferred_...]
    ppermute x1 -> x11, waiting for transfers between devices: 30.6 us -> 55 us  [the longest x10 29.7 us: ring_rest(): totals[way] = lax.ppermute(totals[way], 'dp', ways[way])]
    dot_general x16 -> x10, matrix products: 41.1 us -> 17.8 us  [dot_plain(): return jnp.dot(first_op, second_op, preferred_element_type=jnp.float32)]
    ppermute x1 -> x11, starting transfers between devices: 1.03 us -> 11.4 us  [the longest x10 10.4 us: ring_rest(): totals[way] = lax.ppermute(totals[way], 'dp', ways[way])]
    unnamed x378 -> x276, local copies, waits for them, and re-layouts: 23.2 us -> 26.7 us
  transfers between devices with their start and end apart: 17 -> 21, of which waited for: 2 -> 5; matrix products, arithmetic and copies ran while one was open for 13% -> 13% of each run, Pallas kernels for 5% -> 27%
where the time goes in v3:
time: 798 us; the launch traced here: 791 us
  Pallas kernels  548 us (69%)
  other arithmetic  102 us (13%)
  waiting for transfers between devices  55 us (7%)
  matrix products  38.3 us (5%)
  local copies, waits for them, and re-layouts  31.2 us (4%)
  starting transfers between devices  13.4 us (2%)
    pallas_call x2, Pallas kernels, mlp_ring(): pl.pallas_call(functools.partial(mlp_ring_kernel, order, stream, seqs, bl...  329 us
    pallas_call x1, Pallas kernels, grad_ring(): pl.pallas_call(functools.partial(grad_ring_kernel, order, count, swaps, r...  140 us
    pallas_call x1, Pallas kernels, mod_backward(): pl.pallas_call(functools.partial(mod_backward_kernel, data_size, tensor_s...  32 us
    ppermute x10, waiting for transfers between devices, ring_rest(): totals[way] = lax.ppermute(totals[way], 'dp', ways[way])  29.7 us
    unnamed x276, local copies, waits for them, and re-layouts  26.7 us
    ppermute x1, waiting for transfers between devices, on_device(): got = lax.ppermute(branch_sums[1], 'tensor', swap_pairs(tensor_size, 2))  25.2 us
    pallas_call x1, Pallas kernels, attn_backward(): pl.pallas_call(functools.partial(attn_backward_kernel, real), grid=(seqs,...  22.5 us
    dot_general x14, matrix products, dot_right_t(): lax.dot_general(first_op, second_op, (((1,), (1,)), ((), ())), preferred_...  20.5 us
  transfers between devices with their start and end apart: 21, of which 5 were waited for; matrix products, arithmetic and copies ran while one was open for 13% of the time, Pallas kernels for 27%

profile of v3, /device:TPU:0, one launch (start us, length us, event | category | flops | bytes accessed | tf_op | source)
XLA Modules:
  0.0 790.8 jit_solution(8034168221754623155)
XLA Ops:
  5.3 15.0 %mod_forward.1.refs_0_ = f32[12,3,1536]{2,1,0:T(4,128)S(1)} custom-call(bf16[24,1536]{1,0:T(8,128)(2,1)S(1)} %copy-done.5, bf16[2,288,1536]{2,1,0:T(8,128)(2,1)S(1)} %bitcast.313, bf16[2,288]{1,0:T(2,128)(2,1)S(1)} %copy-done.8), custom_call_target="tpu_custom_call" | custom-call | tf_op jit(solution)/shard_map/mod_forward/pallas_call | solution.py:351
  27.7 2.9 subtract_multiply_fusion.1
  33.6 3.5 subtract_multiply_fusion
  42.4 9.8 %attn_forward.1 = (bf16[2,3,128,384]{3,2,1,0:T(8,128)(2,1)S(1)}, bf16[2,3,80,384]{3,2,1,0:T(8,128)(2,1)S(1)}) custom-call(f32[2,2,128]{2,1,0:T(2,128)S(1)} %pad_maximum_fusion.10.gain_ref, f32[2,3,128,384]{3,2,1,0:T(8,128)S(1)} %bitcast.322, f32[2,3,128,384]{3,2,1,0:T(8,128)S(1)} %bitcast.320, f32[2,3,128,384]{3,2,1,0:T(8,128)} %bitcast.421, ...), custom_call_target="tpu_custom_call" | custom-call | flops 797442048 | bytes 6709248 | tf_op jit(solution)/shard_map/attn_forward/pallas_call | solution.py:212
  57.6 3.4 fusion.9.refs_1_
  61.1 3.7 fusion.3.refs_0_
  74.2 3.9 convolution_add_fusion.4.refs_9_.refs_3_
  78.1 25.2 %collective-permute-done.2.refs_4_ = f32[240,1536]{1,0:T(8,128)S(1)} collective-permute-done((f32[240,1536]{1,0:T(8,128)S(1)}, f32[240,1536]{1,0:T(8,128)S(1)}, u32[]{:S(2)}, u32[]{:S(2)}) %collective-permute-start.2) | collective-permute-done | bytes 1474592 | tf_op jit(solution)/shard_map/ppermute | solution.py:1146
  104.4 173.4 %mlp_ring.2 = (f32[192,1536]{1,0:T(8,128)}, f32[192,1536]{1,0:T(8,128)}, f32[192,1536]{1,0:T(8,128)}, f32[192,1536]{1,0:T(8,128)}, f32[384,1536]{1,0:T(8,128)}, ...) custom-call(f32[12,3,1536]{2,1,0:T(4,128)} %copy-done.2, ...), custom_call_target="tpu_custom_call" | custom-call | flops 165150720000 | bytes 16515072 | tf_op jit(solution)/shard_map/mlp_ring/pallas_call | solution.py:929
  287.1 3.6 multiply_reduce_fusion.6
  290.8 155.2 %mlp_ring.3 = (f32[192,1536]{1,0:T(8,128)}, f32[192,1536]{1,0:T(8,128)}, f32[192,1536]{1,0:T(8,128)}, f32[192,1536]{1,0:T(8,128)}, f32[192,1536]{1,0:T(8,128)}, ...) custom-call(f32[12,3,1536]{2,1,0:T(4,128)} %copy-done.2, ...), custom_call_target="tpu_custom_call" | custom-call | flops 165150720000 | bytes 16515072 | tf_op jit(solution)/shard_map/mlp_ring/pallas_call | solution.py:929
  449.1 3.8 fusion.19
  456.6 3.9 multiply_reduce_fusion.2
  466.4 8.8 %collective-permute-done.15 = f32[192,1536]{1,0:T(8,128)S(1)} collective-permute-done((f32[192,1536]{1,0:T(8,128)}, f32[192,1536]{1,0:T(8,128)S(1)}, u32[]{:S(2)}, u32[]{:S(2)}) %collective-permute-start.15) | collective-permute-done | bytes 1179680 | tf_op jit(solution)/shard_map/ppermute | solution.py:1016
  481.6 3.0 fusion.6
  491.4 22.5 %attn_backward.1 = (bf16[2,3,128,1152]{3,2,1,0:T(8,128)(2,1)}, bf16[2,3,80,1152]{3,2,1,0:T(8,128)(2,1)}, f32[3,2,1152]{2,1,0:T(2,128)}, f32[3,4,128]{2,1,0:T(4,128)}) custom-call(f32[2,2,128]{2,1,0:T(2,128)} %copy-done.7, f32[2,3,128,384]{3,2,1,0:T(8,128)} %bitcast.323, f32[2,3,128,384]{3,2,1,0:T(8,128)} %bitcast.321, f32[2,3,128,384]{3,2,1,0:T(8,128)} %bitcast.422, ...), custom_call_target="tpu_custom_call" | custom-call | flops 1993605120 | bytes 9584640 | tf_op jit(solution)/shard_map/attn_backward/pallas_call | solution.py:237
  529.8 4.0 fusion
  546.5 139.8 %shard_map.279 = (f32[96,3072]{1,0:T(8,128)}, f32[96,3072]{1,0:T(8,128)}, f32[96,3072]{1,0:T(8,128)}, f32[96,3072]{1,0:T(8,128)}, f32[96,3072]{1,0:T(8,128)}, /*...) custom-call(bf16[768,1536]{1,0:T(8,128)(2,1)} %fusion.3.refs_0_, bf16[480,1536]{1,0:T(8,128)(2,1)} %fusion.9.refs_1_, ...), custom_call_target="tpu_custom_call" | custom-call | flops 165150720000 | bytes 16515072 | tf_op jit(solution)/shard_map/pallas_call | solution.py:993
  686.4 2.8 fusion.18
  699.4 4.1 multiply_reduce_fusion.7
  703.8 3.0 multiply_reduce_fusion.3
  709.4 32.0 %mod_backward.1 = (f32[2,288,1536]{2,1,0:T(8,128)S(1)}, f32[2,288]{1,0:T(2,128)S(1)}, f32[3,1536]{1,0:T(4,128)S(1)}, f32[2,1152]{1,0:T(2,128)S(1)}, f32[2,1536]{...) custom-call(f32[12,3,1536]{2,1,0:T(4,128)S(1)} %constant_dynamic-update-slice_fusion.mod_ref, ...), custom_call_target="tpu_custom_call" | custom-call | tf_op jit(solution)/shard_map/mod_backward/pallas_call | solution.py:499
  754.1 20.0 %collective-permute-done.12 = f32[96,3072]{1,0:T(8,128)S(1)} collective-permute-done((f32[96,3072]{1,0:T(8,128)S(1)}, f32[96,3072]{1,0:T(8,128)S(1)}, u32[]{:S(2)}, u32[]{:S(2)}) %collective-permute-start.12) | collective-permute-done | bytes 1179680 | tf_op jit(solution)/shard_map/ppermute | solution.py:1016
  779.2 2.6 fusion.2
  (440 shorter events, 138.0 us)
Async XLA Ops:
  1.5 40.9 %copy-start.7 = (f32[2,2,128]{2,1,0:T(2,128)}, f32[2,2,128]{2,1,0:T(2,128)S(1)}, u32[]{:S(2)}) copy-start(f32[2,2,128]{2,1,0:T(2,128)S(1)} %pad_maximum_fusion.10.gain_ref) | copy-start | bytes 6148
  21.1 39.9 %copy-start.68 = (f32[3,1536]{1,0:T(4,128)}, f32[3,1536]{1,0:T(4,128)S(1)}, u32[]{:S(2)}) copy-start(f32[3,1536]{1,0:T(4,128)S(1)} %get-tuple-element.246) | copy-start | bytes 55300
  54.7 11.9 %collective-permute-start.1 = (f32[240,1536]{1,0:T(8,128)}, f32[240,1536]{1,0:T(8,128)}, u32[]{:S(2)}, u32[]{:S(2)}) collective-permute-start(f32[240,1536]{1,0:T(8,128)} %fusion.27), channel_id=1, source_target_pairs={{0,1},{1,0},{2,3},{3,2},{4,5},{5,4},{6,7},{7,6},{8,9},{9,8},{10,11... | collective-permute-start | bytes 4423688 | tf_op jit(solution)/shard_map/ppermute | solution.py:544
  57.3 16.9 %collective-permute-start = (f32[384,1536]{1,0:T(8,128)}, f32[384,1536]{1,0:T(8,128)}, u32[]{:S(2)}, u32[]{:S(2)}) collective-permute-start(f32[384,1536]{1,0:T(8,128)} %fusion.31), channel_id=1, source_target_pairs={{0,1},{1,0},{2,3},{3,2},{4,5},{5,4},{6,7},{7,6},{8,9},{9,8},{10,11... | collective-permute-start | bytes 7077896 | tf_op jit(solution)/shard_map/ppermute | solution.py:544
  68.7 34.6 %collective-permute-start.2 = (f32[240,1536]{1,0:T(8,128)S(1)}, f32[240,1536]{1,0:T(8,128)S(1)}, u32[]{:S(2)}, u32[]{:S(2)}) collective-permute-start(f32[240,1536]{1,0:T(8,128)S(1)} %convolution_add_fusion.9.refs_3_), channel_id=1, source_target_pairs={{0,2},{1,3},{2,0},{3,1},{4,6},{5,7},{6,4},{7,5},{8,10},{9,11},{10,... | collective-permute-start | bytes 4423688 | tf_op jit(solution)/shard_map/ppermute | solution.py:1146
  282.6 179.3 %collective-permute-start.19 = (f32[192,1536]{1,0:T(8,128)}, f32[192,1536]{1,0:T(8,128)}, u32[]{:S(2)}, u32[]{:S(2)}) collective-permute-start(f32[192,1536]{1,0:T(8,128)} %get-tuple-element.112), channel_id=1, source_target_pairs={{0,4},{4,12},{12,20},{20,28},{28,24},{24,16},{16,8},{8,0},{1,5},{5... | collective-permute-start | bytes 3538952 | tf_op jit(solution)/shard_map/ppermute | solution.py:1016
  283.6 181.0 %collective-permute-start.20 = (f32[192,1536]{1,0:T(8,128)}, f32[192,1536]{1,0:T(8,128)}, u32[]{:S(2)}, u32[]{:S(2)}) collective-permute-start(f32[192,1536]{1,0:T(8,128)} %get-tuple-element.114), channel_id=1, source_target_pairs={{4,0},{12,4},{20,12},{28,20},{24,28},{16,24},{8,16},{0,8},{5,1},{1... | collective-permute-start | bytes 3538952 | tf_op jit(solution)/shard_map/ppermute | solution.py:1016
  290.7 190.5 %collective-permute-start.4 = (f32[3,80,1536]{2,1,0:T(8,128)}, f32[3,80,1536]{2,1,0:T(8,128)}, u32[]{:S(2)}, u32[]{:S(2)}) collective-permute-start(f32[3,80,1536]{2,1,0:T(8,128)} %get-tuple-element.202), channel_id=1, source_target_pairs={{0,1},{1,0},{2,3},{3,2},{4,5},{5,4},{6,7},{7,6},{8,9},{9,8},{10,11... | collective-permute-start | bytes 4423688 | tf_op jit(solution)/shard_map/ppermute | solution.py:548
  447.0 28.1 %collective-permute-start.15 = (f32[192,1536]{1,0:T(8,128)}, f32[192,1536]{1,0:T(8,128)S(1)}, u32[]{:S(2)}, u32[]{:S(2)}) collective-permute-start(f32[192,1536]{1,0:T(8,128)} %get-tuple-element.106), channel_id=1, source_target_pairs={{0,4},{4,12},{12,20},{20,28},{28,24},{24,16},{16,8},{8,0},{1,5},{5... | collective-permute-start | bytes 3538952 | tf_op jit(solution)/shard_map/ppermute | solution.py:1016
  448.8 27.7 %collective-permute-start.17 = (f32[192,1536]{1,0:T(8,128)}, f32[192,1536]{1,0:T(8,128)S(1)}, u32[]{:S(2)}, u32[]{:S(2)}) collective-permute-start(f32[192,1536]{1,0:T(8,128)} %get-tuple-element.109), channel_id=1, source_target_pairs={{4,0},{12,4},{20,12},{28,20},{24,28},{16,24},{8,16},{0,8},{5,1},{1... | collective-permute-start | bytes 3538952 | tf_op jit(solution)/shard_map/ppermute | solution.py:1016
  462.7 21.9 %collective-permute-start.6 = (f32[3,80,1536]{2,1,0:T(8,128)S(1)}, f32[3,80,1536]{2,1,0:T(8,128)S(1)}, u32[]{:S(2)}, u32[]{:S(2)}) collective-permute-start(f32[3,80,1536]{2,1,0:T(8,128)S(1)} %copy-done.50), channel_id=1, source_target_pairs={{0,1},{1,0},{2,3},{3,2},{4,5},{5,4},{6,7},{7,6},{8,9},{9,8},{10,11... | collective-permute-start | bytes 4423688 | tf_op jit(solution)/shard_map/ppermute | solution.py:548
  464.6 64.4 %collective-permute-start.3 = (f32[3,128,1536]{2,1,0:T(8,128)}, f32[3,128,1536]{2,1,0:T(8,128)}, u32[]{:S(2)}, u32[]{:S(2)}) collective-permute-start(f32[3,128,1536]{2,1,0:T(8,128)} %get-tuple-element.186), channel_id=1, source_target_pairs={{0,1},{1,0},{2,3},{3,2},{4,5},{5,4},{6,7},{7,6},{8,9},{9,8},{10,11... | collective-permute-start | bytes 7077896 | tf_op jit(solution)/shard_map/ppermute | solution.py:548
  475.1 13.4 %collective-permute-start.5 = (f32[3,128,1536]{2,1,0:T(8,128)S(1)}, f32[3,128,1536]{2,1,0:T(8,128)S(1)}, u32[]{:S(2)}, u32[]{:S(2)}) collective-permute-start(f32[3,128,1536]{2,1,0:T(8,128)S(1)} %get-tuple-element.177), channel_id=1, source_target_pairs={{0,1},{1,0},{2,3},{3,2},{4,5},{5,4},{6,7},{7,6},{8,9},{9,8},{10,11... | collective-permute-start | bytes 7077896 | tf_op jit(solution)/shard_map/ppermute | solution.py:548
  476.5 57.3 %collective-permute-start.16 = (f32[192,1536]{1,0:T(8,128)}, f32[192,1536]{1,0:T(8,128)}, u32[]{:S(2)}, u32[]{:S(2)}) collective-permute-start(f32[192,1536]{1,0:T(8,128)} %add.477), channel_id=1, source_target_pairs={{0,4},{4,12},{12,20},{20,28},{28,24},{24,16},{16,8},{8,0},{1,5},{5... | collective-permute-start | bytes 3538952 | tf_op jit(solution)/shard_map/ppermute | solution.py:1016
  481.2 54.1 %collective-permute-start.18 = (f32[192,1536]{1,0:T(8,128)}, f32[192,1536]{1,0:T(8,128)}, u32[]{:S(2)}, u32[]{:S(2)}) collective-permute-start(f32[192,1536]{1,0:T(8,128)} %add.479), channel_id=1, source_target_pairs={{4,0},{12,4},{20,12},{28,20},{24,28},{16,24},{8,16},{0,8},{5,1},{1... | collective-permute-start | bytes 3538952 | tf_op jit(solution)/shard_map/ppermute | solution.py:1016
  521.6 21.0 %collective-permute-start.8 = (f32[240,1536]{1,0:T(8,128)S(1)}, f32[240,1536]{1,0:T(8,128)S(1)}, u32[]{:S(2)}, u32[]{:S(2)}) collective-permute-start(f32[240,1536]{1,0:T(8,128)S(1)} %convolution_add_fusion.5), channel_id=1, source_target_pairs={{0,1},{1,0},{2,3},{3,2},{4,5},{5,4},{6,7},{7,6},{8,9},{9,8},{10,11... | collective-permute-start | bytes 4423688 | tf_op jit(solution)/shard_map/ppermute | solution.py:544
  525.5 18.8 %collective-permute-start.7 = (f32[384,1536]{1,0:T(8,128)S(1)}, f32[384,1536]{1,0:T(8,128)S(1)}, u32[]{:S(2)}, u32[]{:S(2)}) collective-permute-start(f32[384,1536]{1,0:T(8,128)S(1)} %convolution_add_fusion), channel_id=1, source_target_pairs={{0,1},{1,0},{2,3},{3,2},{4,5},{5,4},{6,7},{7,6},{8,9},{9,8},{10,11... | collective-permute-start | bytes 7077896 | tf_op jit(solution)/shard_map/ppermute | solution.py:544
  546.5 139.8 %copy-start.69 = (f32[3,1536]{1,0:T(4,128)S(1)}, f32[3,1536]{1,0:T(4,128)}, u32[]{:S(2)}) copy-start(f32[3,1536]{1,0:T(4,128)} %copy-done.68) | copy-start | bytes 55300
  697.2 47.4 %collective-permute-start.11 = (f32[96,3072]{1,0:T(8,128)}, f32[96,3072]{1,0:T(8,128)}, u32[]{:S(2)}, u32[]{:S(2)}) collective-permute-start(f32[96,3072]{1,0:T(8,128)} %get-tuple-element.97), channel_id=1, source_target_pairs={{0,4},{4,12},{12,20},{20,28},{28,24},{24,16},{16,8},{8,0},{1,5},{5... | collective-permute-start | bytes 3538952 | tf_op jit(solution)/shard_map/ppermute | solution.py:1016
  698.0 49.5 %collective-permute-start.13 = (f32[96,3072]{1,0:T(8,128)}, f32[96,3072]{1,0:T(8,128)S(1)}, u32[]{:S(2)}, u32[]{:S(2)}) collective-permute-start(f32[96,3072]{1,0:T(8,128)} %get-tuple-element.100), channel_id=1, source_target_pairs={{4,0},{12,4},{20,12},{28,20},{24,28},{16,24},{8,16},{0,8},{5,1},{1... | collective-permute-start | bytes 3538952 | tf_op jit(solution)/shard_map/ppermute | solution.py:1016
  703.6 44.9 %collective-permute-start.10 = (f32[3,80,1536]{2,1,0:T(8,128)}, f32[3,80,1536]{2,1,0:T(8,128)}, u32[]{:S(2)}, u32[]{:S(2)}) collective-permute-start(f32[3,80,1536]{2,1,0:T(8,128)} %get-tuple-element.185), channel_id=1, source_target_pairs={{0,1},{1,0},{2,3},{3,2},{4,5},{5,4},{6,7},{7,6},{8,9},{9,8},{10,11... | collective-permute-start | bytes 4423688 | tf_op jit(solution)/shard_map/ppermute | solution.py:548
  706.7 71.6 %collective-permute-start.9 = (f32[3,128,1536]{2,1,0:T(8,128)}, f32[3,128,1536]{2,1,0:T(8,128)}, u32[]{:S(2)}, u32[]{:S(2)}) collective-permute-start(f32[3,128,1536]{2,1,0:T(8,128)} %get-tuple-element.184), channel_id=1, source_target_pairs={{0,1},{1,0},{2,3},{3,2},{4,5},{5,4},{6,7},{7,6},{8,9},{9,8},{10,11... | collective-permute-start | bytes 7077896 | tf_op jit(solution)/shard_map/ppermute | solution.py:548
  746.2 28.0 %collective-permute-start.12 = (f32[96,3072]{1,0:T(8,128)S(1)}, f32[96,3072]{1,0:T(8,128)S(1)}, u32[]{:S(2)}, u32[]{:S(2)}) collective-permute-start(f32[96,3072]{1,0:T(8,128)S(1)} %add.473), channel_id=1, source_target_pairs={{0,4},{4,12},{12,20},{20,28},{28,24},{24,16},{16,8},{8,0},{1,5},{5... | collective-permute-start | bytes 3538952 | tf_op jit(solution)/shard_map/ppermute | solution.py:1016
  747.6 27.4 %collective-permute-start.14 = (f32[96,3072]{1,0:T(8,128)S(1)}, f32[96,3072]{1,0:T(8,128)S(1)}, u32[]{:S(2)}, u32[]{:S(2)}) collective-permute-start(f32[96,3072]{1,0:T(8,128)S(1)} %add.475), channel_id=1, source_target_pairs={{4,0},{12,4},{20,12},{28,20},{24,28},{16,24},{8,16},{0,8},{5,1},{1... | collective-permute-start | bytes 3538952 | tf_op jit(solution)/shard_map/ppermute | solution.py:1016
  (126 other events, 592.1 us)

commit v4 on v3

--- a/solution.py
+++ b/solution.py
@@ -13,7 +13,7 @@
 GELU_A = 0.044715
 ROW_TILE = 16
 NEG = -1e30
-RESTS = (1, 2, 2)
+RESTS = (1, 1)
 
 
 def dot_plain(first_op, second_op):
@@ -365,58 +365,28 @@
     )(conditioning, ada_weight, ada_bias)
 
 
-def mod_backward_kernel(
-    data_size,
-    tensor_size,
-    mod_ref,
-    cond_ref,
-    weight_ref,
-    *refs,
-):
-    refs = list(refs)
-
-    def take(number):
-        taken = refs[:number]
-        del refs[:number]
-        return taken
-
-    group_refs, all_refs = take(2), take(3)
-    weight_out, bias_out, silu_out = take(3)
-    group_outs, all_outs = take(2), take(3)
-    blocks, core_in, outgoing, cols_in, lines, lines_in, lines_own, lines_all = take(8)
-    silu_blocks, silu_in, silu_send, silu_recv, all_send, all_recv, sems = take(7)
+def mod_backward_steps(data_size, tensor_size, mod_rows, cond_ref, weight_of, lines_of, put, scratch, sems):
+    blocks, core_in, outgoing, cols_in, lines, lines_in, lines_own, lines_all = scratch[:8]
+    silu_blocks, silu_in, silu_send, silu_recv, all_send, all_recv = scratch[8:]
     row, col, around, across = peers_of(data_size, tensor_size)
-    seqs, feat = silu_out.shape
-    cols = bias_out.shape[1]
+    seqs, cols = outgoing.shape[1] // 2, outgoing.shape[2]
+    half, width = lines.shape[1] // 2, lines.shape[2]
     for stream in range(2):
-        full = jnp.concatenate([mod_ref[stream * 6 + index] for index in range(6)], axis=1)
+        full = mod_rows(stream)
         for first in range(data_size):
             for second in range(tensor_size):
                 start = (first * tensor_size + second) * cols
                 blocks[second, first, stream * seqs : (stream + 1) * seqs] = full[
                     :, start : start + cols
                 ]
-    silu_cond = silu_of(cond_ref)
-    half = lines.shape[1] // 2
-    width = lines.shape[2]
-
-    def line_up(sources):
-        padded = [
-            jnp.pad(ref[...], ((0, 0), (0, feat - ref.shape[1]))) for ref in sources
-        ]
-        short = half - sum(ref.shape[0] for ref in sources)
-        if short:
-            padded.append(jnp.zeros((short, feat), jnp.float32))
-        return jnp.concatenate(padded, axis=0)
-
-    every_line = jnp.concatenate([line_up(group_refs), line_up(all_refs)], axis=0)
+    every_line = lines_of()
     for index in range(data_size):
         lines[index] = every_line[:, index * width : (index + 1) * width]
-    greet(around + across)
 
     used = 0
     copy = remote(blocks.at[xor_index(col, 1)], core_in, sems, used, across[0])
     used += 1
+    yield
     copy.wait()
     for first in range(data_size):
         outgoing[first] = blocks[col, first] + core_in[first]
@@ -430,6 +400,8 @@
                 remote(source.at[partner[0]], target.at[row], sems, used, partner)
             )
             used += 1
+    silu_cond = silu_of(cond_ref)
+    yield
     for copy in copies:
         copy.wait()
     lines_own[...] = functools.reduce(jnp.add, [lines_in[index] for index in range(data_size)])
@@ -439,13 +411,13 @@
             [cols_in[index, stream * seqs : (stream + 1) * seqs] for index in range(data_size)],
             axis=0,
         )
-        bias_out[stream : stream + 1] = jnp.sum(wide, axis=0, keepdims=True)
+        put(("ada_bias", stream), jnp.sum(wide, axis=0, keepdims=True))
         low.append(wide.astype(jnp.bfloat16))
-    silu_grad = dot_plain(low[0], weight_ref[0]) + dot_plain(low[1], weight_ref[1])
+    silu_grad = dot_plain(low[0], weight_of(0)) + dot_plain(low[1], weight_of(1))
     for index in range(data_size):
         silu_blocks[index] = silu_grad[index * seqs : (index + 1) * seqs]
     for stream in range(2):
-        weight_out[stream] = dot_left_t(low[stream], silu_cond)
+        put(("ada_weight", stream), lambda span: dot_left_t(low[stream], silu_cond[:, span]))
 
     silu_in[row] = silu_blocks[row]
     lines_all[row] = lines_own[...]
@@ -457,20 +429,13 @@
         ):
             copies.append(remote(source, target, sems, used, partner))
             used += 1
+    yield
     for copy in copies:
         copy.wait()
     silu_send[0] = functools.reduce(jnp.add, [silu_in[index] for index in range(data_size)])
     every_line = jnp.concatenate([lines_all[index] for index in range(data_size)], axis=1)
     all_send[0] = every_line[half:]
-
-    def hand_out(values, targets):
-        start = 0
-        for target in targets:
-            count, size = target.shape
-            target[...] = values[start : start + count, :size]
-            start += count
-
-    hand_out(every_line[:half], group_outs)
+    put("group", every_line[:half])
 
     for level, partner in enumerate(across):
         copies = [
@@ -478,56 +443,38 @@
             remote(all_send.at[level], all_recv.at[level], sems, used + 1, partner),
         ]
         used += 2
+        yield
         for copy in copies:
             copy.wait()
         silu_send[level + 1] = silu_send[level] + silu_recv[level]
         all_send[level + 1] = all_send[level] + all_recv[level]
-    silu_out[...] = silu_send[len(across)]
-    hand_out(all_send[len(across)], all_outs)
-
-
-def mod_backward(mod_grads, conditioning, ada_weight, group, every, data_size, tensor_size):
-    _, seqs, feat = mod_grads.shape
-    cols = ada_weight.shape[1]
-    levels = tensor_size.bit_length() - 1
-    vmem = pl.BlockSpec(memory_space=pltpu.VMEM)
-    lines, width = 16, feat // data_size
+    put("silu", silu_send[len(across)])
+    put("every", all_send[len(across)])
+
+
+def mod_scratch(data_size, tensor_size, seqs, feat, cols):
+    levels, lines = tensor_size.bit_length() - 1, 16
+    width = feat // data_size
 
     def wide(*shape):
         return pltpu.VMEM(shape, jnp.float32)
 
-    return pl.pallas_call(
-        functools.partial(mod_backward_kernel, data_size, tensor_size),
-        out_shape=[
-            jax.ShapeDtypeStruct(ada_weight.shape, jnp.float32),
-            jax.ShapeDtypeStruct((2, cols), jnp.float32),
-            jax.ShapeDtypeStruct((seqs, feat), jnp.float32),
-        ]
-        + [jax.ShapeDtypeStruct(each.shape, jnp.float32) for each in group + every],
-        in_specs=[vmem] * (3 + len(group) + len(every)),
-        out_specs=[vmem] * (3 + len(group) + len(every)),
-        scratch_shapes=[
-            wide(tensor_size, data_size, 2 * seqs, cols),
-            wide(data_size, 2 * seqs, cols),
-            wide(data_size, 2 * seqs, cols),
-            wide(data_size, 2 * seqs, cols),
-            wide(data_size, lines, width),
-            wide(data_size, lines, width),
-            wide(lines, width),
-            wide(data_size, lines, width),
-            wide(data_size, seqs, feat),
-            wide(data_size, seqs, feat),
-            wide(levels + 1, seqs, feat),
-            wide(levels, seqs, feat),
-            wide(levels + 1, lines // 2, feat),
-            wide(levels, lines // 2, feat),
-            pltpu.SemaphoreType.DMA((2, 1 + 4 * (data_size - 1) + 2 * levels)),
-        ],
-        compiler_params=pltpu.CompilerParams(
-            collective_id=1, has_side_effects=True, vmem_limit_bytes=48 << 20
-        ),
-        name="mod_backward",
-    )(mod_grads, conditioning, ada_weight, *group, *every)
+    return [
+        wide(tensor_size, data_size, 2 * seqs, cols),
+        wide(data_size, 2 * seqs, cols),
+        wide(data_size, 2 * seqs, cols),
+        wide(data_size, 2 * seqs, cols),
+        wide(data_size, lines, width),
+        wide(data_size, lines, width),
+        wide(lines, width),
+        wide(data_size, lines, width),
+        wide(data_size, seqs, feat),
+        wide(data_size, seqs, feat),
+        wide(levels + 1, seqs, feat),
+        wide(levels, seqs, feat),
+        wide(levels + 1, lines // 2, feat),
+        wide(levels, lines // 2, feat),
+    ], pltpu.SemaphoreType.DMA((2, 1 + 4 * (data_size - 1) + 2 * levels))
 
 
 def norm_of(values):
@@ -542,11 +489,6 @@
 
 def core_sum(own_part, other_part, tensor_size):
     return own_part + lax.ppermute(other_part, "tensor", swap_pairs(tensor_size, 1))
-
-
-def share(own_rows, tensor_size):
-    other = lax.ppermute(own_rows, "tensor", swap_pairs(tensor_size, 1))
-    return jnp.stack([own_rows, other])
 
 
 def ring_order(mesh):
@@ -595,6 +537,28 @@
     return value
 
 
+def over_rows(base, length, feat, count, body):
+    tile = ROW_TILE
+    group = next(size for size in (4, 5, 3, 2, 1) if length // tile % size == 0)
+
+    def step(index, carry):
+        for place in range(group):
+            start = pl.multiple_of(base + (index * group + place) * tile, tile)
+            adds = body(pl.ds(start, tile))
+            carry = tuple(
+                total + add[: tile // 2] + add[tile // 2 :] for total, add in zip(carry, adds)
+            )
+        return carry
+
+    zero = jnp.zeros((tile // 2, feat), jnp.float32)
+    totals = lax.fori_loop(0, length // (tile * group), step, (zero,) * count)
+    return [jnp.sum(total, axis=0, keepdims=True) for total in totals]
+
+
+def shifted(rows, by):
+    return pl.ds(pl.multiple_of(rows.start + by, ROW_TILE), rows.size)
+
+
 class Ring:
     def __init__(self, order, rest, lefts, rights, slots, terms, turned, sems):
         self.order, self.size, self.rest = order, len(order), rest
@@ -641,15 +605,16 @@
         slot = self.slots[which].at[way, step]
         self.copy_of(which, way, step, slot, step).wait_recv()
 
-    def begin(self):
-        for which, left in enumerate(self.lefts):
-            self.turned[which][...] = left[...].T
-            for way in range(2):
-                first = self.slots[which].at[way, self.size - 1]
-                first[...] = self.term(which, way, (self.before, self.after)[way])
-                self.copy_of(which, way, 0, first, 0).start()
-
-    def rounds(self):
+    def begin(self, which):
+        width = 256
+        for start in range(0, self.turned[which].shape[0], width):
+            self.turned[which][start : start + width] = self.lefts[which][:, start : start + width].T
+        for way in range(2):
+            first = self.slots[which].at[way, self.size - 1]
+            first[...] = self.term(which, way, (self.before, self.after)[way])
+            self.copy_of(which, way, 0, first, 0).start()
+
+    def rounds(self, first, last):
         def round_of(step, carry):
             self.work_out(self.blocks_at(step))
             for which, way in self.chains:
@@ -659,7 +624,7 @@
                 self.copy_of(which, way, step + 1, slot, step + 1).start()
             return carry
 
-        lax.fori_loop(0, self.last, round_of, 0)
+        lax.fori_loop(first, last, round_of, 0)
 
     def finish(self, put_later, put_total):
         for later in range(self.rest):
@@ -700,57 +665,22 @@
     )
 
 
-def grad_ring_kernel(order, count, swaps, rest, *refs):
-    take = taker(refs)
-    lefts, rights, gives = take(count), take(count), take(swaps)
-    outs = take(2 * (rest + 1)) if rest else take(count)
-    gets = take(swaps)
-    slots, terms, turned = take(count), take(count), take(count)
-    sems, swap_sems = take(2)
-    ring = Ring(order, rest, lefts, rights, slots, terms, turned, sems)
-    facing = (lax.axis_index("dp"), xor_index(lax.axis_index("tensor"), 2))
-    greet(ring.targets + (facing,))
-    swapped = [
-        remote(gives[index], gets[index], swap_sems, index, facing) for index in range(swaps)
-    ]
-    widths = [right.shape[1] for right in rights]
-    starts = [sum(widths[:which]) for which in range(count)]
-
-    def put_later(later, which, way, values):
-        columns = slice(starts[which], starts[which] + widths[which])
-        outs[2 * (later + 1) + way][:, columns] = values
-
-    def put_total(which, way, values):
-        if rest:
-            outs[way][:, starts[which] : starts[which] + widths[which]] = values
-            return
-        parts, _, width = outs[which].shape
-        for part in range(parts):
-            outs[which][part, way * ring.half : (way + 1) * ring.half] = values[
-                :, part * width : (part + 1) * width
-            ]
-
-    ring.begin()
-    ring.rounds()
-    ring.finish(put_later, put_total)
-    for copy in swapped:
-        copy.wait()
-
-
 def mlp_ring_kernel(order, stream, seqs, block, swaps, rest, *refs):
     take = taker(refs)
-    mod_ref, proj_bias_ref, up_bias_ref = take(3)
-    mine_hbm, got_hbm, input_hbm, cot_hbm, up_hbm, down_hbm = take(6)
+    mod_ref, proj_bias_ref, up_bias_ref, down_bias_ref = take(4)
+    mine_hbm, got_hbm, input_hbm, cot_hbm, up_hbm, down_hbm, proj_hbm = take(7)
     gives = take(swaps)
     outs = take(2 * (rest + 1)) if rest else take(2)
     gets = take(swaps)
-    inverse_ref, up_sum_ref, down_sum_ref = take(3)
-    branch_hbm, normed_hbm, hidden_sum_hbm, hidden_got_hbm, mlp_sum_hbm, mlp_got_hbm = take(6)
+    up_sum_ref, down_sum_ref, proj_sum_ref, mod_sum_ref = take(4)
+    branch_hbm, normed_hbm, hidden_got_hbm, mlp_got_hbm, through_hbm = take(5)
+    grad_branch_hbm, grad_attn_hbm, out_hbm = take(3)
     slots, terms, turned = take(2), take(2), take(2)
     (ring_sems,) = take(1)
     up_ref, down_ref, input_ref, hidden_ref, active_ref, grad_up_ref, grad_mlp_ref = take(7)
+    proj_ref, grad_attn_ref, inverse_ref = take(3)
     mine_ref, got_ref, branch_ref, normed_ref, normed_in, spare = take(6)
-    load_sems, core_sems, swap_sems, out_sems = take(4)
+    load_sems, core_sems, swap_sems, out_sems, again_sems, ready_sem = take(6)
     rows, feat = mine_ref.shape
     units = active_ref.shape[1]
     length = rows // seqs
@@ -768,6 +698,7 @@
         (cot_hbm, grad_mlp_ref),
         (up_hbm.at[stream], up_ref),
         (down_hbm.at[stream], down_ref),
+        (proj_hbm.at[stream], proj_ref),
     ):
         loads.append(pltpu.make_async_copy(source, target, load_sems.at[len(loads)]))
         loads[-1].start()
@@ -775,6 +706,8 @@
     swapped = [
         remote(gives[index], gets[index], swap_sems, index, facing) for index in range(swaps)
     ]
+    spans = [slice(seq * length, (seq + 1) * length) for seq in range(seqs)]
+    other_spans = [slice(rows + seq * length, rows + (seq + 1) * length) for seq in range(seqs)]
 
     def mod(index, seq):
         return mod_ref[stream * 6 + index, seq : seq + 1, :]
@@ -787,36 +720,60 @@
         stored.append(copy)
         return copy
 
+    loaded = []
+
+    def load_again(source, target):
+        copy = pltpu.make_async_copy(source, target, again_sems.at[len(loaded)])
+        copy.start()
+        loaded.append(copy)
+        return copy
+
+    def row_sum(values):
+        return jnp.sum(values, axis=0, keepdims=True)
+
     for load in loads[:3]:
         load.wait()
     copies = []
-    for seq in range(seqs):
-        span = slice(seq * length, (seq + 1) * length)
-        branch = mine_ref[span] + got_ref[span] + proj_bias_ref[stream : stream + 1].astype(jnp.float32)
-        branch_ref[span] = branch
-        normed, inverse = norm_of(input_ref[span].astype(jnp.float32) + mod(2, seq) * branch)
-        normed_ref[span] = normed
-        inverse_ref[span] = inverse
-        hidden_ref[span] = (normed * (1.0 + mod(4, seq)) + mod(3, seq)).astype(jnp.bfloat16)
+    proj_bias = proj_bias_ref[stream : stream + 1].astype(jnp.float32)
+    for seq, span in enumerate(spans):
+        gate, shift, scale = mod(2, seq), mod(3, seq), 1.0 + mod(4, seq)
+
+        def second_norm(at):
+            branch = mine_ref[at] + got_ref[at] + proj_bias
+            branch_ref[at] = branch
+            normed, inverse = norm_of(input_ref[at].astype(jnp.float32) + gate * branch)
+            normed_ref[at] = normed
+            inverse_ref[at] = inverse
+            hidden_ref[at] = (normed * scale + shift).astype(jnp.bfloat16)
+            return ()
+
+        over_rows(span.start, length, feat, 0, second_norm)
         copies.append(remote(normed_ref.at[span], normed_in.at[span], core_sems, seq, partner))
     kept = [store(branch_ref, branch_hbm), store(normed_ref, normed_hbm)]
     loads[3].wait()
-    down_total = None
-    for half in range(2):
-        for seq in range(seqs):
-            span = slice(half * rows + seq * length, half * rows + (seq + 1) * length)
-            grad_mlp = grad_mlp_ref[span].astype(jnp.float32) * mod(5, seq)
-            grad_mlp_ref[span] = grad_mlp.astype(jnp.bfloat16)
-            if half == 0:
-                total = jnp.sum(grad_mlp, axis=0, keepdims=True)
-                down_total = total if down_total is None else down_total + total
+    down_total = 0.0
+    for half_spans in (spans, other_spans):
+        for seq, span in enumerate(half_spans):
+            gate = mod(5, seq)
+
+            def gated(at):
+                grad_mlp = grad_mlp_ref[at].astype(jnp.float32) * gate
+                grad_mlp_ref[at] = grad_mlp.astype(jnp.bfloat16)
+                return (grad_mlp,)
+
+            (total,) = over_rows(span.start, length, feat, 1, gated)
+            if half_spans is spans:
+                down_total = down_total + total
     down_sum_ref[...] = down_total
     for seq, copy in enumerate(copies):
         copy.wait()
-        span = slice(seq * length, (seq + 1) * length)
-        hidden_ref[rows + seq * length : rows + (seq + 1) * length] = (
-            normed_in[span] * (1.0 + mod(4, seq)) + mod(3, seq)
-        ).astype(jnp.bfloat16)
+        shift, scale = mod(3, seq), 1.0 + mod(4, seq)
+
+        def other_hidden(at):
+            hidden_ref[shifted(at, rows)] = (normed_in[at] * scale + shift).astype(jnp.bfloat16)
+            return ()
+
+        over_rows(spans[seq].start, length, feat, 0, other_hidden)
     for load in loads[4:]:
         load.wait()
 
@@ -828,12 +785,13 @@
         active, slope = gelu_both(upward)
         active_ref[:, cols] = active.astype(jnp.bfloat16)
         grad_up = dot_right_t(grad_mlp_ref[...], down_ref[cols, :]) * slope
-        up_sum_ref[:, cols] = jnp.sum(grad_up, axis=0, keepdims=True)
+        up_sum_ref[:, cols] = row_sum(grad_up)
         grad_up_ref[:, cols] = grad_up.astype(jnp.bfloat16)
         return carry
 
     lax.fori_loop(0, units // block, unit_block, 0)
-    ring.begin()
+    for which in range(2):
+        ring.begin(which)
 
     for copy in kept:
         copy.wait()
@@ -858,16 +816,96 @@
                     partner,
                 )
             )
-    for kind, (target, swap) in enumerate(
-        ((hidden_sum_hbm, hidden_got_hbm), (mlp_sum_hbm, mlp_got_hbm))
-    ):
+    exchanges = []
+    for kind, got in enumerate((hidden_got_hbm, mlp_got_hbm)):
         _, incoming, own = sums[kind]
-        for copy in copies[kind * count : (kind + 1) * count]:
-            copy.wait()
-        own[...] = own[...] + incoming[...]
-        store(own, target)
-        swapped.append(remote(own, swap, swap_sems, swaps + kind, facing))
-    ring.rounds()
+        for index in range(count):
+            copies[kind * count + index].wait()
+            cols = slice(index * block, (index + 1) * block)
+            own[:, cols] = own[:, cols] + incoming[:, cols]
+        exchanges.append(remote(own, got, swap_sems, swaps + kind, facing))
+    pl.semaphore_signal(ready_sem, inc=1, device_id=partner, device_id_type=pl.DeviceIdType.MESH)
+    again = [load_again(branch_hbm, branch_ref), load_again(normed_hbm, normed_ref)]
+    cot_again = load_again(cot_hbm, hidden_ref)
+    middle = min(3, ring.last)
+    ring.rounds(0, middle)
+
+    exchanges[0].wait()
+    again.append(load_again(hidden_got_hbm, mine_ref))
+    for copy in again + [cot_again]:
+        copy.wait()
+    pl.semaphore_wait(ready_sem, 1)
+    copies, proj_total = [], 0.0
+    for seq, span in enumerate(spans):
+        gate, scale = mod(2, seq), 1.0 + mod(4, seq)
+
+        def back(at):
+            grad_hidden = normed_in[at] + mine_ref[at]
+            normed = normed_ref[at]
+            through = norm_back(grad_hidden * scale, normed, inverse_ref[at])
+            grad_resid = hidden_ref[at].astype(jnp.float32) + through
+            branch = branch_ref[at]
+            normed_in[at] = through
+            branch_ref[at] = grad_resid
+            grad_mlp_ref[at] = (grad_resid * gate).astype(jnp.bfloat16)
+            return grad_resid * branch, grad_hidden, grad_hidden * normed, grad_resid
+
+        totals = over_rows(span.start, length, feat, 4, back)
+        for index in range(3):
+            mod_sum_ref[index, seq : seq + 1] = totals[index]
+        proj_total = proj_total + totals[3] * gate
+        copies.append(
+            remote(branch_ref.at[span], got_ref.at[span], core_sems, seqs + 2 * count + seq, partner)
+        )
+    proj_sum_ref[...] = proj_total
+    store(normed_in, through_hbm)
+    for seq, copy in enumerate(copies):
+        copy.wait()
+        gate = mod(2, seq)
+
+        def other_back(at):
+            grad_mlp_ref[shifted(at, rows)] = (got_ref[at] * gate).astype(jnp.bfloat16)
+            return ()
+
+        over_rows(spans[seq].start, length, feat, 0, other_back)
+    grad_attn_ref[...] = dot_right_t(grad_mlp_ref[...], proj_ref[...]).astype(jnp.bfloat16)
+    store(grad_mlp_ref, grad_branch_hbm)
+    store(grad_attn_ref, grad_attn_hbm)
+    pl.semaphore_signal(ready_sem, inc=1, device_id=partner, device_id_type=pl.DeviceIdType.MESH)
+    again = [load_again(branch_hbm, branch_ref)]
+    ring.rounds(middle, ring.last)
+
+    exchanges[1].wait()
+    again.append(load_again(mlp_got_hbm, mine_ref))
+    for copy in again:
+        copy.wait()
+    pl.semaphore_wait(ready_sem, 1)
+    copies = []
+    down_bias = down_bias_ref[stream : stream + 1].astype(jnp.float32)
+    for seq, span in enumerate(spans):
+        first_gate, second_gate = mod(2, seq), mod(5, seq)
+
+        def finish_rows(at):
+            mlp_out = spare[at] + mine_ref[at] + down_bias
+            added = first_gate * branch_ref[at] + second_gate * mlp_out
+            normed_ref[at] = added
+            input_ref[at] = (input_ref[at].astype(jnp.float32) + added).astype(jnp.bfloat16)
+            return (hidden_ref[at].astype(jnp.float32) * mlp_out,)
+
+        (mod_sum_ref[3, seq : seq + 1],) = over_rows(span.start, length, feat, 1, finish_rows)
+        copies.append(
+            remote(normed_ref.at[span], got_ref.at[span], core_sems, 2 * seqs + 2 * count + seq, partner)
+        )
+
+    def other_rows(at):
+        there = shifted(at, rows)
+        input_ref[there] = (input_ref[there].astype(jnp.float32) + got_ref[at]).astype(jnp.bfloat16)
+        return ()
+
+    for seq, copy in enumerate(copies):
+        copy.wait()
+        over_rows(spans[seq].start, length, feat, 0, other_rows)
+    store(input_ref, out_hbm)
 
     buffers = (mine_ref, got_ref, branch_ref, normed_ref)
     each = rows // (2 * ring.half)
@@ -896,60 +934,71 @@
 
 
 def mlp_ring(
-    stream, mine, got, inputs, cots, modulate, proj_bias, up_bias, up_weight, down_weight, gives, order, rest,
-    collective_id,
+    stream, mine, got, inputs, cots, modulate, proj_bias, up_bias, down_bias, up_weight, down_weight,
+    proj_weight, gives, order, rest, collective_id,
 ):
     _, seqs, length, feat = inputs.shape
     rows, units, size, swaps = seqs * length, up_weight.shape[2], len(order), len(gives)
+    local = proj_weight.shape[1]
     block = 256
     half = feat // (2 * size)
     vmem = pl.BlockSpec(memory_space=pltpu.VMEM)
     anywhere = pl.BlockSpec(memory_space=pl.ANY)
 
-    def shape(kind, *dims):
-        return jax.ShapeDtypeStruct(dims, kind)
+    def wide(*dims):
+        return jax.ShapeDtypeStruct(dims, jnp.float32)
+
+    def narrow(*dims):
+        return jax.ShapeDtypeStruct(dims, jnp.bfloat16)
 
     def low(*dims):
         return pltpu.VMEM(dims, jnp.bfloat16)
 
-    ring_outs = (
-        [shape(jnp.float32, 2 * half, units)] * (2 * (rest + 1))
-        if rest
-        else [shape(jnp.float32, 1, 2 * half, units)] * 2
-    )
-    gets = [shape(give.dtype, *give.shape) for give in gives]
-    small = [
-        shape(jnp.float32, rows, 1),
-        shape(jnp.float32, 1, units),
-        shape(jnp.float32, 1, feat),
-    ]
-    large = [shape(jnp.float32, rows, feat)] * 6
+    ring_outs = [wide(2 * half, units)] * (2 * (rest + 1)) if rest else [wide(1, 2 * half, units)] * 2
+    gets = [jax.ShapeDtypeStruct(give.shape, give.dtype) for give in gives]
+    small = {
+        "up_bias": wide(1, units),
+        "down_bias": wide(1, feat),
+        "proj_bias": wide(1, feat),
+        "mod_sums": wide(4, seqs, feat),
+    }
+    large = {name: wide(rows, feat) for name in ("branch", "normed", "hidden_got", "mlp_got", "through")}
+    large |= {
+        "grad_branch": narrow(2 * rows, feat),
+        "grad_attn": narrow(2 * rows, local),
+        "out": narrow(2 * rows, feat),
+    }
     moved = 4 * 2 * 2 * (size - 1) * half * units
     blocks = 2 * feat // block
     results = pl.pallas_call(
         functools.partial(mlp_ring_kernel, order, stream, seqs, block, swaps, rest),
-        out_shape=ring_outs + gets + small + large,
-        in_specs=[vmem] * 3 + [anywhere] * (6 + swaps),
+        out_shape=ring_outs + gets + list(small.values()) + list(large.values()),
+        in_specs=[vmem] * 4 + [anywhere] * (7 + swaps),
         out_specs=[anywhere if rest else vmem] * len(ring_outs)
         + [anywhere] * swaps
-        + [vmem] * 3
-        + [anywhere] * 6,
+        + [vmem] * len(small)
+        + [anywhere] * len(large),
         scratch_shapes=ring_scratch(size, [(half, units)] * 2, [(2 * rows, feat)] * 2)
         + [
             low(feat, units),
             low(units, feat),
-            low(rows, feat),
+            low(2 * rows, feat),
             low(2 * rows, feat),
             low(2 * rows, units),
             low(2 * rows, units),
             low(2 * rows, feat),
+            low(local, feat),
+            low(2 * rows, local),
+            pltpu.VMEM((rows, 1), jnp.float32),
         ]
         + [pltpu.VMEM((rows, feat), jnp.float32)] * 6
         + [
+            pltpu.SemaphoreType.DMA((7,)),
+            pltpu.SemaphoreType.DMA((2, 3 * seqs + blocks)),
+            pltpu.SemaphoreType.DMA((2, swaps + 2)),
+            pltpu.SemaphoreType.DMA((6 + len(ring_outs),)),
             pltpu.SemaphoreType.DMA((6,)),
-            pltpu.SemaphoreType.DMA((2, seqs + blocks)),
-            pltpu.SemaphoreType.DMA((2, swaps + 2)),
-            pltpu.SemaphoreType.DMA((4 + len(ring_outs),)),
+            pltpu.SemaphoreType.REGULAR,
         ],
         compiler_params=pltpu.CompilerParams(
             collective_id=collective_id, has_side_effects=True, vmem_limit_bytes=67043328
@@ -960,50 +1009,331 @@
         modulate,
         proj_bias,
         up_bias,
+        down_bias,
         mine,
         got,
-        inputs[0].reshape(rows, feat),
+        inputs.reshape(2 * rows, feat),
         cots.reshape(2 * rows, feat),
         up_weight,
         down_weight,
+        proj_weight,
         *gives,
     )
     ring_parts, results = results[: len(ring_outs)], results[len(ring_outs) :]
-    names = ("inverse", "up_bias", "down_bias", "branch", "normed", "hidden_sum", "hidden_got", "mlp_sum", "mlp_got")
-    made = dict(zip(names, results[swaps:]))
-    for name in ("inverse", "branch", "normed"):
-        made[name] = made[name].reshape(seqs, length, -1)
+    made = dict(zip(list(small) + list(large), results[swaps:]))
     made["ring"], made["gets"] = ring_parts, results[:swaps]
     return made
 
 
-def grad_ring(pairs, gives, order, rest, collective_id):
-    size, count, swaps = len(order), len(pairs), len(gives)
+def attn_ring_kernel(order, tensor_size, seqs, block, row_share, *refs):
+    take = taker(refs)
+    mod_ref, cond_ref, own_cond_ref, gain_sum_ref, bias_sum_ref = take(5)
+    small_sums = (take(4), take(4))
+    packed_hbm, attn_hbm, hidden_hbm, branch_hbm = take(2), take(2), take(2), take(2)
+    through_hbm, input_hbm, cot_hbm = take(2), take(2), take(2)
+    weight_hbm, ada_hbm = take(2)
+    out_hbm, got_hbm = take(2), take(2)
+    qkv_out, proj_out, ada_out = take(3)
+    cond_out, ada_bias_out, qkv_bias_out, up_bias_out, gain_out, proj_bias_out, down_bias_out = take(7)
+    slots, terms, turned = take(4), take(4), take(4)
+    (ring_sems,) = take(1)
+    packed, attn, left, inputs = take(2), take(2), take(2), take(2)
+    (weight_ref,) = take(1)
+    outgoing, incoming, own = take(2), take(2), take(2)
+    (edge_sums,) = take(1)
+    load_sems, core_sems, swap_sems, out_sems, ready_sem = take(5)
+    scratch = take(14)
+    (mod_sems,) = take(1)
+    size = len(order)
+    feat = mod_ref.shape[2]
+    local = attn[0].shape[1]
+    cols = ada_hbm.shape[1]
+    rows = [ref.shape[0] for ref in own]
+    lengths = [count // seqs for count in rows]
+    _, _, around, across = peers_of(size, tensor_size)
+    partner, facing = across[0], across[1]
+    ring = Ring(
+        order, 0, (left[0], left[1], left[0], left[1]), packed + attn, slots, terms, turned, ring_sems
+    )
+    started = []
+
+    def load(source, target):
+        copy = pltpu.make_async_copy(source, target, load_sems.at[len(started)])
+        copy.start()
+        started.append(copy)
+        return copy
+
+    stored = []
+
+    def store(source, target):
+        copy = pltpu.make_async_copy(source, target, out_sems.at[len(stored)])
+        copy.start()
+        stored.append(copy)
+        return copy
+
+    first = [
+        (load(hidden_hbm[stream], left[stream]), load(packed_hbm[stream], packed[stream]))
+        for stream in range(2)
+    ]
+    second = [load(attn_hbm[stream], attn[stream]) for stream in range(2)]
+    weight_load = load(weight_hbm, weight_ref)
+    input_loads = [
+        load(input_hbm[stream].at[: rows[stream]], inputs[stream]) for stream in range(2)
+    ]
+    greet(around + across)
+    again = []
+    for stream in range(2):
+        for copy in first[stream]:
+            copy.wait()
+        ring.begin(stream)
+        again.append(load(branch_hbm[stream], left[stream]))
+    for stream in range(2):
+        again[stream].wait()
+        second[stream].wait()
+        ring.begin(2 + stream)
+    cot_loads = [load(cot_hbm[stream], left[stream]) for stream in range(2)]
+
+    weight_load.wait()
+    count = feat // block
+    exchanges = []
+    copies = {}
+    for stream in (1, 0):
+        for index in range(count):
+            span = slice(index * block, (index + 1) * block)
+            both = sum(
+                dot_right_t(
+                    packed[stream][:, part * local : (part + 1) * local], weight_ref[stream, part, span, :]
+                )
+                for part in range(3)
+            )
+            own[stream][:, span] = both[: rows[stream]]
+            outgoing[stream][:, span] = both[rows[stream] :]
+            copies[stream, index] = remote(
+                outgoing[stream].at[:, span],
+                incoming[stream].at[:, span],
+                core_sems,
+                stream * count + index,
+                partner,
+            )
+    for stream in (1, 0):
+        for index in range(count):
+            copies[stream, index].wait()
+            span = slice(index * block, (index + 1) * block)
+            own[stream][:, span] = own[stream][:, span] + incoming[stream][:, span]
+        exchanges.append(remote(own[stream], got_hbm[stream], swap_sems, stream, facing))
+    through_loads = [load(through_hbm[stream], incoming[stream]) for stream in range(2)]
+    middle = max(ring.last - 2, 0)
+    ring.rounds(0, middle)
+
+    for copy in exchanges:
+        copy.wait()
+    got_loads = [load(got_hbm[stream], outgoing[stream]) for stream in range(2)]
+    for stream in range(2):
+        input_loads[stream].wait()
+        through_loads[stream].wait()
+        cot_loads[stream].wait()
+    for stream in (1, 0):
+        got_loads[stream].wait()
+        for seq in range(seqs):
+            scale = 1.0 + mod_ref[stream * 6 + 1, seq : seq + 1, :]
+
+            def back(at):
+                normed, inverse = norm_of(inputs[stream][at].astype(jnp.float32))
+                grad_hidden = own[stream][at] + outgoing[stream][at]
+                added = incoming[stream][at] + norm_back(grad_hidden * scale, normed, inverse)
+                own[stream][at] = added
+                left[stream][at] = (left[stream][at].astype(jnp.float32) + added).astype(jnp.bfloat16)
+                return grad_hidden, grad_hidden * normed
+
+            totals = over_rows(seq * lengths[stream], lengths[stream], feat, 2, back)
+            for index in range(2):
+                edge_sums[2 * stream + index, seq : seq + 1] = totals[index]
+    pl.semaphore_signal(ready_sem, inc=1, device_id=partner, device_id_type=pl.DeviceIdType.MESH)
+
+    def mod_rows(stream):
+        inner = small_sums[stream][3]
+        return jnp.concatenate(
+            [edge_sums[2 * stream], edge_sums[2 * stream + 1]] + [inner[index] for index in range(4)],
+            axis=1,
+        )
+
+    def lines_of():
+        def wide(values):
+            return jnp.pad(values, ((0, 0), (0, feat - values.shape[1])))
+
+        bias = functools.reduce(jnp.add, [bias_sum_ref[seq] for seq in range(seqs)])
+        gain = functools.reduce(jnp.add, [gain_sum_ref[seq] for seq in range(seqs)])
+        gain = gain[:, : gain.shape[1] // 2] + gain[:, gain.shape[1] // 2 :]
+        group = [wide(bias)] + [wide(small_sums[stream][0][...]) for stream in range(2)]
+        every = [wide(gain)]
+        every += [small_sums[stream][1][...] * row_share for stream in range(2)]
+        every += [small_sums[stream][2][...] * row_share for stream in range(2)]
+        return jnp.concatenate(group + [jnp.zeros((4, feat), jnp.float32)] + every, axis=0)
+
+    def put(name, values):
+        if name == "group":
+            for part in range(3):
+                qkv_bias_out[part] = values[0:2, part * local : (part + 1) * local]
+            up_bias_out[...] = values[2:4, : up_bias_out.shape[1]]
+        elif name == "every":
+            for stream in range(2):
+                gain_out[stream] = values[2 * stream : 2 * stream + 2, : gain_out.shape[2]]
+            proj_bias_out[...] = values[4:6]
+            down_bias_out[...] = values[6:8]
+        elif name == "silu":
+            cond = own_cond_ref[...]
+            sig = 1.0 / (1.0 + jnp.exp(-cond))
+            cond_out[...] = values * sig * (1.0 + cond * (1.0 - sig))
+        elif name[0] == "ada_bias":
+            ada_bias_out[name[1] : name[1] + 1] = values
+        else:
+            target = own[0] if name[1] == 0 else incoming[0]
+            for start in range(0, feat, block):
+                target[:cols, start : start + block] = values(slice(start, start + block))
+            store(target.at[:cols], ada_out.at[name[1]])
+
+    def weight_of(stream):
+        return left[0][stream * cols : (stream + 1) * cols]
+
+    steps = mod_backward_steps(
+        size, tensor_size, mod_rows, cond_ref, weight_of, lines_of, put, scratch, mod_sems
+    )
+    next(steps)
+    pl.semaphore_wait(ready_sem, 1)
+    shares = [
+        remote(own[stream], outgoing[stream], core_sems, 2 * count + stream, partner)
+        for stream in range(2)
+    ]
+    next(steps)
+    for copy in shares:
+        copy.wait()
+    results = []
+    for stream in (1, 0):
+        def other_rows(at):
+            there = shifted(at, rows[stream])
+            left[stream][there] = (
+                left[stream][there].astype(jnp.float32) + outgoing[stream][at]
+            ).astype(jnp.bfloat16)
+            return ()
+
+        for seq in range(seqs):
+            over_rows(seq * lengths[stream], lengths[stream], feat, 0, other_rows)
+        results.append(store(left[stream], out_hbm[stream]))
+    ring.rounds(middle, ring.last - 1)
+    results[1].wait()
+    ada_loads = [
+        load(ada_hbm.at[stream], left[0].at[stream * cols : (stream + 1) * cols]) for stream in range(2)
+    ]
+    for copy in ada_loads:
+        copy.wait()
+    next(steps)
+    ring.rounds(ring.last - 1, ring.last)
+    for _ in range(len(across)):
+        next(steps)
+
+    def put_total(which, way, values):
+        slot = slots[which].at[way, ring.last]
+        slot[...] = values
+        place = slice(way * ring.half, (way + 1) * ring.half)
+        if which < 2:
+            for part in range(3):
+                store(slot.at[:, part * local : (part + 1) * local], qkv_out.at[which, part, place])
+        else:
+            store(slot, proj_out.at[which - 2, place])
+
+    ring.finish(None, put_total)
+    for _ in steps:
+        pass
+    for copy in [results[0]] + stored[2:]:
+        copy.wait()
+
+
+def attn_ring(
+    modulate, conditioning, own_cond, gain_sums, bias_sums, states, packed, attn, hidden, inputs, cots, weight,
+    ada_weight, order, tensor_size, row_share, collective_id,
+):
+    seqs, feat = inputs[0].shape[1], inputs[0].shape[3]
+    size, local, cols = len(order), attn[0].shape[1], ada_weight.shape[1]
+    rows = [array.shape[1] * array.shape[2] for array in inputs]
+    units = states[0]["up_bias"].shape[1]
+    block = 256
+    half = feat // (2 * size)
     vmem = pl.BlockSpec(memory_space=pltpu.VMEM)
     anywhere = pl.BlockSpec(memory_space=pl.ANY)
-    halves = [(left.shape[1] // (2 * size), right.shape[1]) for left, right, _ in pairs]
-    moved = sum(4 * 2 * (size - 1) * rows * cols for rows, cols in halves)
-    if rest:
-        whole = (halves[0][0], sum(cols for _, cols in halves))
-        shapes = [whole] * (2 * (rest + 1))
-    else:
-        shapes = [
-            (parts, 2 * rows, cols // parts) for (rows, cols), (_, _, parts) in zip(halves, pairs)
+
+    def wide(*dims):
+        return jax.ShapeDtypeStruct(dims, jnp.float32)
+
+    def low(*dims):
+        return pltpu.VMEM(dims, jnp.bfloat16)
+
+    large = [jax.ShapeDtypeStruct((2 * count, feat), jnp.bfloat16) for count in rows]
+    large += [wide(count, feat) for count in rows]
+    large += [wide(2, 3, 2 * half, local), wide(2, 2 * half, local), wide(2, cols, feat)]
+    small = [
+        wide(seqs, feat),
+        wide(2, cols),
+        wide(3, 2, local),
+        wide(2, units),
+        wide(2, 2, gain_sums.shape[2] // 2),
+        wide(2, feat),
+        wide(2, feat),
+    ]
+    halves = [(half, 3 * local)] * 2 + [(half, local)] * 2
+    doubled = [(2 * count, feat) for count in rows]
+    mod_refs, mod_sems = mod_scratch(size, tensor_size, seqs, feat, cols)
+    moved = 4 * 2 * (size - 1) * half * 8 * local
+    blocks = feat // block
+    sums = [
+        state[name] for state in states for name in ("up_bias", "proj_bias", "down_bias", "mod_sums")
+    ]
+    pairs = [
+        packed,
+        attn,
+        hidden,
+        [state["grad_branch"] for state in states],
+        [state["through"] for state in states],
+        [array.reshape(-1, feat) for array in inputs],
+        [array.reshape(-1, feat) for array in cots],
+    ]
+    return pl.pallas_call(
+        functools.partial(attn_ring_kernel, order, tensor_size, seqs, block, row_share),
+        out_shape=large + small,
+        in_specs=[vmem] * (5 + len(sums)) + [anywhere] * (2 * len(pairs) + 2),
+        out_specs=[anywhere] * len(large) + [vmem] * len(small),
+        scratch_shapes=ring_scratch(size, halves, doubled + doubled)
+        + [low(2 * count, 3 * local) for count in rows]
+        + [low(2 * count, local) for count in rows]
+        + [low(2 * count, feat) for count in rows]
+        + [low(count, feat) for count in rows]
+        + [low(2, 3, feat, local)]
+        + [pltpu.VMEM((count, feat), jnp.float32) for count in rows] * 3
+        + [
+            pltpu.VMEM((4, seqs, feat), jnp.float32),
+            pltpu.SemaphoreType.DMA((20,)),
+            pltpu.SemaphoreType.DMA((2, 2 * blocks + 2)),
+            pltpu.SemaphoreType.DMA((2, 2)),
+            pltpu.SemaphoreType.DMA((20,)),
+            pltpu.SemaphoreType.REGULAR,
         ]
-    results = pl.pallas_call(
-        functools.partial(grad_ring_kernel, order, count, swaps, rest),
-        out_shape=[jax.ShapeDtypeStruct(shape, jnp.float32) for shape in shapes]
-        + [jax.ShapeDtypeStruct(give.shape, give.dtype) for give in gives],
-        in_specs=[vmem] * (2 * count) + [anywhere] * swaps,
-        out_specs=[vmem] * len(shapes) + [anywhere] * swaps,
-        scratch_shapes=ring_scratch(size, halves, [left.shape for left, _, _ in pairs])
-        + [pltpu.SemaphoreType.DMA((2, swaps))],
+        + mod_refs
+        + [mod_sems],
         compiler_params=pltpu.CompilerParams(
-            collective_id=collective_id, has_side_effects=True, vmem_limit_bytes=58 << 20
+            collective_id=collective_id, has_side_effects=True, vmem_limit_bytes=67043328
         ),
         cost_estimate=pl.CostEstimate(flops=moved * 10000, bytes_accessed=moved, transcendentals=0),
-    )(*[left for left, _, _ in pairs], *[right for _, right, _ in pairs], *gives)
-    return results[: len(shapes)], results[len(shapes) :]
+        name="attn_ring",
+    )(
+        modulate,
+        conditioning,
+        own_cond,
+        gain_sums,
+        bias_sums,
+        *sums,
+        *[array for pair in pairs for array in pair],
+        weight,
+        ada_weight,
+    )
 
 
 def ring_rest(parts, order, rest):
@@ -1017,24 +1347,6 @@
         for way in range(2):
             totals[way] = totals[way] + parts[2 * (later + 1) + way]
     return totals
-
-
-def by_columns(totals, pairs):
-    blocks, start = [], 0
-    for _, right, split in pairs:
-        width = right.shape[1] // split
-        blocks.append(
-            jnp.stack(
-                [
-                    jnp.concatenate(
-                        [total[:, start + part * width : start + (part + 1) * width] for total in totals]
-                    )
-                    for part in range(split)
-                ]
-            )
-        )
-        start += right.shape[1]
-    return blocks
 
 
 def by_rows(totals):
@@ -1098,9 +1410,9 @@
     shapes = [array.shape for array in inputs]
     gain_pair = jnp.concatenate([norm_gain, norm_gain], axis=2)
 
-    hidden1, raw, stats1 = [], [], []
+    hidden1, raw = [], []
     for stream in range(2):
-        normed, inverse = layer_norm(inputs[stream].astype(jnp.float32))
+        normed, _ = layer_norm(inputs[stream].astype(jnp.float32))
         hidden = (normed * (1.0 + piece[stream][1]) + piece[stream][0]).astype(jnp.bfloat16)
         hidden = hidden.reshape(-1, feat)
         flat = [
@@ -1109,7 +1421,6 @@
         ]
         hidden1.append(hidden)
         raw.append([each.reshape(shapes[stream][:3] + (-1,)) for each in flat])
-        stats1.append((normed[0], inverse[0]))
     attn = attn_forward(gain_pair, raw[0], raw[1], reals[1])
     local = attn[0].shape[3]
 
@@ -1123,8 +1434,10 @@
             modulate,
             proj_bias,
             up_bias,
+            down_bias,
             up_weight,
             down_weight,
+            proj_weight,
             gives,
             order,
             rest,
@@ -1147,108 +1460,37 @@
     state[1] = mlp_stage(1, got, [branch_sums[0]], RESTS[0], 2)
     state[0] = mlp_stage(0, state[1]["gets"][0], [], RESTS[1], 3)
     mlp_rings = [state[stream]["ring"] for stream in range(2)]
-    hidden_sums = [state[stream]["hidden_sum"] + state[stream]["hidden_got"] for stream in range(2)]
-    mlp_sums = [state[stream]["mlp_sum"] + state[stream]["mlp_got"] for stream in range(2)]
-
-    grad_attn, proj_pairs, proj_sums, resid_grads, mod_grads = ([None, None] for _ in range(5))
-    outputs = [None, None]
-    for stream in (1, 0):
-        branch, normed, inverse = (state[stream][key] for key in ("branch", "normed", "inverse"))
-        grad_out = cotangents[stream][0].astype(jnp.float32)
-        grad_hidden = hidden_sums[stream].reshape(normed.shape)
-        through = norm_back(grad_hidden * (1.0 + piece[stream][4]), normed, inverse)
-        grad_resid = grad_out + through
-        grad_branch = share(grad_resid, tensor_size) * piece[stream][2]
-        branch_low = grad_branch.astype(jnp.bfloat16).reshape(-1, feat)
-        grad_attn[stream] = (
-            dot_right_t(branch_low, proj_weight[stream])
-            .astype(jnp.bfloat16)
-            .reshape(attn[stream].shape)
-        )
-        proj_pairs[stream] = (branch_low, attn[stream].reshape(-1, local), 1)
-        proj_sums[stream] = jnp.sum(grad_resid * piece[stream][2], axis=(0, 1))
-        resid_grads[stream] = through
-        mod_grads[stream] = [
-            None,
-            None,
-            jnp.sum(grad_resid * branch, axis=1),
-            jnp.sum(grad_hidden, axis=1),
-            jnp.sum(grad_hidden * normed, axis=1),
-            None,
-        ]
+
+    grad_attn = [state[stream]["grad_attn"].reshape(attn[stream].shape) for stream in range(2)]
     grad_packed = attn_backward(gain_pair, raw[0], raw[1], grad_attn[0], grad_attn[1], reals[1])
-    qkv_bias_sums = jnp.sum(grad_packed[2], axis=0)
-    gain_sums = jnp.sum(grad_packed[3], axis=0)
-    head_dim = norm_gain.shape[2]
-    gain_sums = gain_sums[:, :head_dim] + gain_sums[:, head_dim:]
-    qkv_pairs, first_sums = [None, None], [None, None]
-    for stream in (1, 0):
-        packed_low = grad_packed[stream].reshape(-1, 3 * local)
-        half = packed_low.shape[0] // 2
-
-        def through_weights(rows):
-            return sum(
-                dot_right_t(
-                    packed_low[rows, part * local : (part + 1) * local], qkv_weight[stream, :, part]
-                )
-                for part in range(3)
-            )
-
-        first_sums[stream] = core_sum(
-            through_weights(slice(None, half)),
-            through_weights(slice(half, None)),
-            tensor_size,
-        )
-        qkv_pairs[stream] = (hidden1[stream], packed_low, 3)
-    pairs = qkv_pairs + proj_pairs
-    rings, swapped = grad_ring(pairs, first_sums, order, RESTS[2], 4)
-    if RESTS[2]:
-        rings = by_columns(ring_rest(rings, order, RESTS[2]), pairs)
-    qkv_rings, proj_rings = rings[:2], rings[2:]
-    first_sums = [give + get for give, get in zip(first_sums, swapped)]
-
-    grad_inputs = [None, None]
-    for stream in (1, 0):
-        branch = state[stream]["branch"]
-        grad_out = cotangents[stream][0].astype(jnp.float32)
-        mlp_out = mlp_sums[stream].reshape(branch.shape) + down_bias[stream]
-        added = piece[stream][2] * branch + piece[stream][5] * mlp_out
-        outputs[stream] = join_rows(
-            inputs[stream].astype(jnp.float32) + share(added, tensor_size), reals[stream]
-        )
-        mod_grads[stream][5] = jnp.sum(grad_out * mlp_out, axis=1)
-        normed, inverse = stats1[stream]
-        grad_hidden = first_sums[stream].reshape(normed.shape)
-        added = resid_grads[stream] + norm_back(
-            grad_hidden * (1.0 + piece[stream][1]), normed, inverse
-        )
-        grad_inputs[stream] = join_rows(
-            cotangents[stream].astype(jnp.float32) + share(added, tensor_size), reals[stream]
-        )
-        mod_grads[stream][0] = jnp.sum(grad_hidden, axis=1)
-        mod_grads[stream][1] = jnp.sum(grad_hidden * normed, axis=1)
-
-    row_share = 2.0 / tensor_size
-    sums = mod_backward(
-        jnp.stack(mod_grads[0] + mod_grads[1]),
-        conditioning,
-        ada_weight,
-        [qkv_bias_sums, jnp.concatenate([state[0]["up_bias"], state[1]["up_bias"]])],
-        [
-            gain_sums,
-            jnp.stack(proj_sums) * row_share,
-            jnp.concatenate([state[0]["down_bias"], state[1]["down_bias"]]) * row_share,
-        ],
-        data_size,
-        tensor_size,
-    )
-    grad_ada_weight, grad_ada_bias, silu_rows, qkv_bias_sums, up_bias_sums = sums[:5]
-    gain_sums, proj_sums, down_sums = sums[5:]
     own_cond = lax.dynamic_slice_in_dim(
         conditioning, lax.axis_index("dp") * seqs, seqs, axis=0
     ).astype(jnp.float32)
-    own_sig = jax.nn.sigmoid(own_cond)
-    grad_conditioning = silu_rows * own_sig * (1.0 + own_cond * (1.0 - own_sig))
+    made = attn_ring(
+        modulate,
+        conditioning,
+        own_cond,
+        grad_packed[3],
+        grad_packed[2],
+        state,
+        [grad_packed[stream].reshape(-1, 3 * local) for stream in range(2)],
+        [attn[stream].reshape(-1, local) for stream in range(2)],
+        hidden1,
+        inputs,
+        cotangents,
+        qkv_weight.transpose(0, 2, 1, 3),
+        ada_weight,
+        order,
+        tensor_size,
+        2.0 / tensor_size,
+        4,
+    )
+    grad_qkv, grad_proj, grad_ada_weight, grad_conditioning, grad_ada_bias = made[4:9]
+    qkv_bias_sums, up_bias_sums, gain_sums, proj_sums, down_sums = made[9:]
+    outputs = [
+        join_rows(state[stream]["out"].reshape(shapes[stream]), reals[stream]) for stream in range(2)
+    ]
+    grad_inputs = [join_rows(made[stream].reshape(shapes[stream]), reals[stream]) for stream in range(2)]
     down_rings, up_rings = ([mlp_rings[0][index], mlp_rings[1][index]] for index in range(2))
     return (
         outputs[0],
@@ -1258,10 +1500,10 @@
         grad_conditioning,
         grad_ada_weight.transpose(0, 2, 1),
         grad_ada_bias,
-        jnp.stack(qkv_rings).transpose(0, 2, 1, 3),
-        qkv_bias_sums.reshape(2, 3, -1),
-        gain_sums.reshape(norm_gain.shape),
-        jnp.concatenate(proj_rings).transpose(0, 2, 1),
+        grad_qkv.transpose(0, 2, 1, 3),
+        qkv_bias_sums.transpose(1, 0, 2),
+        gain_sums,
+        grad_proj.transpose(0, 2, 1),
         proj_sums,
         jnp.concatenate(up_rings),
         up_bias_sums,

time: 798 us -> 731 us (0.916)
  Pallas kernels: 548 us -> 617 us
  other arithmetic: 102 us -> 35.4 us
  waiting for transfers between devices: 55 us -> 18.9 us
  matrix products: 38.3 us -> 20 us
    pallas_call x2 -> x1, Pallas kernels: 172 us -> 216 us  [attn_ring(): pl.pallas_call(functools.partial(attn_ring_kernel, order, tensor_size, se...]
    reduce_sum x12 -> x0, other arithmetic: 31.6 us -> none  [the longest x4 10.5 us: norm_back(): jnp.mean(grad_normed, axis=-1, keepdims=True)]
    ppermute x10 -> x4, waiting for transfers between devices: 29.7 us -> 0.01 us  [ring_rest(): totals[way] = lax.ppermute(totals[way], 'dp', ways[way])]
    pallas_call x2, Pallas kernels: 329 us -> 354 us  [mlp_ring(): pl.pallas_call(functools.partial(mlp_ring_kernel, order, stream, seqs, bl...]
    dot_general x14 -> x0, matrix products: 20.5 us -> none  [dot_right_t(): lax.dot_general(first_op, second_op, (((1,), (1,)), ((), ())), preferred_...]
    convert_element_type x7 -> x1, other arithmetic: 13.2 us -> 0.62 us  [on_device(): own_cond = lax.dynamic_slice_in_dim(conditioning, lax.axis_index('dp') *...]
    add x8 -> x1, other arithmetic: 8.4 us -> 0.02 us  [on_device(): 1.0 + piece[stream][1]]
    unnamed x276 -> x116, local copies, waits for them, and re-layouts: 26.7 us -> 20 us
  transfers between devices with their start and end apart: 21 -> 7, of which waited for: 5 -> 1; matrix products, arithmetic and copies ran while one was open for 13% -> 4% of each run, Pallas kernels for 27% -> 33%
where the time goes in v4:
time: 731 us; the launch traced here: 723 us
  Pallas kernels  617 us (84%)
  other arithmetic  35.4 us (5%)
  local copies, waits for them, and re-layouts  24.1 us (3%)
  matrix products  20 us (3%)
  waiting for transfers between devices  18.9 us (3%)
    pallas_call x2, Pallas kernels, mlp_ring(): pl.pallas_call(functools.partial(mlp_ring_kernel, order, stream, seqs, bl...  354 us
    pallas_call x1, Pallas kernels, attn_ring(): pl.pallas_call(functools.partial(attn_ring_kernel, order, tensor_size, se...  216 us
    pallas_call x1, Pallas kernels, attn_backward(): pl.pallas_call(functools.partial(attn_backward_kernel, real), grid=(seqs,...  22.2 us
    dot_general x10, matrix products, dot_plain(): return jnp.dot(first_op, second_op, preferred_element_type=jnp.float32)  20 us
    unnamed x116, local copies, waits for them, and re-layouts  20 us
    ppermute x1, waiting for transfers between devices, on_device(): got = lax.ppermute(branch_sums[1], 'tensor', swap_pairs(tensor_size, 2))  18.9 us
    pallas_call x1, Pallas kernels, mod_forward(): pl.pallas_call(functools.partial(mod_forward_kernel, data_size, tensor_si...  15 us
  transfers between devices with their start and end apart: 7, of which 1 were waited for; matrix products, arithmetic and copies ran while one was open for 4% of the time, Pallas kernels for 33%

profile of v4, /device:TPU:0, one launch (start us, length us, event | category | flops | bytes accessed | tf_op | source)
XLA Modules:
  0.0 722.6 jit_solution(9395107240696620168)
XLA Ops:
  2.7 1.9 select_bitcast_fusion.5
  6.3 15.0 %mod_forward.1.refs_0_ = f32[12,3,1536]{2,1,0:T(4,128)S(1)} custom-call(bf16[24,1536]{1,0:T(8,128)(2,1)S(1)} %copy-done.4, bf16[2,288,1536]{2,1,0:T(8,128)(2,1)S(1)} %bitcast.131, bf16[2,288]{1,0:T(2,128)(2,1)S(1)} %copy-done.6), custom_call_target="tpu_custom_call" | custom-call | tf_op jit(solution)/shard_map/mod_forward/pallas_call | solution.py:351
  22.9 2.8 convolution_add_fusion.6
  29.3 1.7 select_bitcast_fusion.1
  32.1 1.6 fusion.5
  33.8 2.4 convolution_add_fusion.2
  39.1 9.7 %attn_forward.1 = (bf16[2,3,128,384]{3,2,1,0:T(8,128)(2,1)S(1)}, bf16[2,3,80,384]{3,2,1,0:T(8,128)(2,1)S(1)}) custom-call(f32[2,2,128]{2,1,0:T(2,128)S(1)} %pad_maximum_fusion.9.gain_ref, f32[2,3,128,384]{3,2,1,0:T(8,128)S(1)} %bitcast.134, f32[2,3,128,384]{3,2,1,0:T(8,128)S(1)} %bitcast.136, f32[2,3,128,384]{3,2,1,0:T(8,128)} %bitcast.176, ...), custom_call_target="tpu_custom_call" | custom-call | flops 797442048 | bytes 6709248 | tf_op jit(solution)/shard_map/attn_forward/pallas_call | solution.py:212
  49.7 1.7 fusion.14
  51.8 2.2 fusion.17
  55.5 2.5 convolution_add_fusion.1.refs_4_
  60.5 2.2 fusion.13.refs_18_
  62.9 3.8 fusion.6.refs_17_
  67.3 1.6 pad_maximum_fusion.1
  69.8 3.9 convolution_add_fusion.refs_11_.refs_4_
  73.7 18.9 %collective-permute-done.2.refs_5_ = f32[240,1536]{1,0:T(8,128)S(1)} collective-permute-done((f32[240,1536]{1,0:T(8,128)S(1)}, f32[240,1536]{1,0:T(8,128)S(1)}, u32[]{:S(2)}, u32[]{:S(2)}) %collective-permute-start.2) | collective-permute-done | bytes 1474592 | tf_op jit(solution)/shard_map/ppermute | solution.py:1459
  93.8 174.4 %mlp_ring.2 = (f32[192,1536]{1,0:T(8,128)}, f32[192,1536]{1,0:T(8,128)}, f32[192,1536]{1,0:T(8,128)}, f32[192,1536]{1,0:T(8,128)}, f32[384,1536]{1,0:T(8,128)}, ...) custom-call(f32[12,3,1536]{2,1,0:T(4,128)} %copy-done.2, ...), custom_call_target="tpu_custom_call" | custom-call | flops 165150720000 | bytes 16515072 | tf_op jit(solution)/shard_map/mlp_ring/pallas_call | solution.py:973
  268.2 179.5 %mlp_ring.3 = (f32[192,1536]{1,0:T(8,128)}, f32[192,1536]{1,0:T(8,128)}, f32[192,1536]{1,0:T(8,128)}, f32[192,1536]{1,0:T(8,128)}, f32[1,1536]{1,0:T(1,128)}, /*...) custom-call(f32[12,3,1536]{2,1,0:T(4,128)} %copy-done.2, ...), custom_call_target="tpu_custom_call" | custom-call | flops 165150720000 | bytes 16515072 | tf_op jit(solution)/shard_map/mlp_ring/pallas_call | solution.py:973
  447.7 1.7 collective-permute-start.3
  449.8 1.7 collective-permute-start.5
  451.8 22.2 %attn_backward.1 = (bf16[2,3,128,1152]{3,2,1,0:T(8,128)(2,1)}, bf16[2,3,80,1152]{3,2,1,0:T(8,128)(2,1)}, f32[3,2,1152]{2,1,0:T(2,128)}, f32[3,4,128]{2,1,0:T(4,128)}) custom-call(f32[2,2,128]{2,1,0:T(2,128)} %copy-done.5, f32[2,3,128,384]{3,2,1,0:T(8,128)} %bitcast.135, f32[2,3,128,384]{3,2,1,0:T(8,128)} %bitcast.137, f32[2,3,128,384]{3,2,1,0:T(8,128)} %bitcast.177, ...), custom_call_target="tpu_custom_call" | custom-call | flops 1993605120 | bytes 9584640 | tf_op jit(solution)/shard_map/attn_backward/pallas_call | solution.py:237
  474.1 216.0 %attn_ring.1 = (bf16[768,1536]{1,0:T(8,128)(2,1)}, bf16[480,1536]{1,0:T(8,128)(2,1)}, f32[384,1536]{1,0:T(8,128)}, f32[240,1536]{1,0:T(8,128)}, f32[2,3,192,384]...) custom-call(f32[12,3,1536]{2,1,0:T(4,128)} %copy-done.2, ...), custom_call_target="tpu_custom_call" | custom-call | flops 165150720000 | bytes 16515072 | tf_op jit(solution)/shard_map/attn_ring/pallas_call | solution.py:1299
  690.0 1.6 broadcast_select_fusion.5
  710.0 1.6 maximum_bitcast_fusion
  714.6 1.8 copy.43
  (173 shorter events, 48.7 us)
Async XLA Ops:
  4.6 16.9 %copy-start.12 = (bf16[1,3,80,1536]{3,2,1,0:T(8,128)(2,1)}, bf16[1,3,80,1536]{3,2,1,0:T(8,128)(2,1)S(1)}, u32[]{:S(2)}) copy-start(bf16[1,3,80,1536]{3,2,1,0:T(8,128)(2,1)S(1)} %get-tuple-element.141) | copy-start | bytes 2211844
  5.4 16.0 %copy-start.40 = (bf16[2,3,384]{2,0,1:T(2,128)(2,1)S(1)}, bf16[2,3,384]{2,0,1:T(2,128)(2,1)}, u32[]{:S(2)}) copy-start(bf16[2,3,384]{2,0,1:T(2,128)(2,1)} %param.22) | copy-start | bytes 13828
  21.5 4.2 copy-start.51
  25.6 13.5 %copy-start.9 = (f32[480,384]{1,0:T(8,128)}, f32[480,384]{1,0:T(8,128)S(1)}, u32[]{:S(2)}) copy-start(f32[480,384]{1,0:T(8,128)S(1)} %convolution_add_fusion.6) | copy-start | bytes 2211844
  26.6 12.5 %copy-start.10 = (f32[480,384]{1,0:T(8,128)}, f32[480,384]{1,0:T(8,128)S(1)}, u32[]{:S(2)}) copy-start(f32[480,384]{1,0:T(8,128)S(1)} %convolution_add_fusion.5) | copy-start | bytes 2211844
  29.3 9.9 %copy-start.11 = (f32[480,384]{1,0:T(8,128)}, f32[480,384]{1,0:T(8,128)S(1)}, u32[]{:S(2)}) copy-start(f32[480,384]{1,0:T(8,128)S(1)} %convolution_add_fusion.7) | copy-start | bytes 2211844
  39.0 9.9 %copy-start.8 = (f32[768,384]{1,0:T(8,128)}, f32[768,384]{1,0:T(8,128)S(1)}, u32[]{:S(2)}) copy-start(f32[768,384]{1,0:T(8,128)S(1)} %convolution_add_fusion.3) | copy-start | bytes 3538948
  39.1 9.8 %copy-start.5 = (f32[2,2,128]{2,1,0:T(2,128)}, f32[2,2,128]{2,1,0:T(2,128)S(1)}, u32[]{:S(2)}) copy-start(f32[2,2,128]{2,1,0:T(2,128)S(1)} %pad_maximum_fusion.9.gain_ref) | copy-start | bytes 6148
  39.1 10.6 %copy-start.14 = (bf16[2,384,1536]{2,1,0:T(8,128)(2,1)S(1)}, bf16[2,384,1536]{2,1,0:T(8,128)(2,1)}, u32[]{:S(2)}) copy-start(bf16[2,384,1536]{2,1,0:T(8,128)(2,1)} %refs_10_.3) | copy-start | bytes 7077892
  51.4 4.1 collective-permute-start.1
  54.0 14.9 %collective-permute-start = (f32[384,1536]{1,0:T(8,128)}, f32[384,1536]{1,0:T(8,128)}, u32[]{:S(2)}, u32[]{:S(2)}) collective-permute-start(f32[384,1536]{1,0:T(8,128)} %fusion.17), channel_id=1, source_target_pairs={{0,1},{1,0},{2,3},{3,2},{4,5},{5,4},{6,7},{7,6},{8,9},{9,8},{10,11... | collective-permute-start | bytes 7077896 | tf_op jit(solution)/shard_map/ppermute | solution.py:491
  55.5 3.6 copy-start.13
  55.5 3.6 copy-start.21
  55.5 3.5 copy-start.22
  58.0 34.6 %collective-permute-start.2 = (f32[240,1536]{1,0:T(8,128)S(1)}, f32[240,1536]{1,0:T(8,128)S(1)}, u32[]{:S(2)}, u32[]{:S(2)}) collective-permute-start(f32[240,1536]{1,0:T(8,128)S(1)} %convolution_add_fusion.1.refs_4_), channel_id=1, source_target_pairs={{0,2},{1,3},{2,0},{3,1},{4,6},{5,7},{6,4},{7,5},{8,10},{9,11},{10,... | collective-permute-start | bytes 4423688 | tf_op jit(solution)/shard_map/ppermute | solution.py:1459
  62.9 3.8 copy-start.16
  62.9 4.4 copy-start.18
  62.9 4.4 copy-start.19
  447.7 253.3 %collective-permute-start.3 = (f32[192,1536]{1,0:T(8,128)}, f32[192,1536]{1,0:T(8,128)}, u32[]{:S(2)}, u32[]{:S(2)}) collective-permute-start(f32[192,1536]{1,0:T(8,128)} %get-tuple-element.92), channel_id=1, source_target_pairs={{0,4},{4,12},{12,20},{20,28},{28,24},{24,16},{16,8},{8,0},{1,5},{5... | collective-permute-start | bytes 3538952 | tf_op jit(solution)/shard_map/ppermute | solution.py:1346
  449.5 253.2 %collective-permute-start.4 = (f32[192,1536]{1,0:T(8,128)}, f32[192,1536]{1,0:T(8,128)}, u32[]{:S(2)}, u32[]{:S(2)}) collective-permute-start(f32[192,1536]{1,0:T(8,128)} %get-tuple-element.94), channel_id=1, source_target_pairs={{4,0},{12,4},{20,12},{28,20},{24,28},{16,24},{8,16},{0,8},{5,1},{1... | collective-permute-start | bytes 3538952 | tf_op jit(solution)/shard_map/ppermute | solution.py:1346
  449.8 255.6 %collective-permute-start.5 = (f32[192,1536]{1,0:T(8,128)}, f32[192,1536]{1,0:T(8,128)}, u32[]{:S(2)}, u32[]{:S(2)}) collective-permute-start(f32[192,1536]{1,0:T(8,128)} %get-tuple-element.96), channel_id=1, source_target_pairs={{0,4},{4,12},{12,20},{20,28},{28,24},{24,16},{16,8},{8,0},{1,5},{5... | collective-permute-start | bytes 3538952 | tf_op jit(solution)/shard_map/ppermute | solution.py:1346
  451.5 255.6 %collective-permute-start.6 = (f32[192,1536]{1,0:T(8,128)}, f32[192,1536]{1,0:T(8,128)}, u32[]{:S(2)}, u32[]{:S(2)}) collective-permute-start(f32[192,1536]{1,0:T(8,128)} %get-tuple-element.98), channel_id=1, source_target_pairs={{4,0},{12,4},{20,12},{28,20},{24,28},{16,24},{8,16},{0,8},{5,1},{1... | collective-permute-start | bytes 3538952 | tf_op jit(solution)/shard_map/ppermute | solution.py:1346
  717.3 3.8 copy-start.42
  717.4 4.4 copy-start.41
  (36 other events, 68.0 us)

commit v5 on v4

--- a/solution.py
+++ b/solution.py
@@ -30,12 +30,6 @@
     return lax.dot_general(
         first_op, second_op, (((0,), (0,)), ((), ())), preferred_element_type=jnp.float32
     )
-
-
-def layer_norm(values):
-    center = values - jnp.mean(values, axis=-1, keepdims=True)
-    inverse = lax.rsqrt(jnp.mean(center * center, axis=-1, keepdims=True) + epsilon)
-    return (center * inverse, inverse)
 
 
 def norm_back(grad_normed, normed, inverse):
@@ -105,8 +99,7 @@
     return weights * (1.0 / jnp.sum(weights, axis=-1, keepdims=True))
 
 
-def attn_forward_kernel(real, gain_ref, *refs):
-    raw_refs, (out_img_ref, out_txt_ref) = (refs[:3], refs[3:6]), refs[6:]
+def attn_forward(real, gain_ref, raw_refs, out_img_ref, out_txt_ref):
     img, txt = out_img_ref.shape[2], out_txt_ref.shape[2]
     local = out_img_ref.shape[3]
     pair = gain_ref.shape[2]
@@ -203,26 +196,6 @@
 
 def whole_of(array):
     return pl.BlockSpec(array.shape, lambda seq: (0,) * array.ndim)
-
-
-def attn_forward(gain_pair, raw_img, raw_txt, real):
-    seqs, local = raw_img[0].shape[1], raw_img[0].shape[3]
-    outs = [jax.ShapeDtypeStruct(raw[0].shape, jnp.bfloat16) for raw in (raw_img, raw_txt)]
-    rows = 2 * (raw_img[0].shape[2] + raw_txt[0].shape[2])
-    return pl.pallas_call(
-        functools.partial(attn_forward_kernel, real),
-        grid=(seqs,),
-        out_shape=outs,
-        in_specs=[whole_of(gain_pair)] + [block_of(raw) for raw in raw_img + raw_txt],
-        out_specs=[block_of(out) for out in outs],
-        compiler_params=pltpu.CompilerParams(vmem_limit_bytes=48 << 20),
-        cost_estimate=pl.CostEstimate(
-            flops=seqs * rows * rows * local * 4,
-            bytes_accessed=seqs * rows * local * 14,
-            transcendentals=seqs * rows * rows * (local // 64),
-        ),
-        name="attn_forward",
-    )(gain_pair, *raw_img, *raw_txt)
 
 
 def attn_backward(gain_pair, raw_img, raw_txt, grad_img, grad_txt, real):
@@ -483,14 +456,6 @@
     return center * inverse, inverse
 
 
-def swap_pairs(size, distance):
-    return [(index, index ^ distance) for index in range(size)]
-
-
-def core_sum(own_part, other_part, tensor_size):
-    return own_part + lax.ppermute(other_part, "tensor", swap_pairs(tensor_size, 1))
-
-
 def ring_order(mesh):
     size = mesh.shape["dp"]
     fallback = list(range(0, size, 2)) + list(range(1, size, 2))[::-1]
@@ -559,6 +524,27 @@
     return pl.ds(pl.multiple_of(rows.start + by, ROW_TILE), rows.size)
 
 
+def half_of(array, half, seq, by_seq):
+    return array.at[seq, half] if by_seq else array.at[half, seq]
+
+
+def move_halves(move, array, rows_ref, seqs, by_seq, to_array=False, halves=2):
+    core = lax.axis_index("tensor") % 2
+    length = rows_ref.shape[0] // (halves * seqs)
+    copies = []
+    for half, position in enumerate((core, 1 - core)[:halves]):
+        for seq in range(seqs):
+            start = (half * seqs + seq) * length
+            ends = (half_of(array, position, seq, by_seq), rows_ref.at[start : start + length])
+            copies.append(move(*(ends[::-1] if to_array else ends)))
+    return copies
+
+
+def wait_all(copies):
+    for copy in copies:
+        copy.wait()
+
+
 class Ring:
     def __init__(self, order, rest, lefts, rights, slots, terms, turned, sems):
         self.order, self.size, self.rest = order, len(order), rest
@@ -665,7 +651,198 @@
     )
 
 
-def mlp_ring_kernel(order, stream, seqs, block, swaps, rest, *refs):
+def front_kernel(seqs, real, block, by_seqs, *refs):
+    take = taker(refs)
+    mod_ref, gain_ref, bias_ref = take(3)
+    input_hbm = take(2)
+    weight_hbm, proj_hbm = take(2)
+    hidden_hbm, raw_hbm, attn_hbm, sum_hbm = take(2), (take(3), take(3)), take(2), take(2)
+    (got_hbm,) = take(1)
+    inputs, hidden, raw, attn = take(2), take(2), (take(3), take(3)), take(2)
+    weight_ref, proj_ref = take(2)
+    outgoing, incoming, own = take(2), take(2), take(2)
+    load_sems, core_sems, swap_sems, out_sems = take(4)
+    feat = hidden[0].shape[1]
+    lengths = [ref.shape[2] for ref in attn]
+    partner = (lax.axis_index("dp"), xor_index(lax.axis_index("tensor"), 1))
+    facing = (lax.axis_index("dp"), xor_index(lax.axis_index("tensor"), 2))
+    started = []
+
+    def load(source, target):
+        copy = pltpu.make_async_copy(source, target, load_sems.at[len(started)])
+        copy.start()
+        started.append(copy)
+        return copy
+
+    input_loads = [
+        move_halves(load, input_hbm[stream], inputs[stream], seqs, by_seqs[stream]) for stream in range(2)
+    ]
+    weight_loads = [load(weight_hbm, weight_ref), load(proj_hbm, proj_ref)]
+    greet((partner, facing))
+    for copies in input_loads:
+        wait_all(copies)
+
+    def core_copy(stream, seq):
+        span = pl.ds(pl.multiple_of(seq * lengths[stream], ROW_TILE), lengths[stream])
+        return pltpu.make_async_remote_copy(
+            src_ref=outgoing[stream].at[span],
+            dst_ref=incoming[stream].at[span],
+            send_sem=core_sems.at[0, stream, seq],
+            recv_sem=core_sems.at[1, stream, seq],
+            device_id=partner,
+            device_id_type=pl.DeviceIdType.MESH,
+        )
+
+    def chip_copy(seq):
+        span = pl.ds(pl.multiple_of(seq * lengths[1], ROW_TILE), lengths[1])
+        return pltpu.make_async_remote_copy(
+            src_ref=own[1].at[span],
+            dst_ref=got_hbm.at[span],
+            send_sem=swap_sems.at[0, seq],
+            recv_sem=swap_sems.at[1, seq],
+            device_id=facing,
+            device_id_type=pl.DeviceIdType.MESH,
+        )
+
+    def normalize(seq):
+        for stream in range(2):
+            shift = mod_ref[stream * 6, pl.ds(seq, 1), :]
+            scale = 1.0 + mod_ref[stream * 6 + 1, pl.ds(seq, 1), :]
+
+            def first_norm(at):
+                normed, _ = norm_of(inputs[stream][at].astype(jnp.float32))
+                hidden[stream][at] = (normed * scale + shift).astype(jnp.bfloat16)
+                return ()
+
+            for half in range(2):
+                over_rows((half * seqs + seq) * lengths[stream], lengths[stream], feat, 0, first_norm)
+
+    def attend(seq):
+        for stream in range(2):
+            length = lengths[stream]
+            left = jnp.concatenate(
+                [
+                    hidden[stream][pl.ds(pl.multiple_of((half * seqs + seq) * length, ROW_TILE), length), :]
+                    for half in range(2)
+                ],
+                axis=0,
+            )
+            for part in range(3):
+                values = dot_plain(left, weight_ref[stream, part]) + bias_ref[stream, part : part + 1].astype(
+                    jnp.float32
+                )
+                raw[stream][part][0, seq] = values[:length]
+                raw[stream][part][1, seq] = values[length:]
+        one = pl.ds(seq, 1)
+        attn_forward(
+            real,
+            gain_ref,
+            [[ref.at[:, one] for ref in raw[stream]] for stream in range(2)],
+            attn[0].at[:, one],
+            attn[1].at[:, one],
+        )
+        for stream in (1, 0):
+            length = lengths[stream]
+            span = pl.ds(pl.multiple_of(seq * length, ROW_TILE), length)
+            left = jnp.concatenate([attn[stream][0, seq], attn[stream][1, seq]], axis=0)
+            for start in range(0, feat, block):
+                cols = slice(start, start + block)
+                both = dot_plain(left, proj_ref[stream, :, cols])
+                own[stream][span, cols] = both[:length]
+                outgoing[stream][span, cols] = both[length:]
+            core_copy(stream, seq).start()
+
+    def pass_on(seq):
+        for stream in (1, 0):
+            core_copy(stream, seq).wait()
+
+            def add(at):
+                own[stream][at] = own[stream][at] + incoming[stream][at]
+                return ()
+
+            over_rows(seq * lengths[stream], lengths[stream], feat, 0, add)
+            if stream == 1:
+                chip_copy(seq).start()
+
+    def one_sequence(seq, carry):
+        normalize(seq)
+
+        @pl.when(seq == 0)
+        def _():
+            wait_all(weight_loads)
+
+        @pl.when(seq > 0)
+        def _():
+            pass_on(seq - 1)
+
+        attend(seq)
+        return carry
+
+    lax.fori_loop(0, seqs, one_sequence, 0)
+    stores = []
+    for source, target in zip(
+        list(hidden) + list(raw[0]) + list(raw[1]) + list(attn),
+        list(hidden_hbm) + list(raw_hbm[0]) + list(raw_hbm[1]) + list(attn_hbm),
+    ):
+        stores.append(pltpu.make_async_copy(source, target, out_sems.at[len(stores)]))
+        stores[-1].start()
+    pass_on(seqs - 1)
+    for source, target in zip(own, sum_hbm):
+        stores.append(pltpu.make_async_copy(source, target, out_sems.at[len(stores)]))
+        stores[-1].start()
+    for copy in stores:
+        copy.wait()
+
+    def arrive(seq, carry):
+        chip_copy(seq).wait()
+        return carry
+
+    lax.fori_loop(0, seqs, arrive, 0)
+
+
+def front(modulate, gain_pair, inputs, by_seqs, weight, bias, proj_weight, real, collective_id):
+    seqs, feat = modulate.shape[1:]
+    local = weight.shape[3]
+    lengths = [array.shape[2] for array in inputs]
+    rows = [seqs * length for length in lengths]
+    vmem = pl.BlockSpec(memory_space=pltpu.VMEM)
+    anywhere = pl.BlockSpec(memory_space=pl.ANY)
+    shapes = [((2 * count, feat), jnp.bfloat16) for count in rows]
+    shapes += [((2, seqs, length, local), jnp.float32) for length in lengths for _ in range(3)]
+    shapes += [((2, seqs, length, local), jnp.bfloat16) for length in lengths]
+    sums = [((count, feat), jnp.float32) for count in rows]
+    outs = shapes + sums + sums[1:]
+    results = pl.pallas_call(
+        functools.partial(front_kernel, seqs, real, 512, by_seqs),
+        out_shape=[jax.ShapeDtypeStruct(*out) for out in outs],
+        in_specs=[vmem] * 3 + [anywhere] * 4,
+        out_specs=[anywhere] * len(outs),
+        scratch_shapes=[pltpu.VMEM((2 * count, feat), jnp.bfloat16) for count in rows]
+        + [pltpu.VMEM(*shape) for shape in shapes]
+        + [pltpu.VMEM(weight.shape, jnp.bfloat16), pltpu.VMEM(proj_weight.shape, jnp.bfloat16)]
+        + [pltpu.VMEM(*each) for each in sums] * 3
+        + [
+            pltpu.SemaphoreType.DMA((2 + 4 * seqs,)),
+            pltpu.SemaphoreType.DMA((2, 2, seqs)),
+            pltpu.SemaphoreType.DMA((2, seqs)),
+            pltpu.SemaphoreType.DMA((len(shapes) + 2,)),
+        ],
+        compiler_params=pltpu.CompilerParams(
+            collective_id=collective_id, has_side_effects=True, vmem_limit_bytes=60 << 20
+        ),
+        name="front",
+    )(
+        modulate,
+        gain_pair,
+        bias,
+        *inputs,
+        weight,
+        proj_weight,
+    )
+    return results[:2], (results[2:5], results[5:8]), results[8:10], results[10:12], results[12]
+
+
+def mlp_ring_kernel(order, stream, seqs, block, swaps, rest, direct, *refs):
     take = taker(refs)
     mod_ref, proj_bias_ref, up_bias_ref, down_bias_ref = take(4)
     mine_hbm, got_hbm, input_hbm, cot_hbm, up_hbm, down_hbm, proj_hbm = take(7)
@@ -680,7 +857,7 @@
     up_ref, down_ref, input_ref, hidden_ref, active_ref, grad_up_ref, grad_mlp_ref = take(7)
     proj_ref, grad_attn_ref, inverse_ref = take(3)
     mine_ref, got_ref, branch_ref, normed_ref, normed_in, spare = take(6)
-    load_sems, core_sems, swap_sems, out_sems, again_sems, ready_sem = take(6)
+    load_sems, core_sems, swap_sems, out_sems, ready_sem = take(5)
     rows, feat = mine_ref.shape
     units = active_ref.shape[1]
     length = rows // seqs
@@ -690,18 +867,22 @@
     partner = (lax.axis_index("dp"), xor_index(lax.axis_index("tensor"), 1))
     facing = (lax.axis_index("dp"), xor_index(lax.axis_index("tensor"), 2))
 
-    loads = []
-    for source, target in (
-        (mine_hbm, mine_ref),
-        (got_hbm, got_ref),
-        (input_hbm, input_ref),
-        (cot_hbm, grad_mlp_ref),
-        (up_hbm.at[stream], up_ref),
-        (down_hbm.at[stream], down_ref),
-        (proj_hbm.at[stream], proj_ref),
-    ):
-        loads.append(pltpu.make_async_copy(source, target, load_sems.at[len(loads)]))
-        loads[-1].start()
+    started = []
+
+    def load(source, target):
+        copy = pltpu.make_async_copy(source, target, load_sems.at[len(started)])
+        copy.start()
+        started.append(copy)
+        return copy
+
+    first_loads = [load(mine_hbm, mine_ref), load(got_hbm, got_ref)]
+    first_loads += move_halves(load, input_hbm, input_ref, seqs, direct)
+    cot_loads = move_halves(load, cot_hbm, grad_mlp_ref, seqs, direct)
+    weight_loads = [
+        load(up_hbm.at[stream], up_ref),
+        load(down_hbm.at[stream], down_ref),
+        load(proj_hbm.at[stream], proj_ref),
+    ]
     greet(ring.targets + (facing, partner))
     swapped = [
         remote(gives[index], gets[index], swap_sems, index, facing) for index in range(swaps)
@@ -720,19 +901,10 @@
         stored.append(copy)
         return copy
 
-    loaded = []
-
-    def load_again(source, target):
-        copy = pltpu.make_async_copy(source, target, again_sems.at[len(loaded)])
-        copy.start()
-        loaded.append(copy)
-        return copy
-
     def row_sum(values):
         return jnp.sum(values, axis=0, keepdims=True)
 
-    for load in loads[:3]:
-        load.wait()
+    wait_all(first_loads)
     copies = []
     proj_bias = proj_bias_ref[stream : stream + 1].astype(jnp.float32)
     for seq, span in enumerate(spans):
@@ -750,7 +922,7 @@
         over_rows(span.start, length, feat, 0, second_norm)
         copies.append(remote(normed_ref.at[span], normed_in.at[span], core_sems, seq, partner))
     kept = [store(branch_ref, branch_hbm), store(normed_ref, normed_hbm)]
-    loads[3].wait()
+    wait_all(cot_loads)
     down_total = 0.0
     for half_spans in (spans, other_spans):
         for seq, span in enumerate(half_spans):
@@ -774,8 +946,7 @@
             return ()
 
         over_rows(spans[seq].start, length, feat, 0, other_hidden)
-    for load in loads[4:]:
-        load.wait()
+    wait_all(weight_loads)
 
     def unit_block(index, carry):
         cols = pl.ds(pl.multiple_of(index * block, block), block)
@@ -825,15 +996,14 @@
             own[:, cols] = own[:, cols] + incoming[:, cols]
         exchanges.append(remote(own, got, swap_sems, swaps + kind, facing))
     pl.semaphore_signal(ready_sem, inc=1, device_id=partner, device_id_type=pl.DeviceIdType.MESH)
-    again = [load_again(branch_hbm, branch_ref), load_again(normed_hbm, normed_ref)]
-    cot_again = load_again(cot_hbm, hidden_ref)
+    again = [load(branch_hbm, branch_ref), load(normed_hbm, normed_ref)]
+    again += move_halves(load, cot_hbm, hidden_ref.at[:rows], seqs, direct, halves=1)
     middle = min(3, ring.last)
     ring.rounds(0, middle)
 
     exchanges[0].wait()
-    again.append(load_again(hidden_got_hbm, mine_ref))
-    for copy in again + [cot_again]:
-        copy.wait()
+    again.append(load(hidden_got_hbm, mine_ref))
+    wait_all(again)
     pl.semaphore_wait(ready_sem, 1)
     copies, proj_total = [], 0.0
     for seq, span in enumerate(spans):
@@ -872,13 +1042,12 @@
     store(grad_mlp_ref, grad_branch_hbm)
     store(grad_attn_ref, grad_attn_hbm)
     pl.semaphore_signal(ready_sem, inc=1, device_id=partner, device_id_type=pl.DeviceIdType.MESH)
-    again = [load_again(branch_hbm, branch_ref)]
+    again = [load(branch_hbm, branch_ref)]
     ring.rounds(middle, ring.last)
 
     exchanges[1].wait()
-    again.append(load_again(mlp_got_hbm, mine_ref))
-    for copy in again:
-        copy.wait()
+    again.append(load(mlp_got_hbm, mine_ref))
+    wait_all(again)
     pl.semaphore_wait(ready_sem, 1)
     copies = []
     down_bias = down_bias_ref[stream : stream + 1].astype(jnp.float32)
@@ -905,7 +1074,7 @@
     for seq, copy in enumerate(copies):
         copy.wait()
         over_rows(spans[seq].start, length, feat, 0, other_rows)
-    store(input_ref, out_hbm)
+    move_halves(store, out_hbm, input_ref, seqs, direct, to_array=True)
 
     buffers = (mine_ref, got_ref, branch_ref, normed_ref)
     each = rows // (2 * ring.half)
@@ -935,9 +1104,10 @@
 
 def mlp_ring(
     stream, mine, got, inputs, cots, modulate, proj_bias, up_bias, down_bias, up_weight, down_weight,
-    proj_weight, gives, order, rest, collective_id,
+    proj_weight, gives, order, rest, direct, collective_id,
 ):
-    _, seqs, length, feat = inputs.shape
+    seqs, feat = modulate.shape[1:]
+    length = inputs.shape[2]
     rows, units, size, swaps = seqs * length, up_weight.shape[2], len(order), len(gives)
     local = proj_weight.shape[1]
     block = 256
@@ -966,12 +1136,12 @@
     large |= {
         "grad_branch": narrow(2 * rows, feat),
         "grad_attn": narrow(2 * rows, local),
-        "out": narrow(2 * rows, feat),
+        "out": narrow(*inputs.shape),
     }
     moved = 4 * 2 * 2 * (size - 1) * half * units
     blocks = 2 * feat // block
     results = pl.pallas_call(
-        functools.partial(mlp_ring_kernel, order, stream, seqs, block, swaps, rest),
+        functools.partial(mlp_ring_kernel, order, stream, seqs, block, swaps, rest, direct),
         out_shape=ring_outs + gets + list(small.values()) + list(large.values()),
         in_specs=[vmem] * 4 + [anywhere] * (7 + swaps),
         out_specs=[anywhere if rest else vmem] * len(ring_outs)
@@ -993,11 +1163,10 @@
         ]
         + [pltpu.VMEM((rows, feat), jnp.float32)] * 6
         + [
-            pltpu.SemaphoreType.DMA((7,)),
+            pltpu.SemaphoreType.DMA((10 + 5 * seqs,)),
             pltpu.SemaphoreType.DMA((2, 3 * seqs + blocks)),
             pltpu.SemaphoreType.DMA((2, swaps + 2)),
-            pltpu.SemaphoreType.DMA((6 + len(ring_outs),)),
-            pltpu.SemaphoreType.DMA((6,)),
+            pltpu.SemaphoreType.DMA((6 + 2 * seqs + len(ring_outs),)),
             pltpu.SemaphoreType.REGULAR,
         ],
         compiler_params=pltpu.CompilerParams(
@@ -1012,8 +1181,8 @@
         down_bias,
         mine,
         got,
-        inputs.reshape(2 * rows, feat),
-        cots.reshape(2 * rows, feat),
+        inputs,
+        cots,
         up_weight,
         down_weight,
         proj_weight,
@@ -1025,15 +1194,17 @@
     return made
 
 
-def attn_ring_kernel(order, tensor_size, seqs, block, row_share, *refs):
+def attn_ring_kernel(order, tensor_size, seqs, block, row_share, directs, *refs):
     take = taker(refs)
     mod_ref, cond_ref, own_cond_ref, gain_sum_ref, bias_sum_ref = take(5)
     small_sums = (take(4), take(4))
     packed_hbm, attn_hbm, hidden_hbm, branch_hbm = take(2), take(2), take(2), take(2)
     through_hbm, input_hbm, cot_hbm = take(2), take(2), take(2)
     weight_hbm, ada_hbm = take(2)
+    arrived = (take(4), take(4))
     out_hbm, got_hbm = take(2), take(2)
     qkv_out, proj_out, ada_out = take(3)
+    mlp_outs = take(2)
     cond_out, ada_bias_out, qkv_bias_out, up_bias_out, gain_out, proj_bias_out, down_bias_out = take(7)
     slots, terms, turned = take(4), take(4), take(4)
     (ring_sems,) = take(1)
@@ -1078,7 +1249,8 @@
     second = [load(attn_hbm[stream], attn[stream]) for stream in range(2)]
     weight_load = load(weight_hbm, weight_ref)
     input_loads = [
-        load(input_hbm[stream].at[: rows[stream]], inputs[stream]) for stream in range(2)
+        move_halves(load, input_hbm[stream], inputs[stream], seqs, directs[stream], halves=1)
+        for stream in range(2)
     ]
     greet(around + across)
     again = []
@@ -1091,7 +1263,9 @@
         again[stream].wait()
         second[stream].wait()
         ring.begin(2 + stream)
-    cot_loads = [load(cot_hbm[stream], left[stream]) for stream in range(2)]
+    cot_loads = [
+        move_halves(load, cot_hbm[stream], left[stream], seqs, directs[stream]) for stream in range(2)
+    ]
 
     weight_load.wait()
     count = feat // block
@@ -1129,9 +1303,7 @@
         copy.wait()
     got_loads = [load(got_hbm[stream], outgoing[stream]) for stream in range(2)]
     for stream in range(2):
-        input_loads[stream].wait()
-        through_loads[stream].wait()
-        cot_loads[stream].wait()
+        wait_all(input_loads[stream] + cot_loads[stream] + [through_loads[stream]])
     for stream in (1, 0):
         got_loads[stream].wait()
         for seq in range(seqs):
@@ -1218,16 +1390,52 @@
 
         for seq in range(seqs):
             over_rows(seq * lengths[stream], lengths[stream], feat, 0, other_rows)
-        results.append(store(left[stream], out_hbm[stream]))
+        results.append(
+            move_halves(store, out_hbm[stream], left[stream], seqs, directs[stream], to_array=True)
+        )
+
+    height = arrived[0][0].shape[0]
+    sides = (
+        (outgoing[0].at[:height], outgoing[0].at[height : 2 * height]),
+        (outgoing[1].at[:height], incoming[1].at[:height]),
+    )
+
+    def fetch(stream):
+        return [
+            load(arrived[stream][2 * way + side], sides[way][side]) for way in range(2) for side in range(2)
+        ]
+
+    def add_up(stream, copies):
+        puts = []
+        for copy in copies:
+            copy.wait()
+        for way, (first, second) in enumerate(sides):
+            first[...] = first[...] + second[...]
+            for which in range(2):
+                puts.append(
+                    store(
+                        first.at[which * ring.half : (which + 1) * ring.half],
+                        mlp_outs[which].at[stream, way * ring.half : (way + 1) * ring.half],
+                    )
+                )
+        return puts
+
+    fetched = fetch(1)
     ring.rounds(middle, ring.last - 1)
-    results[1].wait()
+    puts = add_up(1, fetched)
+    for copy in results[1]:
+        copy.wait()
     ada_loads = [
         load(ada_hbm.at[stream], left[0].at[stream * cols : (stream + 1) * cols]) for stream in range(2)
     ]
     for copy in ada_loads:
         copy.wait()
     next(steps)
+    for copy in puts:
+        copy.wait()
+    fetched = fetch(0)
     ring.rounds(ring.last - 1, ring.last)
+    add_up(0, fetched)
     for _ in range(len(across)):
         next(steps)
 
@@ -1244,17 +1452,19 @@
     ring.finish(None, put_total)
     for _ in steps:
         pass
-    for copy in [results[0]] + stored[2:]:
-        copy.wait()
+    waited = {id(copy) for copy in puts + results[1]}
+    for copy in stored:
+        if id(copy) not in waited:
+            copy.wait()
 
 
 def attn_ring(
     modulate, conditioning, own_cond, gain_sums, bias_sums, states, packed, attn, hidden, inputs, cots, weight,
-    ada_weight, order, tensor_size, row_share, collective_id,
+    ada_weight, order, tensor_size, row_share, directs, collective_id,
 ):
-    seqs, feat = inputs[0].shape[1], inputs[0].shape[3]
+    seqs, feat = modulate.shape[1:]
     size, local, cols = len(order), attn[0].shape[1], ada_weight.shape[1]
-    rows = [array.shape[1] * array.shape[2] for array in inputs]
+    rows = [seqs * array.shape[2] for array in inputs]
     units = states[0]["up_bias"].shape[1]
     block = 256
     half = feat // (2 * size)
@@ -1267,9 +1477,10 @@
     def low(*dims):
         return pltpu.VMEM(dims, jnp.bfloat16)
 
-    large = [jax.ShapeDtypeStruct((2 * count, feat), jnp.bfloat16) for count in rows]
+    large = [jax.ShapeDtypeStruct(array.shape, jnp.bfloat16) for array in inputs]
     large += [wide(count, feat) for count in rows]
     large += [wide(2, 3, 2 * half, local), wide(2, 2 * half, local), wide(2, cols, feat)]
+    large += [wide(2, 2 * half, units)] * 2
     small = [
         wide(seqs, feat),
         wide(2, cols),
@@ -1293,13 +1504,13 @@
         hidden,
         [state["grad_branch"] for state in states],
         [state["through"] for state in states],
-        [array.reshape(-1, feat) for array in inputs],
-        [array.reshape(-1, feat) for array in cots],
+        inputs,
+        cots,
     ]
     return pl.pallas_call(
-        functools.partial(attn_ring_kernel, order, tensor_size, seqs, block, row_share),
+        functools.partial(attn_ring_kernel, order, tensor_size, seqs, block, row_share, directs),
         out_shape=large + small,
-        in_specs=[vmem] * (5 + len(sums)) + [anywhere] * (2 * len(pairs) + 2),
+        in_specs=[vmem] * (5 + len(sums)) + [anywhere] * (2 * len(pairs) + 10),
         out_specs=[anywhere] * len(large) + [vmem] * len(small),
         scratch_shapes=ring_scratch(size, halves, doubled + doubled)
         + [low(2 * count, 3 * local) for count in rows]
@@ -1310,10 +1521,10 @@
         + [pltpu.VMEM((count, feat), jnp.float32) for count in rows] * 3
         + [
             pltpu.VMEM((4, seqs, feat), jnp.float32),
-            pltpu.SemaphoreType.DMA((20,)),
+            pltpu.SemaphoreType.DMA((28 + 6 * seqs,)),
             pltpu.SemaphoreType.DMA((2, 2 * blocks + 2)),
             pltpu.SemaphoreType.DMA((2, 2)),
-            pltpu.SemaphoreType.DMA((20,)),
+            pltpu.SemaphoreType.DMA((32 + 4 * seqs,)),
             pltpu.SemaphoreType.REGULAR,
         ]
         + mod_refs
@@ -1333,6 +1544,7 @@
         *[array for pair in pairs for array in pair],
         weight,
         ada_weight,
+        *[array for state in states for pair in state["ring"] for array in pair],
     )
 
 
@@ -1343,18 +1555,10 @@
     totals = list(parts[:2])
     for later in range(rest):
         for way in range(2):
+            if later:
+                totals[way] = totals[way] + parts[2 * later + way]
             totals[way] = lax.ppermute(totals[way], "dp", ways[way])
-        for way in range(2):
-            totals[way] = totals[way] + parts[2 * (later + 1) + way]
-    return totals
-
-
-def by_rows(totals):
-    half = totals[0].shape[0] // 2
-    return [
-        jnp.concatenate([total[which * half : (which + 1) * half] for total in totals])[None]
-        for which in range(2)
-    ]
+    return [(totals[way], parts[2 * rest + way]) for way in range(2)]
 
 
 def on_device(
@@ -1379,49 +1583,42 @@
 ):
     data_size = len(order)
     seqs, _, feat = input_img.shape
-    core = lax.axis_index("tensor") % 2
     reals = (input_img.shape[1] // 2, input_txt.shape[1] // 2)
-
-    def split_rows(array):
-        half = array.shape[1] // 2
-        pad = -half % ROW_TILE
-        lower, upper = (
-            jnp.pad(part, ((0, 0), (0, pad), (0, 0))) for part in (array[:, :half], array[:, half:])
+    directs = [
+        shape[1] == 2 * real and real % ROW_TILE == 0
+        for shape, real in zip((input_img.shape, input_txt.shape), reals)
+    ]
+
+    def split_rows(array, stream):
+        real = reals[stream]
+        if directs[stream]:
+            return array.reshape(seqs, 2, real, feat)
+        pad = -real % ROW_TILE
+        return jnp.stack(
+            [
+                jnp.pad(part, ((0, 0), (0, pad), (0, 0)))
+                for part in (array[:, :real], array[:, real:])
+            ]
         )
-        first = core == 0
-        return jnp.stack([jnp.where(first, lower, upper), jnp.where(first, upper, lower)])
-
-    def join_rows(halves, real):
-        own, other = halves.astype(jnp.bfloat16)
-        first = core == 0
-        lower, upper = jnp.where(first, own, other), jnp.where(first, other, own)
-        return jnp.concatenate([lower[:, :real], upper[:, :real]], axis=1)
+
+    def join_rows(halves, stream):
+        real = reals[stream]
+        if directs[stream]:
+            return halves.reshape(seqs, 2 * real, feat)
+        return jnp.concatenate([halves[0][:, :real], halves[1][:, :real]], axis=1)
 
     ada_weight = ada_weight.transpose(0, 2, 1)
     modulate = mod_forward(
         conditioning, ada_weight, ada_bias, seqs, feat, data_size, tensor_size
     )
-    piece = [
-        [modulate[stream * 6 + index][:, None, :] for index in range(6)] for stream in range(2)
-    ]
-
-    inputs = [split_rows(input_img), split_rows(input_txt)]
-    cotangents = [split_rows(cotangent_img), split_rows(cotangent_txt)]
-    shapes = [array.shape for array in inputs]
+    inputs = [split_rows(input_img, 0), split_rows(input_txt, 1)]
+    cotangents = [split_rows(cotangent_img, 0), split_rows(cotangent_txt, 1)]
     gain_pair = jnp.concatenate([norm_gain, norm_gain], axis=2)
 
-    hidden1, raw = [], []
-    for stream in range(2):
-        normed, _ = layer_norm(inputs[stream].astype(jnp.float32))
-        hidden = (normed * (1.0 + piece[stream][1]) + piece[stream][0]).astype(jnp.bfloat16)
-        hidden = hidden.reshape(-1, feat)
-        flat = [
-            dot_plain(hidden, qkv_weight[stream, :, part]) + qkv_bias[stream, part].astype(jnp.float32)
-            for part in range(3)
-        ]
-        hidden1.append(hidden)
-        raw.append([each.reshape(shapes[stream][:3] + (-1,)) for each in flat])
-    attn = attn_forward(gain_pair, raw[0], raw[1], reals[1])
+    qkv_weight = qkv_weight.transpose(0, 2, 1, 3)
+    hidden1, raw, attn, branch_sums, got = front(
+        modulate, gain_pair, inputs, directs, qkv_weight, qkv_bias, proj_weight, reals[1], 5
+    )
     local = attn[0].shape[3]
 
     def mlp_stage(stream, got, gives, rest, collective_id):
@@ -1441,28 +1638,18 @@
             gives,
             order,
             rest,
+            directs[stream],
             collective_id,
         )
-        if rest:
-            made["ring"] = by_rows(ring_rest(made["ring"], order, rest))
+        made["ring"] = ring_rest(made["ring"], order, rest)
         return made
 
-    branch_sums = [None, None]
-    for stream in (1, 0):
-        rows = attn[stream].reshape(2, -1, local)
-        branch_sums[stream] = core_sum(
-            dot_plain(rows[0], proj_weight[stream]),
-            dot_plain(rows[1], proj_weight[stream]),
-            tensor_size,
-        )
     state = [None, None]
-    got = lax.ppermute(branch_sums[1], "tensor", swap_pairs(tensor_size, 2))
     state[1] = mlp_stage(1, got, [branch_sums[0]], RESTS[0], 2)
     state[0] = mlp_stage(0, state[1]["gets"][0], [], RESTS[1], 3)
-    mlp_rings = [state[stream]["ring"] for stream in range(2)]
 
     grad_attn = [state[stream]["grad_attn"].reshape(attn[stream].shape) for stream in range(2)]
-    grad_packed = attn_backward(gain_pair, raw[0], raw[1], grad_attn[0], grad_attn[1], reals[1])
+    grad_packed = attn_backward(gain_pair, list(raw[0]), list(raw[1]), grad_attn[0], grad_attn[1], reals[1])
     own_cond = lax.dynamic_slice_in_dim(
         conditioning, lax.axis_index("dp") * seqs, seqs, axis=0
     ).astype(jnp.float32)
@@ -1478,20 +1665,19 @@
         hidden1,
         inputs,
         cotangents,
-        qkv_weight.transpose(0, 2, 1, 3),
+        qkv_weight,
         ada_weight,
         order,
         tensor_size,
         2.0 / tensor_size,
+        directs,
         4,
     )
-    grad_qkv, grad_proj, grad_ada_weight, grad_conditioning, grad_ada_bias = made[4:9]
-    qkv_bias_sums, up_bias_sums, gain_sums, proj_sums, down_sums = made[9:]
-    outputs = [
-        join_rows(state[stream]["out"].reshape(shapes[stream]), reals[stream]) for stream in range(2)
-    ]
-    grad_inputs = [join_rows(made[stream].reshape(shapes[stream]), reals[stream]) for stream in range(2)]
-    down_rings, up_rings = ([mlp_rings[0][index], mlp_rings[1][index]] for index in range(2))
+    grad_qkv, grad_proj, grad_ada_weight, grad_down, grad_up, grad_conditioning, grad_ada_bias = made[4:11]
+    qkv_bias_sums, up_bias_sums, gain_sums, proj_sums, down_sums = made[11:]
+
+    outputs = [join_rows(state[stream]["out"], stream) for stream in range(2)]
+    grad_inputs = [join_rows(made[stream], stream) for stream in range(2)]
     return (
         outputs[0],
         outputs[1],
@@ -1505,9 +1691,9 @@
         gain_sums,
         grad_proj.transpose(0, 2, 1),
         proj_sums,
-        jnp.concatenate(up_rings),
+        grad_up,
         up_bias_sums,
-        jnp.concatenate(down_rings).transpose(0, 2, 1),
+        grad_down.transpose(0, 2, 1),
         down_sums,
     )
 
@@ -1553,4 +1739,6 @@
     def step(*arrays):
         return on_device(ring_order(mesh), mesh.shape["tensor"], *arrays)
 
-    return jax.shard_map(step, mesh=mesh, in_specs=in_specs, out_specs=out_specs, check_vma=False)
+    return jax.shard_map(
+        step, mesh=mesh, in_specs=in_specs, out_specs=out_specs, check_vma=False
+    )

time: 731 us -> 694 us (0.949)
  Pallas kernels: 617 us -> 646 us
  other arithmetic: 35.4 us -> 7.56 us
  matrix products: 20 us -> 0 us
  waiting for transfers between devices: 18.9 us -> 0.6 us
    pallas_call x1, Pallas kernels: 9.74 us -> 46.9 us  [front(): pl.pallas_call(functools.partial(front_kernel, seqs, real, 512, by_seqs),...]
    pallas_call x1, Pallas kernels: 216 us -> 194 us  [attn_ring(): pl.pallas_call(functools.partial(attn_ring_kernel, order, tensor_size, se...]
    dot_general x10 -> x0, matrix products: 20 us -> none  [dot_plain(): return jnp.dot(first_op, second_op, preferred_element_type=jnp.float32)]
    ppermute x3 -> x0, waiting for transfers between devices: 18.9 us -> none  [the longest x1 18.9 us: on_device(): got = lax.ppermute(branch_sums[1], 'tensor', swap_pairs(tensor_size, 2))]
    pallas_call x2, Pallas kernels: 354 us -> 367 us  [mlp_ring(): pl.pallas_call(functools.partial(mlp_ring_kernel, order, stream, seqs, bl...]
    convert_element_type x5 -> x0, other arithmetic: 8.95 us -> none  [the longest x4 8.91 us: on_device(): (normed * (1.0 + piece[stream][1]) + piece[stream][0]).astype(jnp.bfloat16)]
    unnamed x116 -> x59, local copies, waits for them, and re-layouts: 20 us -> 21.2 us
  transfers between devices with their start and end apart: 7 -> 4, of which waited for: 1 -> 1; matrix products, arithmetic and copies ran while one was open for 4% -> 0% of each run, Pallas kernels for 33% -> 30%
where the time goes in v5:
time: 694 us; the launch traced here: 684 us
  Pallas kernels  646 us (93%)
  local copies, waits for them, and re-layouts  24.5 us (4%)
  other arithmetic  7.56 us (1%)
    pallas_call x2, Pallas kernels, mlp_ring(): pl.pallas_call(functools.partial(mlp_ring_kernel, order, stream, seqs, bl...  367 us
    pallas_call x1, Pallas kernels, attn_ring(): pl.pallas_call(functools.partial(attn_ring_kernel, order, tensor_size, se...  194 us
    pallas_call x1, Pallas kernels, front(): pl.pallas_call(functools.partial(front_kernel, seqs, real, 512, by_seqs),...  46.9 us
    pallas_call x1, Pallas kernels, attn_backward(): pl.pallas_call(functools.partial(attn_backward_kernel, real), grid=(seqs,...  22.3 us
    unnamed x59, local copies, waits for them, and re-layouts  21.2 us
    pallas_call x1, Pallas kernels, mod_forward(): pl.pallas_call(functools.partial(mod_forward_kernel, data_size, tensor_si...  15 us
  transfers between devices with their start and end apart: 4, of which 1 were waited for; matrix products, arithmetic and copies ran while one was open for 0% of the time, Pallas kernels for 30%

profile of v5, /device:TPU:0, one launch (start us, length us, event | category | flops | bytes accessed | tf_op | source)
XLA Modules:
  0.0 683.9 jit_solution(15570575010150851918)
XLA Ops:
  0.6 1.4 pad_maximum_fusion.4.refs_1_.gain_ref
  2.1 1.3 copy.32.refs_2_
  3.3 1.4 slice.39
  5.2 1.1 copy-done.10
  6.5 1.3 copy-done
  7.8 15.0 %mod_forward.1.refs_0_ = f32[12,3,1536]{2,1,0:T(4,128)S(1)} custom-call(bf16[24,1536]{1,0:T(8,128)(2,1)S(1)} %copy-done.2, bf16[2,288,1536]{2,1,0:T(8,128)(2,1)S(1)} %bitcast.38, bf16[2,288]{1,0:T(2,128)(2,1)S(1)} %copy-done.3), custom_call_target="tpu_custom_call" | custom-call | tf_op jit(solution)/shard_map/mod_forward/pallas_call | solution.py:324
  22.9 1.9 pad_maximum_fusion
  24.8 46.9 %front.1 = (bf16[768,1536]{1,0:T(8,128)(2,1)}, bf16[480,1536]{1,0:T(8,128)(2,1)}, f32[2,3,128,384]{3,2,1,0:T(8,128)}, f32[2,3,128,384]{3,2,1,0:T(8,128)}, f32[2,...) custom-call(f32[12,3,1536]{2,1,0:T(4,128)} %copy-done.1, ...), custom_call_target="tpu_custom_call" | custom-call | tf_op jit(solution)/shard_map/front/pallas_call | solution.py:815
  71.7 185.6 %mlp_ring.2 = (f32[192,1536]{1,0:T(8,128)}, f32[192,1536]{1,0:T(8,128)}, f32[192,1536]{1,0:T(8,128)}, f32[192,1536]{1,0:T(8,128)}, f32[384,1536]{1,0:T(8,128)}, ...) custom-call(f32[12,3,1536]{2,1,0:T(4,128)} %copy-done.1, ...), custom_call_target="tpu_custom_call" | custom-call | flops 165150720000 | bytes 16515072 | tf_op jit(solution)/shard_map/mlp_ring/pallas_call | solution.py:1143
  259.4 181.9 %mlp_ring.3 = (f32[192,1536]{1,0:T(8,128)}, f32[192,1536]{1,0:T(8,128)}, f32[192,1536]{1,0:T(8,128)}, f32[192,1536]{1,0:T(8,128)}, f32[1,1536]{1,0:T(1,128)}, /*...) custom-call(f32[12,3,1536]{2,1,0:T(4,128)} %copy-done.1, ...), custom_call_target="tpu_custom_call" | custom-call | flops 165150720000 | bytes 16515072 | tf_op jit(solution)/shard_map/mlp_ring/pallas_call | solution.py:1143
  441.3 1.7 collective-permute-start
  443.3 22.3 %attn_backward.1 = (bf16[2,3,128,1152]{3,2,1,0:T(8,128)(2,1)}, bf16[2,3,80,1152]{3,2,1,0:T(8,128)(2,1)}, f32[3,2,1152]{2,1,0:T(2,128)}, f32[3,4,128]{2,1,0:T(4,128)}) custom-call(f32[2,2,128]{2,1,0:T(2,128)} %pad_maximum_fusion.4.refs_1_.gain_ref, f32[2,3,128,384]{3,2,1,0:T(8,128)} %get-tuple-element.78.refs_0_, ...), custom_call_target="tpu_custom_call" | custom-call | flops 1993605120 | bytes 9584640 | tf_op jit(solution)/shard_map/attn_backward/pallas_call | solution.py:210
  465.7 1.4 dynamic-slice_convert_fusion.refs_2_
  467.2 1.3 pad_maximum_fusion.2
  469.2 194.1 %attn_ring.1 = (bf16[3,2,128,1536]{3,2,1,0:T(8,128)(2,1)}, bf16[2,3,80,1536]{3,2,1,0:T(8,128)(2,1)}, f32[384,1536]{1,0:T(8,128)}, f32[240,1536]{1,0:T(8,128)}, f...) custom-call(f32[12,3,1536]{2,1,0:T(4,128)} %copy-done.1, ...), custom_call_target="tpu_custom_call" | custom-call | flops 165150720000 | bytes 16515072 | tf_op jit(solution)/shard_map/attn_ring/pallas_call | solution.py:1510
  663.3 1.4 slice_bitcast_fusion.1
  664.8 1.3 pad_maximum_fusion.3
  667.0 1.4 copy.47
  668.4 1.1 copy-done.8
  669.5 1.4 copy.48
  672.4 1.8 copy.50
  675.1 1.2 copy.52
  679.0 1.4 copy.57
  681.5 1.4 copy.59
  (61 shorter events, 11.4 us)
Async XLA Ops:
  3.3 1.6 copy-start.11
  5.0 1.4 copy-start.21
  6.3 1.5 copy-start
  6.3 1.5 copy-start.2
  6.3 1.5 copy-start.3
  22.9 1.9 copy-start.1
  257.3 211.3 %collective-permute-start.2 = (f32[192,1536]{1,0:T(8,128)}, f32[192,1536]{1,0:T(8,128)}, u32[]{:S(2)}, u32[]{:S(2)}) collective-permute-start(f32[192,1536]{1,0:T(8,128)} %get-tuple-element.110), channel_id=1, source_target_pairs={{0,4},{4,12},{12,20},{20,28},{28,24},{24,16},{16,8},{8,0},{1,5},{5... | collective-permute-start | bytes 3538952 | tf_op jit(solution)/shard_map/ppermute | solution.py:1560
  258.3 210.2 %collective-permute-start.3 = (f32[192,1536]{1,0:T(8,128)}, f32[192,1536]{1,0:T(8,128)}, u32[]{:S(2)}, u32[]{:S(2)}) collective-permute-start(f32[192,1536]{1,0:T(8,128)} %get-tuple-element.112), channel_id=1, source_target_pairs={{4,0},{12,4},{20,12},{28,20},{24,28},{16,24},{8,16},{0,8},{5,1},{1... | collective-permute-start | bytes 3538952 | tf_op jit(solution)/shard_map/ppermute | solution.py:1560
  441.3 27.3 %collective-permute-start = (f32[192,1536]{1,0:T(8,128)}, f32[192,1536]{1,0:T(8,128)}, u32[]{:S(2)}, u32[]{:S(2)}) collective-permute-start(f32[192,1536]{1,0:T(8,128)} %get-tuple-element.106), channel_id=1, source_target_pairs={{0,4},{4,12},{12,20},{20,28},{28,24},{24,16},{16,8},{8,0},{1,5},{5... | collective-permute-start | bytes 3538952 | tf_op jit(solution)/shard_map/ppermute | solution.py:1560
  443.0 26.2 %collective-permute-start.1 = (f32[192,1536]{1,0:T(8,128)}, f32[192,1536]{1,0:T(8,128)}, u32[]{:S(2)}, u32[]{:S(2)}) collective-permute-start(f32[192,1536]{1,0:T(8,128)} %get-tuple-element.108), channel_id=1, source_target_pairs={{4,0},{12,4},{20,12},{28,20},{24,28},{16,24},{8,16},{0,8},{5,1},{1... | collective-permute-start | bytes 3538952 | tf_op jit(solution)/shard_map/ppermute | solution.py:1560
  443.3 23.8 %copy-start.12 = (bf16[2,3,80,1536]{3,2,1,0:T(8,128)(2,1)S(1)}, bf16[2,3,80,1536]{3,2,1,0:T(8,128)(2,1)}, u32[]{:S(2)}) copy-start(bf16[2,3,80,1536]{3,2,1,0:T(8,128)(2,1)} %get-tuple-element.77) | copy-start | bytes 4423684
  664.8 2.2 copy-start.5
  667.0 2.5 copy-start.8
  669.5 1.4 copy-start.14
  669.5 2.9 copy-start.4
  672.4 1.8 copy-start.19
  672.4 2.8 copy-start.9
  675.1 1.8 copy-start.20
  675.1 2.4 copy-start.13
  675.1 3.2 copy-start.17
  675.1 3.8 copy-start.7
  678.9 1.4 copy-start.16
  679.0 2.5 copy-start.6
  681.5 1.4 copy-start.15
  (2 other events, 2.6 us)
